TPU v7x, 1024 devices: a whole 4x4x32 slice. The times are simulated.
1024 devices in a mesh: ep: 32 (over y, x, core), tp: 32 (over z).
Axes of the slice: x: 4, y: 4, z: 32, core: 2. Of those that a mesh axis runs over, the one named last changes fastest.
Arguments:
- tokens: bfloat16 [4096, 2048], P('ep', 'tp'), may hold values from -6 to 6
- routing: int32 [4096, 8], P('ep'), may hold values from 0 to 127, all different within a row; in each aligned block of 128 rows (0 to 127, 128 to 255, ...) at most 16 rows name the same one
- gate_fixed: int32 [4096, 8], P('ep'), may hold values from 1 to 65535
- gate_weight: bfloat16 [128, 2048, 768], P('ep', 'tp'), may hold values from -0.125 to 0.125
- up_weight: bfloat16 [128, 2048, 768], P('ep', 'tp'), may hold values from -0.25 to 0.25
- down_weight: bfloat16 [128, 2048, 768], P('ep', 'tp'), may hold values from -0.21875 to 0.21875
Outputs:
- layer_out: bfloat16 [4096, 2048], P('ep', 'tp')
Inputs may be any that keep to these rules, and one draw needn't show every extreme that they name: `routing`: each token names 8 different experts. In each aligned block of 128 tokens (the tokens of one index of ep) no expert is named by more than 16 tokens, and in some blocks one expert is named by exactly 16.
All inputs are finite; a program needn't handle non-finite values.
Results may differ from a plain program's by a relative error of at most 0.0057.
Values may be sent and summed in bfloat16 or wider, within the bound.
No kernel may reach another device: no remote copies, remote signals or barrier semaphores. Data moves between devices by JAX's collectives and lax.ppermute only.
A program may use at most 64 MiB of HBM per device.

v0:
```python
import jax
import jax.numpy as jnp
from jax import lax
from jax.sharding import PartitionSpec as P


def sent_together(arrays, axis, split_dim, concat_dim, along):
    ends, at = ([], 0)
    for a in arrays[:-1]:
        at += a.shape[along]
        ends.append(at)
    both = jnp.concatenate(arrays, axis=along)
    return tuple(
        jnp.split(
            lax.all_to_all(both, axis, split_axis=split_dim, concat_axis=concat_dim, tiled=True),
            ends,
            axis=along,
        )
    )


def slot_numbers(routing, experts, capacity):
    token_rows, top_count = routing.shape
    flat_ids = routing.reshape(-1)
    one_hot = (flat_ids[:, None] == jnp.arange(experts, dtype=jnp.int32)[None, :]).astype(jnp.int32)
    earlier = jnp.cumsum(one_hot, axis=0) - one_hot
    position = jnp.sum(earlier * one_hot, axis=1)
    return (flat_ids * capacity + position).reshape(token_rows, top_count)


def on_device(tokens, routing, gate_fixed, gate_weight, up_weight, down_weight):
    ep_count = lax.axis_size("ep")
    tp_count = lax.axis_size("tp")
    local_experts, feature_share, hidden_width = gate_weight.shape
    experts = local_experts * ep_count
    token_rows, top_count = routing.shape
    capacity = max(2, token_rows * top_count * 2 // experts)
    slot_count = experts * capacity
    unit_share = hidden_width // tp_count
    slot_index = slot_numbers(routing, experts, capacity)
    token_ids = jnp.repeat(jnp.arange(token_rows, dtype=jnp.int32), top_count)
    owners = jnp.zeros((slot_count,), jnp.int32).at[slot_index.reshape(-1)].set(token_ids)
    outgoing = jnp.take(tokens, owners, axis=0)
    arrived = lax.all_to_all(outgoing, "ep", split_axis=0, concat_axis=0, tiled=True)
    gate_split, up_split = sent_together((gate_weight, up_weight), "tp", 2, 1, 0)
    portion = lax.all_gather(arrived, "tp", axis=1, tiled=True)
    width = portion.shape[1]
    pieces = portion.reshape(ep_count, local_experts, capacity, width)
    gate_part = jnp.einsum("secd,edf->fsec", pieces, gate_split, preferred_element_type=jnp.float32)
    up_part = jnp.einsum("secd,edf->fsec", pieces, up_split, preferred_element_type=jnp.float32)
    gate_acts = gate_part.reshape(unit_share, slot_count)
    up_acts = up_part.reshape(unit_share, slot_count)
    hidden_share = (jax.nn.silu(gate_acts) * up_acts).astype(jnp.bfloat16)
    portion = lax.all_gather(hidden_share, "tp", axis=0, tiled=True)
    length = portion.shape[0]
    units = portion.reshape(length, ep_count, local_experts, capacity)
    expert_sum = jnp.einsum(
        "fsec,edf->secd", units, down_weight, preferred_element_type=jnp.float32
    )
    expert_out = expert_sum.astype(jnp.bfloat16).reshape(slot_count, feature_share)
    returned = lax.all_to_all(expert_out, "ep", split_axis=0, concat_axis=0, tiled=True)
    picked = jnp.take(returned, slot_index.reshape(-1), axis=0).reshape(
        token_rows, top_count, feature_share
    )
    scales = gate_fixed.astype(jnp.float32) / 65536.0
    mixed = jnp.sum(picked.astype(jnp.float32) * scales[:, :, None], axis=1)
    return mixed.astype(jnp.bfloat16)


def solution(mesh):
    in_specs = (
        P("ep", "tp"),
        P("ep", None),
        P("ep", None),
        P("ep", "tp", None),
        P("ep", "tp", None),
        P("ep", "tp", None),
    )
    out_specs = P("ep", "tp")
    return jax.shard_map(
        on_device, mesh=mesh, in_specs=in_specs, out_specs=out_specs, check_vma=False
    )
```

profile of v0, /device:TPU:1, one launch (start us, length us, event | category | flops | bytes accessed | tf_op | source)
XLA Modules:
  0.0 460.2 jit_solution(3081508536821030283)
XLA Ops:
  9.5 4.3 scatter_custom_fusion
  14.0 6.2 %gather_fusion = bf16[2048,64]{1,0:T(8,128)(2,1)S(1)} fusion(bf16[128,64]{1,0:T(8,128)(2,1)S(1)} %copy.62, s32[2048]{0:T(1024)S(1)} %fusion.26), kind=kCustom, calls=%fused_computation | custom fusion | bytes 532480 | tf_op jit(solution)/shard_map/jit(_take)/gather | solution.py:43
  21.0 25.7 %all_to_all.36 = bf16[32,2,2048]{2,1,0:T(2,128)(2,1)S(1)} all-to-all(bf16[32,2,2048]{2,1,0:T(2,128)(2,1)S(1)} %reshape.136), channel_id=1, replica_groups=mesh['ep'=32,'tp'=32] {'ep'}, dimensions={0} | all-to-all | bytes 524288 | tf_op jit(solution)/shard_map/all_to_all | solution.py:44
  48.7 1.5 copy.58
  50.1 1.0 fusion.30
  51.1 1.1 reshape.138
  52.3 115.2 %all_to_all.37 = bf16[32,2,6144]{2,1,0:T(2,128)(2,1)S(1)} all-to-all(bf16[32,2,6144]{2,1,0:T(2,128)(2,1)S(1)} %reshape.138), channel_id=1, replica_groups=mesh['ep'=32,'tp'=32] {'tp'}, dimensions={0} | all-to-all | bytes 1572864 | tf_op jit(solution)/shard_map/all_to_all | solution.py:15
  167.5 1.0 reshape.139
  169.2 1.4 reshape.129
  171.3 72.3 %all-gather.3.cloned.1.call-done = bf16[2048,2048]{0,1:T(8,128)(2,1)} async-done(((bf16[2048,64]{0,1:T(8,128)(2,1)}), bf16[2048,2048]{0,1:T(8,128)(2,1)}) %all-gather.3.cloned.1.call-update) | async-done | bytes 8388624 | tf_op jit(solution)/shard_map/all_gather | solution.py:46
  243.7 12.4 %copy.64 = bf16[2048,2048]{1,0:T(8,128)(2,1)} copy(bf16[2048,2048]{0,1:T(8,128)(2,1)} %all-gather.3.cloned.1.call-done) | data formatting | bytes 16777216 | tf_op jit(solution)/shard_map/all_gather | solution.py:46
  256.0 9.0 %fusion.9 = f32[24,32,4,16]{1,0,3,2:T(8,128)S(1)} fusion(bf16[32,4,16,2048]{3,2,1,0:T(8,128)(2,1)} %bitcast.54, bf16[4,2048,24,1]{1,2,0,3:T(8,128)(2,1)S(1)} %copy-done.2), kind=kOutput, calls=%fused_computation.11 | convolution fusion | flops 201326592 | bytes 8978432 | tf_op jit(solution)/shard_map/secd,edf->fsec/dot_general | solution.py:49
  265.0 1.4 copy.66
  266.5 1.5 reshape.101
  268.0 9.0 %fusion.12 = f32[24,32,4,16]{1,0,3,2:T(8,128)S(1)} fusion(bf16[32,4,16,2048]{3,2,1,0:T(8,128)(2,1)} %bitcast.55, bf16[4,2048,24,1]{1,2,0,3:T(8,128)(2,1)S(1)} %reshape.130), kind=kOutput, calls=%fused_computation.12 | convolution fusion | flops 201326592 | bytes 8978432 | tf_op jit(solution)/shard_map/secd,edf->fsec/dot_general | solution.py:50
  277.0 1.2 copy.69
  278.2 1.5 reshape.102
  280.6 125.3 %all-gather.5.cloned.1.call-done = bf16[768,2048]{1,0:T(8,128)(2,1)} async-done(((bf16[24,2048]{1,0:T(8,128)(2,1)}), bf16[768,2048]{1,0:T(8,128)(2,1)}) %all-gather.5.cloned.1.call-update) | async-done | bytes 3145744 | tf_op jit(solution)/shard_map/all_gather | solution.py:54
  406.0 3.2 copy.70
  409.2 1.0 fusion.15
  410.2 1.1 reshape.140
  411.3 28.6 %all-to-all-start.2 = ((bf16[32,2,2048]{2,1,0:T(2,128)(2,1)}), bf16[32,2,2048]{2,1,0:T(2,128)(2,1)S(1)}, u32[]{:S(2)}, u32[]{:S(2)}) async-start(bf16[32,2,2048]{2,1,0:T(2,128)(2,1)} %reshape.140), calls=%async_computation.2 | async-start | bytes 524288 | tf_op jit(solution)/shard_map/all_to_all | solution.py:61
  440.1 8.6 %all-to-all-done.2 = bf16[32,2,2048]{2,1,0:T(2,128)(2,1)S(1)} async-done(((bf16[32,2,2048]{2,1,0:T(2,128)(2,1)}), bf16[32,2,2048]{2,1,0:T(2,128)(2,1)S(1)}, u32[]{:S(2)}, u32[]{:S(2)}) %all-to-all-start.2) | async-done | bytes 262176 | tf_op jit(solution)/shard_map/all_to_all | solution.py:61
  449.1 3.2 gather_fusion.1
  (59 shorter events, 9.7 us)
Async XLA Ops:
  6.5 402.6 %copy-start = (bf16[4,64,768]{2,1,0:T(8,128)(2,1)S(1)}, bf16[4,64,768]{2,1,0:T(8,128)(2,1)}, u32[]{:S(2)}) copy-start(bf16[4,64,768]{2,1,0:T(8,128)(2,1)} %param.11) | copy-start | bytes 1179652
  6.5 7.3 %copy-start.4 = (bf16[128,64]{0,1:T(8,128)(2,1)S(1)}, bf16[128,64]{0,1:T(8,128)(2,1)}, u32[]{:S(2)}) copy-start(bf16[128,64]{0,1:T(8,128)(2,1)} %param.6) | copy-start | bytes 49156
  6.5 237.1 %all-gather.3.cloned.1.call-start = ((), (), s32[]{:S(2)}) async-start(), calls=%async_computation.3 | async-start | bytes 8650752 | tf_op jit(solution)/shard_map/all_gather | solution.py:46
  20.2 27.8 %copy-start.1 = (bf16[4,64,768]{2,1,0:T(8,128)(2,1)S(1)}, bf16[4,64,768]{2,1,0:T(8,128)(2,1)}, u32[]{:S(2)}) copy-start(bf16[4,64,768]{2,1,0:T(8,128)(2,1)} %param.9) | copy-start | bytes 1179652
  48.0 358.0 %all-gather.5.cloned.1.call-start = ((), (), s32[]{:S(2)}) async-start(), calls=%async_computation.4 | async-start | bytes 3244032 | tf_op jit(solution)/shard_map/all_gather | solution.py:54
  171.3 84.7 %copy-start.2 = (bf16[4,2048,24,1]{1,2,0,3:T(8,128)(2,1)S(1)}, bf16[4,2048,24,1]{1,2,0,3:T(8,128)(2,1)}, u32[]{:S(2)}) copy-start(bf16[4,2048,24,1]{1,2,0,3:T(8,128)(2,1)} %reshape.129) | copy-start | bytes 1179652
  277.0 3.6 copy-start.3
  409.2 30.7 %copy-start.5 = (s32[128,8]{0,1:T(8,128)S(1)}, s32[128,8]{0,1:T(8,128)}, u32[]{:S(2)}) copy-start(s32[128,8]{0,1:T(8,128)} %param.8) | copy-start | bytes 12292
  411.3 37.4 %all-to-all-start.2 = ((bf16[32,2,2048]{2,1,0:T(2,128)(2,1)}), bf16[32,2,2048]{2,1,0:T(2,128)(2,1)S(1)}, u32[]{:S(2)}, u32[]{:S(2)}) async-start(bf16[32,2,2048]{2,1,0:T(2,128)(2,1)} %reshape.140), calls=%async_computation.2 | async-start | bytes 524288 | tf_op jit(solution)/shard_map/all_to_all | solution.py:61
Sparse Core Ops, SparseCore 0:
  48.1 195.4 all-gather.2
  280.6 125.3 all-gather.4
where the time goes:
time: 461 us; the launch traced here: 460 us
  waiting for transfers between devices  206 us (45%)
  blocking collectives  141 us (31%)
  local copies, waits for them, and re-layouts  47.9 us (10%)
  starting transfers between devices  28.6 us (6%)
  matrix products  18.9 us (4%)
  between operations  13.7 us (3%)
    all_gather x1, waiting for transfers between devices, on_device(): portion = lax.all_gather(hidden_share, 'tp', axis=0, tiled=True)  125 us
    all_to_all x1, blocking collectives, sent_together(): lax.all_to_all(both, axis, split_axis=split_dim, concat_axis=concat_dim,...  115 us
    all_gather x1, waiting for transfers between devices, on_device(): portion = lax.all_gather(arrived, 'tp', axis=1, tiled=True)  72.3 us
    all_to_all x1, starting transfers between devices, on_device(): lax.all_to_all(expert_out, 'ep', split_axis=0, concat_axis=0, tiled=True)  28.6 us
    all_to_all x1, blocking collectives, on_device(): lax.all_to_all(outgoing, 'ep', split_axis=0, concat_axis=0, tiled=True)  25.7 us
    all_gather x1, local copies, waits for them, and re-layouts, on_device(): portion = lax.all_gather(arrived, 'tp', axis=1, tiled=True)  12.4 us
  transfers between devices with their start and end apart: 3, of which 3 were waited for; matrix products, arithmetic and copies ran while one was open for 2% of the time, Pallas kernels for 0%

commit v1 on v0

v1 whole, which is shorter than its diff:
```python
import jax
import jax.numpy as jnp
from jax import lax
from jax.sharding import PartitionSpec as P

F32 = jnp.float32
BF16 = jnp.bfloat16


def exchange(x, axis, groups=None):
    return lax.all_to_all(
        x, axis, split_axis=0, concat_axis=0, tiled=True, axis_index_groups=groups
    )


def by_position(w, halves):
    e, f, u = w.shape
    return w.reshape(e, f, halves, u // halves).transpose(0, 2, 1, 3).reshape(
        e * halves, f, u // halves
    )


def on_device(tokens, routing, gate_fixed, gate_weight, up_weight, down_weight):
    ep = lax.axis_size("ep")
    tp = lax.axis_size("tp")
    local, share, hidden_width = gate_weight.shape
    rows, top = routing.shape
    capacity = max(2, rows * top * 2 // (local * ep))
    spread = 4
    members = tp // spread
    halves = members // local
    units = hidden_width // halves
    slots = ep * capacity
    far = [[j * spread + r for j in range(members)] for r in range(spread)]
    near = [[i * spread + r for r in range(spread)] for i in range(members)]
    z = lax.axis_index("tp")
    mine = z // (spread * halves)
    me = z % spread

    w_in = jnp.concatenate(
        [by_position(gate_weight, halves), by_position(up_weight, halves)], axis=2
    )
    w_gu = exchange(w_in, "tp", far).reshape(members * share, 2 * units)
    w_down = exchange(by_position(down_weight, halves), "tp", far).reshape(
        members * share, units
    )

    xt = exchange(
        jnp.broadcast_to(tokens.T[None], (members, share, rows)), "tp", far
    ).reshape(members * share, rows)

    rt = routing.T
    expert = jnp.arange(ep, dtype=jnp.int32) * local + mine
    hit = rt[:, None, :] == expert[None, :, None]
    named = jnp.any(hit, axis=0)
    scale = jnp.sum(jnp.where(hit, gate_fixed.T[:, None, :], 0), axis=0)
    t = jnp.arange(rows)
    before = (t[:, None] < t[None, :]).astype(BF16)
    position = jnp.dot(named.astype(BF16), before, preferred_element_type=F32)
    slot = jnp.arange(capacity).astype(F32)[None, :, None]
    pick = named[:, None, :] & (position[:, None, :] == slot)
    place = pick.astype(BF16).reshape(slots, rows)
    high = (scale >> 8).astype(F32) / 256.0
    low = (scale & 255).astype(F32) / 65536.0
    mix_high = jnp.where(pick, high[:, None, :], 0.0).astype(BF16).reshape(slots, rows)
    mix_low = jnp.where(pick, low[:, None, :], 0.0).astype(BF16).reshape(slots, rows)

    outgoing = lax.dot_general(
        place, xt, (((1,), (1,)), ((), ())), preferred_element_type=F32
    ).astype(BF16)
    x = exchange(outgoing.reshape(ep, capacity, -1), "ep").reshape(slots, -1)

    part = jnp.dot(x, w_gu, preferred_element_type=F32).reshape(
        spread, slots // spread, 2 * units
    )
    others = exchange(part.astype(BF16), "tp", near).astype(F32)
    own = lax.dynamic_index_in_dim(part, me, 0, keepdims=False)
    keep = (jnp.arange(spread) != me)[:, None, None]
    acts = own + jnp.sum(jnp.where(keep, others, 0.0), axis=0)
    share_hidden = (jax.nn.silu(acts[:, :units]) * acts[:, units:]).astype(BF16)
    hidden = exchange(
        jnp.broadcast_to(share_hidden[None], (spread,) + share_hidden.shape), "tp", near
    ).reshape(slots, units)
    result = lax.dot_general(
        hidden, w_down, (((1,), (1,)), ((), ())), preferred_element_type=F32
    ).astype(BF16)
    back = exchange(result.reshape(ep, capacity, -1), "ep").reshape(slots, -1)

    over_slots = (((0,), (0,)), ((), ()))
    mixed = lax.dot_general(
        back, mix_high, over_slots, preferred_element_type=F32
    ) + lax.dot_general(back, mix_low, over_slots, preferred_element_type=F32)
    mixed = mixed.reshape(members, share, rows)
    parts = exchange(mixed.astype(BF16), "tp", far)
    out = jnp.sum(parts.astype(F32), axis=0).astype(BF16)
    return out.T


def solution(mesh):
    in_specs = (
        P("ep", "tp"),
        P("ep", None),
        P("ep", None),
        P("ep", "tp", None),
        P("ep", "tp", None),
        P("ep", "tp", None),
    )
    return jax.shard_map(
        on_device, mesh=mesh, in_specs=in_specs, out_specs=P("ep", "tp"), check_vma=False
    )
```

time: 461 us -> 315 us (0.68)
  waiting for transfers between devices: 206 us -> 106 us
  local copies, waits for them, and re-layouts: 47.9 us -> 2.64 us
  starting transfers between devices: 28.6 us -> 64.3 us
  matrix products: 18.9 us -> 4.7 us
  between operations: 13.7 us -> 0.21 us
  blocking collectives: 141 us -> 129 us
    all_gather x2 -> x0, waiting for transfers between devices: 198 us -> none  [the longest x1 125 us: on_device(): portion = lax.all_gather(hidden_share, 'tp', axis=0, tiled=True)]
    all_to_all x1 -> x5, waiting for transfers between devices: 8.62 us -> 106 us  [exchange(): lax.all_to_all(x, axis, split_axis=0, concat_axis=0, tiled=True, axis_ind...]
    all_to_all x1 -> x5, starting transfers between devices: 28.6 us -> 64.3 us  [exchange(): lax.all_to_all(x, axis, split_axis=0, concat_axis=0, tiled=True, axis_ind...]
    all_gather x2 -> x0, local copies, waits for them, and re-layouts: 15.5 us -> none  [the longest x1 12.4 us: on_device(): portion = lax.all_gather(arrived, 'tp', axis=1, tiled=True)]
    dot_general x3 -> x6, matrix products: 18.9 us -> 4.7 us  [the longest x1 1.46 us: on_device(): jnp.dot(x, w_gu, preferred_element_type=F32)]
    all_to_all x2 -> x3, blocking collectives: 141 us -> 129 us  [exchange(): lax.all_to_all(x, axis, split_axis=0, concat_axis=0, tiled=True, axis_ind...]
    gather x2 -> x0, local copies, waits for them, and re-layouts: 9.4 us -> none  [the longest x1 6.19 us: on_device(): outgoing = jnp.take(tokens, owners, axis=0)]
    unnamed x22 -> x8, local copies, waits for them, and re-layouts: 7.36 us -> 0.02 us
  transfers between devices with their start and end apart: 3 -> 5, of which waited for: 3 -> 5; matrix products, arithmetic and copies ran while one was open for 2% -> 1% of each run, Pallas kernels for 0% -> 0%
where the time goes in v1:
time: 315 us; the launch traced here: 310 us
  blocking collectives  129 us (41%)
  waiting for transfers between devices  106 us (34%)
  starting transfers between devices  64.3 us (20%)
  matrix products  4.7 us (1%)
    all_to_all x3, blocking collectives, exchange(): lax.all_to_all(x, axis, split_axis=0, concat_axis=0, tiled=True, axis_ind...  129 us
    all_to_all x5, waiting for transfers between devices, exchange(): lax.all_to_all(x, axis, split_axis=0, concat_axis=0, tiled=True, axis_ind...  106 us
    all_to_all x5, starting transfers between devices, exchange(): lax.all_to_all(x, axis, split_axis=0, concat_axis=0, tiled=True, axis_ind...  64.3 us
  transfers between devices with their start and end apart: 5, of which 5 were waited for; matrix products, arithmetic and copies ran while one was open for 1% of the time, Pallas kernels for 0%

profile of v1, /device:TPU:1, one launch (start us, length us, event | category | flops | bytes accessed | tf_op | source)
XLA Modules:
  0.0 309.8 jit_solution(14488635713207077216)
XLA Ops:
  0.0 1.4 broadcast_in_dim.65
  1.4 28.9 %all-to-all-start = ((bf16[8,64,128]{2,1,0:T(8,128)(2,1)}), bf16[8,64,128]{2,1,0:T(8,128)(2,1)S(1)}, u32[]{:S(2)}, u32[]{:S(2)}) async-start(bf16[8,64,128]{2,1,0:T(8,128)(2,1)} %broadcast_in_dim.65), calls=%async_computation | async-start | bytes 262144 | tf_op jit(solution)/shard_map/all_to_all | solution.py:11
  30.3 0.8 compare_reduce_fusion
  31.4 1.1 fusion.12
  32.5 22.6 %all-to-all-done = bf16[8,64,128]{2,1,0:T(8,128)(2,1)S(1)} async-done(((bf16[8,64,128]{2,1,0:T(8,128)(2,1)}), bf16[8,64,128]{2,1,0:T(8,128)(2,1)S(1)}, u32[]{:S(2)}, u32[]{:S(2)}) %all-to-all-start) | async-done | bytes 131104 | tf_op jit(solution)/shard_map/all_to_all | solution.py:11
  55.1 1.1 convolution_convert_fusion.1
  56.2 11.0 %all-to-all-start.1 = ((bf16[32,16,512]{2,1,0:T(8,128)(2,1)}), bf16[32,16,512]{2,1,0:T(8,128)(2,1)S(1)}, u32[]{:S(2)}, u32[]{:S(2)}) async-start(bf16[32,16,512]{2,1,0:T(8,128)(2,1)} %bitcast.4), calls=%async_computation.1 | async-start | bytes 1048576 | tf_op jit(solution)/shard_map/all_to_all | solution.py:11
  67.4 11.2 %all-to-all-done.1 = bf16[32,16,512]{2,1,0:T(8,128)(2,1)S(1)} async-done(((bf16[32,16,512]{2,1,0:T(8,128)(2,1)}), bf16[32,16,512]{2,1,0:T(8,128)(2,1)S(1)}, u32[]{:S(2)}, u32[]{:S(2)}) %all-to-all-start.1) | async-done | bytes 524320 | tf_op jit(solution)/shard_map/all_to_all | solution.py:11
  78.6 84.1 %all_to_all.40 = bf16[8,64,768]{2,1,0:T(8,128)(2,1)S(1)} all-to-all(bf16[8,64,768]{2,1,0:T(8,128)(2,1)S(1)} %pad_maximum_fusion), channel_id=1, replica_groups={{0,4,8,12,16,20,24,28},{1,5,9,13,17,21,25,29},{2,6,10,14,18,22,26,30},{..., dimensions={0} | all-to-all | bytes 1572864 | tf_op jit(solution)/shard_map/all_to_all | solution.py:11
  162.8 1.5 fusion.14
  164.2 3.6 %all-to-all-start.3 = ((bf16[4,128,768]{2,1,0:T(8,128)(2,1)}), bf16[4,128,768]{2,1,0:T(8,128)(2,1)S(1)}, u32[]{:S(2)}, u32[]{:S(2)}) async-start(bf16[4,128,768]{2,1,0:T(8,128)(2,1)} %get-tuple-element.13), calls=%async_computation.3 | async-start | bytes 1572864 | tf_op jit(solution)/shard_map/all_to_all | solution.py:11
  167.9 0.8 pad_maximum_fusion.3
  168.7 18.8 %all-to-all-done.3 = bf16[4,128,768]{2,1,0:T(8,128)(2,1)S(1)} async-done(((bf16[4,128,768]{2,1,0:T(8,128)(2,1)}), bf16[4,128,768]{2,1,0:T(8,128)(2,1)S(1)}, u32[]{:S(2)}, u32[]{:S(2)}) %all-to-all-start.3) | async-done | bytes 786464 | tf_op jit(solution)/shard_map/all_to_all | solution.py:11
  187.5 11.5 %all-to-all-start.5 = ((bf16[8,64,384]{2,1,0:T(8,128)(2,1)}), bf16[8,64,384]{2,1,0:T(8,128)(2,1)S(1)}, u32[]{:S(2)}, u32[]{:S(2)}) async-start(bf16[8,64,384]{2,1,0:T(8,128)(2,1)} %bitcast.12), calls=%async_computation.5 | async-start | bytes 786432 | tf_op jit(solution)/shard_map/all_to_all | solution.py:11
  198.9 0.2 select_reduce_fusion
  199.3 41.8 %all-to-all-done.5 = bf16[8,64,384]{2,1,0:T(8,128)(2,1)S(1)} async-done(((bf16[8,64,384]{2,1,0:T(8,128)(2,1)}), bf16[8,64,384]{2,1,0:T(8,128)(2,1)S(1)}, u32[]{:S(2)}, u32[]{:S(2)}) %all-to-all-start.5) | async-done | bytes 393248 | tf_op jit(solution)/shard_map/all_to_all | solution.py:11
  241.1 12.4 %all_to_all.41 = bf16[4,128,384]{2,1,0:T(8,128)(2,1)S(1)} all-to-all(bf16[4,128,384]{2,1,0:T(8,128)(2,1)S(1)} %broadcast_in_dim.68), channel_id=1, replica_groups={{0,1,2,3},{4,5,6,7},{8,9,10,11},{12,13,14,15},{16,17,18,19},{20,21,22,2..., dimensions={0} | all-to-all | bytes 786432 | tf_op jit(solution)/shard_map/all_to_all | solution.py:11
  253.6 1.3 convolution_convert_fusion
  254.8 9.3 %all-to-all-start.6 = ((bf16[32,16,512]{2,1,0:T(8,128)(2,1)}), bf16[32,16,512]{2,1,0:T(8,128)(2,1)S(1)}, u32[]{:S(2)}, u32[]{:S(2)}) async-start(bf16[32,16,512]{2,1,0:T(8,128)(2,1)} %bitcast.14), calls=%async_computation.6 | async-start | bytes 1048576 | tf_op jit(solution)/shard_map/all_to_all | solution.py:11
  264.3 11.3 %all-to-all-done.6 = bf16[32,16,512]{2,1,0:T(8,128)(2,1)S(1)} async-done(((bf16[32,16,512]{2,1,0:T(8,128)(2,1)}), bf16[32,16,512]{2,1,0:T(8,128)(2,1)S(1)}, u32[]{:S(2)}, u32[]{:S(2)}) %all-to-all-start.6) | async-done | bytes 524320 | tf_op jit(solution)/shard_map/all_to_all | solution.py:11
  275.6 0.4 convolution_bitcast_fusion
  276.0 0.4 fusion.1
  276.4 32.8 %all_to_all.42 = bf16[8,64,128]{2,1,0:T(8,128)(2,1)S(1)} all-to-all(bf16[8,64,128]{2,1,0:T(8,128)(2,1)S(1)} %bitcast.45), channel_id=1, replica_groups={{0,4,8,12,16,20,24,28},{1,5,9,13,17,21,25,29},{2,6,10,14,18,22,26,30},{..., dimensions={0} | all-to-all | bytes 262144 | tf_op jit(solution)/shard_map/all_to_all | solution.py:11
  309.2 0.6 reduce_sum.32
  (23 shorter events, 0.8 us)
Async XLA Ops:
  1.4 53.7 %all-to-all-start = ((bf16[8,64,128]{2,1,0:T(8,128)(2,1)}), bf16[8,64,128]{2,1,0:T(8,128)(2,1)S(1)}, u32[]{:S(2)}, u32[]{:S(2)}) async-start(bf16[8,64,128]{2,1,0:T(8,128)(2,1)} %broadcast_in_dim.65), calls=%async_computation | async-start | bytes 262144 | tf_op jit(solution)/shard_map/all_to_all | solution.py:11
  31.3 35.9 %copy-start = (bf16[4,64,768]{2,1,0:T(8,128)(2,1)S(1)}, bf16[4,64,768]{2,1,0:T(8,128)(2,1)}, u32[]{:S(2)}) copy-start(bf16[4,64,768]{2,1,0:T(8,128)(2,1)} %param.10) | copy-start | bytes 1179652
  56.2 22.4 %all-to-all-start.1 = ((bf16[32,16,512]{2,1,0:T(8,128)(2,1)}), bf16[32,16,512]{2,1,0:T(8,128)(2,1)S(1)}, u32[]{:S(2)}, u32[]{:S(2)}) async-start(bf16[32,16,512]{2,1,0:T(8,128)(2,1)} %bitcast.4), calls=%async_computation.1 | async-start | bytes 1048576 | tf_op jit(solution)/shard_map/all_to_all | solution.py:11
  164.2 3.6 %copy-start.1 = (bf16[4,64,768]{2,1,0:T(8,128)(2,1)S(1)}, bf16[4,64,768]{2,1,0:T(8,128)(2,1)}, u32[]{:S(2)}) copy-start(bf16[4,64,768]{2,1,0:T(8,128)(2,1)} %param.11) | copy-start | bytes 1179652
  164.2 23.3 %all-to-all-start.3 = ((bf16[4,128,768]{2,1,0:T(8,128)(2,1)}), bf16[4,128,768]{2,1,0:T(8,128)(2,1)S(1)}, u32[]{:S(2)}, u32[]{:S(2)}) async-start(bf16[4,128,768]{2,1,0:T(8,128)(2,1)} %get-tuple-element.13), calls=%async_computation.3 | async-start | bytes 1572864 | tf_op jit(solution)/shard_map/all_to_all | solution.py:11
  187.5 53.6 %all-to-all-start.5 = ((bf16[8,64,384]{2,1,0:T(8,128)(2,1)}), bf16[8,64,384]{2,1,0:T(8,128)(2,1)S(1)}, u32[]{:S(2)}, u32[]{:S(2)}) async-start(bf16[8,64,384]{2,1,0:T(8,128)(2,1)} %bitcast.12), calls=%async_computation.5 | async-start | bytes 786432 | tf_op jit(solution)/shard_map/all_to_all | solution.py:11
  241.1 23.1 %copy-start.2 = (s32[128,8]{0,1:T(8,128)S(1)}, s32[128,8]{0,1:T(8,128)}, u32[]{:S(2)}) copy-start(s32[128,8]{0,1:T(8,128)} %param.7) | copy-start | bytes 12292
  241.1 23.1 %copy-start.3 = (s32[128,8]{0,1:T(8,128)S(1)}, s32[128,8]{0,1:T(8,128)}, u32[]{:S(2)}) copy-start(s32[128,8]{0,1:T(8,128)} %param.8) | copy-start | bytes 12292
  254.8 20.8 %all-to-all-start.6 = ((bf16[32,16,512]{2,1,0:T(8,128)(2,1)}), bf16[32,16,512]{2,1,0:T(8,128)(2,1)S(1)}, u32[]{:S(2)}, u32[]{:S(2)}) async-start(bf16[32,16,512]{2,1,0:T(8,128)(2,1)} %bitcast.14), calls=%async_computation.6 | async-start | bytes 1048576 | tf_op jit(solution)/shard_map/all_to_all | solution.py:11

commit v2 on v1

v2 whole, which is shorter than its diff:
```python
import jax
import jax.numpy as jnp
from jax import lax
from jax.sharding import PartitionSpec as P

F32 = jnp.float32
BF16 = jnp.bfloat16


def exchange(x, axis, groups=None):
    return lax.all_to_all(
        x, axis, split_axis=0, concat_axis=0, tiled=True, axis_index_groups=groups
    )


def turned(x, amount):
    n = x.shape[0]
    return lax.dynamic_slice_in_dim(jnp.concatenate([x, x], axis=0), amount, n, axis=0)


def on_device(tokens, routing, gate_fixed, gate_weight, up_weight, down_weight):
    ep = lax.axis_size("ep")
    tp = lax.axis_size("tp")
    local, share, units = gate_weight.shape
    rows, top = routing.shape
    capacity = max(2, rows * top * 2 // (local * ep))
    ring = tp // local
    half = ring // 2
    slots = ep * capacity
    chunk = slots // ring
    cut = chunk // 2
    near = [[p * local + r for r in range(local)] for p in range(ring)]
    z = lax.axis_index("tp")
    me = lax.rem(z, local)
    here = lax.div(z, local)

    def along(x, step):
        return lax.ppermute(
            x, "tp", [(i, (i + step * local) % tp) for i in range(tp)]
        )

    def beside(x, k):
        return lax.ppermute(
            x, "tp", [(g[i], g[(i + k) % local]) for g in near for i in range(local)]
        )

    def weight_block(k):
        e = lax.rem(me + k, local)
        return jnp.concatenate(
            [
                lax.dynamic_index_in_dim(w, e, 0, keepdims=False)
                for w in (gate_weight, up_weight, down_weight)
            ],
            axis=1,
        )

    blocks = [weight_block(0)] + [beside(weight_block(k), k) for k in range(1, local)]
    w_gu = jnp.concatenate([b[:, : 2 * units] for b in blocks], axis=0)
    w_down = jnp.concatenate([b[:, 2 * units :] for b in blocks], axis=0)

    xt = exchange(jnp.broadcast_to(tokens.T[None], (local, share, rows)), "tp", near)
    order = [lax.rem(me - k + local, local) for k in range(local)]
    xt = jnp.concatenate(
        [lax.dynamic_index_in_dim(xt, o, 0, keepdims=False) for o in order], axis=0
    )

    rt = routing.T
    expert = jnp.arange(ep, dtype=jnp.int32) * local + me
    hit = rt[:, None, :] == expert[None, :, None]
    named = jnp.any(hit, axis=0)
    scale = jnp.sum(jnp.where(hit, gate_fixed.T[:, None, :], 0), axis=0)
    t = jnp.arange(rows)
    before = (t[:, None] < t[None, :]).astype(BF16)
    position = jnp.dot(named.astype(BF16), before, preferred_element_type=F32)
    slot = jnp.arange(capacity).astype(F32)[None, :, None]
    pick = named[:, None, :] & (position[:, None, :] == slot)
    place = pick.astype(BF16).reshape(slots, rows)
    factor = scale.astype(F32) / 65536.0
    mix = jnp.where(pick, factor[:, None, :], 0.0).reshape(slots, rows)

    outgoing = lax.dot_general(
        place, xt, (((1,), (1,)), ((), ())), preferred_element_type=F32
    ).astype(BF16)
    x = exchange(outgoing.reshape(ep, capacity, -1), "ep")

    x = turned(x.reshape(ring, chunk, -1), here).reshape(slots, -1)
    part = jnp.dot(x, w_gu, preferred_element_type=F32).reshape(ring, chunk, 2 * units)
    plus = along(part[half, :cut].astype(BF16), 1)
    minus = along(part[half, cut:].astype(BF16), -1)
    for k in range(half - 1, 0, -1):
        up, down = part[k], part[ring - k]
        if k == half - 1:
            up = jnp.concatenate([up[:cut] + plus.astype(F32), up[cut:]], axis=0)
            down = jnp.concatenate([down[:cut], down[cut:] + minus.astype(F32)], axis=0)
        else:
            up = up + plus.astype(F32)
            down = down + minus.astype(F32)
        plus = along(up.astype(BF16), 1)
        minus = along(down.astype(BF16), -1)
    acts = part[0] + (plus.astype(F32) + minus.astype(F32))
    own = (jax.nn.silu(acts[:, :units]) * acts[:, units:]).astype(BF16)

    hidden = [own] + [None] * (ring - 1)
    left = right = own
    for k in range(1, half):
        left, right = along(left, 1), along(right, -1)
        hidden[ring - k], hidden[k] = left, right
    hidden[half] = jnp.concatenate([along(left[:cut], 1), along(right[cut:], -1)], axis=0)
    result = lax.dot_general(
        jnp.concatenate(hidden, axis=0),
        w_down,
        (((1,), (1,)), ((), ())),
        preferred_element_type=F32,
    )
    result = turned(result.reshape(ring, chunk, -1), lax.rem(ring - here, ring))
    back = exchange(result.reshape(ep, capacity, -1), "ep").reshape(slots, -1)

    mixed = lax.dot_general(
        back,
        mix,
        (((0,), (0,)), ((), ())),
        precision=lax.Precision.HIGHEST,
        preferred_element_type=F32,
    ).reshape(local, share, rows)
    mixed = jnp.stack([lax.dynamic_index_in_dim(mixed, o, 0, keepdims=False) for o in order])
    parts = exchange(mixed, "tp", near)
    return jnp.sum(parts, axis=0).astype(BF16).T


def solution(mesh):
    in_specs = (
        P("ep", "tp"),
        P("ep", None),
        P("ep", None),
        P("ep", "tp", None),
        P("ep", "tp", None),
        P("ep", "tp", None),
    )
    return jax.shard_map(
        on_device, mesh=mesh, in_specs=in_specs, out_specs=P("ep", "tp"), check_vma=False
    )
```

time: 315 us -> 239 us (0.76); the launches traced: 310 us -> 238 us
  blocking collectives: 129 us -> 23.5 us
  starting transfers between devices: 64.3 us -> 150 us
  waiting for transfers between devices: 106 us -> 54.5 us
    ppermute x0 -> x19, starting transfers between devices: none -> 110 us  [the longest x16 100 us: along(): lax.ppermute(x, 'tp', [(i, (i + step * local) % tp) for i in range(tp)])]
    all_to_all x3 -> x1, blocking collectives: 129 us -> 23.5 us  [exchange(): lax.all_to_all(x, axis, split_axis=0, concat_axis=0, tiled=True, axis_ind...]
    all_to_all x5 -> x3, waiting for transfers between devices: 106 us -> 20 us  [exchange(): lax.all_to_all(x, axis, split_axis=0, concat_axis=0, tiled=True, axis_ind...]
    ppermute x0 -> x19, waiting for transfers between devices: none -> 34.5 us  [the longest x16 34.5 us: along(): lax.ppermute(x, 'tp', [(i, (i + step * local) % tp) for i in range(tp)])]
    all_to_all x5 -> x3, starting transfers between devices: 64.3 us -> 40.1 us  [exchange(): lax.all_to_all(x, axis, split_axis=0, concat_axis=0, tiled=True, axis_ind...]
  transfers between devices with their start and end apart: 5 -> 22, of which waited for: 5 -> 12; matrix products, arithmetic and copies ran while one was open for 1% -> 2% of each run, Pallas kernels for 0% -> 0%
where the time goes in v2:
time: 239 us; the launch traced here: 238 us
  starting transfers between devices  150 us (63%)
  waiting for transfers between devices  54.5 us (23%)
  blocking collectives  23.5 us (10%)
  local copies, waits for them, and re-layouts  4.18 us (2%)
  matrix products  2.62 us (1%)
  other arithmetic  2.52 us (1%)
    ppermute x16, starting transfers between devices, along(): lax.ppermute(x, 'tp', [(i, (i + step * local) % tp) for i in range(tp)])  100 us
    all_to_all x3, starting transfers between devices, exchange(): lax.all_to_all(x, axis, split_axis=0, concat_axis=0, tiled=True, axis_ind...  40.1 us
    ppermute x16, waiting for transfers between devices, along(): lax.ppermute(x, 'tp', [(i, (i + step * local) % tp) for i in range(tp)])  34.5 us
    all_to_all x1, blocking collectives, exchange(): lax.all_to_all(x, axis, split_axis=0, concat_axis=0, tiled=True, axis_ind...  23.5 us
    all_to_all x3, waiting for transfers between devices, exchange(): lax.all_to_all(x, axis, split_axis=0, concat_axis=0, tiled=True, axis_ind...  20 us
    ppermute x3, starting transfers between devices, beside(): lax.ppermute(x, 'tp', [(g[i], g[(i + k) % local]) for g in near for i in...  9.55 us
  transfers between devices with their start and end apart: 22, of which 12 were waited for; matrix products, arithmetic and copies ran while one was open for 2% of the time, Pallas kernels for 0%

profile of v2, /device:TPU:1, one launch (start us, length us, event | category | flops | bytes accessed | tf_op | source)
XLA Modules:
  0.0 237.9 jit_solution(1264037527392556315)
XLA Ops:
  1.3 6.4 %all-to-all-start = ((bf16[4,64,128]{2,1,0:T(8,128)(2,1)}), bf16[4,64,128]{2,1,0:T(8,128)(2,1)S(1)}, u32[]{:S(2)}, u32[]{:S(2)}) async-start(bf16[4,64,128]{2,1,0:T(8,128)(2,1)} %broadcast_in_dim.22), calls=%async_computation | async-start | bytes 131072 | tf_op jit(solution)/shard_map/all_to_all | solution.py:11
  10.2 4.3 %collective-permute-start.1 = (bf16[64,2304]{1,0:T(8,128)(2,1)S(1)}, bf16[64,2304]{1,0:T(8,128)(2,1)S(1)}, u32[]{:S(2)}, u32[]{:S(2)}) collective-permute-start(bf16[64,2304]{1,0:T(8,128)(2,1)S(1)} %pad_maximum_fusion.1), channel_id=1, source_target_pairs={{0,2},{1,3},{2,0},{3,1},{4,6},{5,7},{6,4},{7,5},{8,10},{9,11},{10,... | collective-permute-start | bytes 884744 | tf_op jit(solution)/shard_map/ppermute | solution.py:43
  14.5 3.1 %collective-permute-start.2 = (bf16[64,2304]{1,0:T(8,128)(2,1)S(1)}, bf16[64,2304]{1,0:T(8,128)(2,1)S(1)}, u32[]{:S(2)}, u32[]{:S(2)}) collective-permute-start(bf16[64,2304]{1,0:T(8,128)(2,1)S(1)} %pad_maximum_fusion.2), channel_id=1, source_target_pairs={{0,3},{1,0},{2,1},{3,2},{4,7},{5,4},{6,5},{7,6},{8,11},{9,8},{10,9... | collective-permute-start | bytes 884744 | tf_op jit(solution)/shard_map/ppermute | solution.py:43
  17.6 2.2 collective-permute-start
  21.3 15.6 %all-to-all-start.1 = ((bf16[32,16,256]{2,1,0:T(8,128)(2,1)}), bf16[32,16,256]{2,1,0:T(8,128)(2,1)S(1)}, u32[]{:S(2)}, u32[]{:S(2)}) async-start(bf16[32,16,256]{2,1,0:T(8,128)(2,1)} %bitcast.8), calls=%async_computation.1 | async-start | bytes 524288 | tf_op jit(solution)/shard_map/all_to_all | solution.py:11
  37.0 8.8 %all-to-all-done.1 = bf16[32,16,256]{2,1,0:T(8,128)(2,1)S(1)} async-done(((bf16[32,16,256]{2,1,0:T(8,128)(2,1)}), bf16[32,16,256]{2,1,0:T(8,128)(2,1)S(1)}, u32[]{:S(2)}, u32[]{:S(2)}) %all-to-all-start.1) | async-done | bytes 262176 | tf_op jit(solution)/shard_map/all_to_all | solution.py:11
  46.5 2.3 collective-permute-start.3
  48.8 10.2 %collective-permute-start.7 = (bf16[32,1536]{1,0:T(8,128)(2,1)S(1)}, bf16[32,1536]{1,0:T(8,128)(2,1)S(1)}, u32[]{:S(2)}, u32[]{:S(2)}) collective-permute-start(bf16[32,1536]{1,0:T(8,128)(2,1)S(1)} %get-tuple-element.12), channel_id=1, source_target_pairs={{0,28},{1,29},{2,30},{3,31},{4,0},{5,1},{6,2},{7,3},{8,4},{9,5},{1... | collective-permute-start | bytes 294920 | tf_op jit(solution)/shard_map/ppermute | solution.py:38
  61.1 8.2 %collective-permute-start.4 = (bf16[64,1536]{1,0:T(8,128)(2,1)S(1)}, bf16[64,1536]{1,0:T(8,128)(2,1)S(1)}, u32[]{:S(2)}, u32[]{:S(2)}) collective-permute-start(bf16[64,1536]{1,0:T(8,128)(2,1)S(1)} %pad_maximum_fusion.3), channel_id=1, source_target_pairs={{0,4},{1,5},{2,6},{3,7},{4,8},{5,9},{6,10},{7,11},{8,12},{9,13},{1... | collective-permute-start | bytes 589832 | tf_op jit(solution)/shard_map/ppermute | solution.py:38
  71.2 2.4 %collective-permute-done.4 = bf16[64,1536]{1,0:T(8,128)(2,1)S(1)} collective-permute-done((bf16[64,1536]{1,0:T(8,128)(2,1)S(1)}, bf16[64,1536]{1,0:T(8,128)(2,1)S(1)}, u32[]{:S(2)}, u32[]{:S(2)}) %collective-permute-start.4) | collective-permute-done | bytes 196640 | tf_op jit(solution)/shard_map/ppermute | solution.py:38
  73.7 6.1 %collective-permute-start.5 = (bf16[64,1536]{1,0:T(8,128)(2,1)S(1)}, bf16[64,1536]{1,0:T(8,128)(2,1)S(1)}, u32[]{:S(2)}, u32[]{:S(2)}) collective-permute-start(bf16[64,1536]{1,0:T(8,128)(2,1)S(1)} %fusion.13), channel_id=1, source_target_pairs={{0,4},{1,5},{2,6},{3,7},{4,8},{5,9},{6,10},{7,11},{8,12},{9,13},{1... | collective-permute-start | bytes 589832 | tf_op jit(solution)/shard_map/ppermute | solution.py:38
  79.8 16.7 %collective-permute-done.5 = bf16[64,1536]{1,0:T(8,128)(2,1)S(1)} collective-permute-done((bf16[64,1536]{1,0:T(8,128)(2,1)S(1)}, bf16[64,1536]{1,0:T(8,128)(2,1)S(1)}, u32[]{:S(2)}, u32[]{:S(2)}) %collective-permute-start.5) | collective-permute-done | bytes 196640 | tf_op jit(solution)/shard_map/ppermute | solution.py:38
  96.5 10.1 %collective-permute-start.9 = (bf16[64,1536]{1,0:T(8,128)(2,1)S(1)}, bf16[64,1536]{1,0:T(8,128)(2,1)S(1)}, u32[]{:S(2)}, u32[]{:S(2)}) collective-permute-start(bf16[64,1536]{1,0:T(8,128)(2,1)S(1)} %get-tuple-element.8), channel_id=1, source_target_pairs={{0,28},{1,29},{2,30},{3,31},{4,0},{5,1},{6,2},{7,3},{8,4},{9,5},{1... | collective-permute-start | bytes 589832 | tf_op jit(solution)/shard_map/ppermute | solution.py:38
  110.3 8.0 %collective-permute-start.10 = (bf16[64,1536]{1,0:T(8,128)(2,1)S(1)}, bf16[64,1536]{1,0:T(8,128)(2,1)S(1)}, u32[]{:S(2)}, u32[]{:S(2)}) collective-permute-start(bf16[64,1536]{1,0:T(8,128)(2,1)S(1)} %fusion.12), channel_id=1, source_target_pairs={{0,28},{1,29},{2,30},{3,31},{4,0},{5,1},{6,2},{7,3},{8,4},{9,5},{1... | collective-permute-start | bytes 589832 | tf_op jit(solution)/shard_map/ppermute | solution.py:38
  118.3 6.7 %collective-permute-done.10 = bf16[64,1536]{1,0:T(8,128)(2,1)S(1)} collective-permute-done((bf16[64,1536]{1,0:T(8,128)(2,1)S(1)}, bf16[64,1536]{1,0:T(8,128)(2,1)S(1)}, u32[]{:S(2)}, u32[]{:S(2)}) %collective-permute-start.10) | collective-permute-done | bytes 196640 | tf_op jit(solution)/shard_map/ppermute | solution.py:38
  127.1 7.3 %collective-permute-start.11 = (bf16[64,768]{1,0:T(8,128)(2,1)S(1)}, bf16[64,768]{1,0:T(8,128)(2,1)S(1)}, u32[]{:S(2)}, u32[]{:S(2)}) collective-permute-start(bf16[64,768]{1,0:T(8,128)(2,1)S(1)} %get-tuple-element.6), channel_id=1, source_target_pairs={{0,28},{1,29},{2,30},{3,31},{4,0},{5,1},{6,2},{7,3},{8,4},{9,5},{1... | collective-permute-start | bytes 294920 | tf_op jit(solution)/shard_map/ppermute | solution.py:38
  134.5 5.5 %collective-permute-start.15 = (bf16[64,768]{1,0:T(8,128)(2,1)S(1)}, bf16[64,768]{1,0:T(8,128)(2,1)S(1)}, u32[]{:S(2)}, u32[]{:S(2)}) collective-permute-start(bf16[64,768]{1,0:T(8,128)(2,1)S(1)} %collective-permute-done.14), channel_id=1, source_target_pairs={{0,4},{1,5},{2,6},{3,7},{4,8},{5,9},{6,10},{7,11},{8,12},{9,13},{1... | collective-permute-start | bytes 294920 | tf_op jit(solution)/shard_map/ppermute | solution.py:38
  140.1 16.6 %collective-permute-start.12 = (bf16[64,768]{1,0:T(8,128)(2,1)S(1)}, bf16[64,768]{1,0:T(8,128)(2,1)S(1)}, u32[]{:S(2)}, u32[]{:S(2)}) collective-permute-start(bf16[64,768]{1,0:T(8,128)(2,1)S(1)} %collective-permute-done.11), channel_id=1, source_target_pairs={{0,28},{1,29},{2,30},{3,31},{4,0},{5,1},{6,2},{7,3},{8,4},{9,5},{1... | collective-permute-start | bytes 294920 | tf_op jit(solution)/shard_map/ppermute | solution.py:38
  158.6 9.2 %collective-permute-start.13 = (bf16[64,768]{1,0:T(8,128)(2,1)S(1)}, bf16[64,768]{1,0:T(8,128)(2,1)S(1)}, u32[]{:S(2)}, u32[]{:S(2)}) collective-permute-start(bf16[64,768]{1,0:T(8,128)(2,1)S(1)} %collective-permute-done.12), channel_id=1, source_target_pairs={{0,28},{1,29},{2,30},{3,31},{4,0},{5,1},{6,2},{7,3},{8,4},{9,5},{1... | collective-permute-start | bytes 294920 | tf_op jit(solution)/shard_map/ppermute | solution.py:38
  170.0 3.2 %collective-permute-start.17 = (bf16[32,768]{1,0:T(8,128)(2,1)S(1)}, bf16[32,768]{1,0:T(8,128)(2,1)S(1)}, u32[]{:S(2)}, u32[]{:S(2)}) collective-permute-start(bf16[32,768]{1,0:T(8,128)(2,1)S(1)} %slice.119), channel_id=1, source_target_pairs={{0,4},{1,5},{2,6},{3,7},{4,8},{5,9},{6,10},{7,11},{8,12},{9,13},{1... | collective-permute-start | bytes 147464 | tf_op jit(solution)/shard_map/ppermute | solution.py:38
  173.2 6.0 %collective-permute-start.18 = (bf16[32,768]{1,0:T(8,128)(2,1)S(1)}, bf16[32,768]{1,0:T(8,128)(2,1)S(1)}, u32[]{:S(2)}, u32[]{:S(2)}) collective-permute-start(bf16[32,768]{1,0:T(8,128)(2,1)S(1)} %slice.120), channel_id=1, source_target_pairs={{0,28},{1,29},{2,30},{3,31},{4,0},{5,1},{6,2},{7,3},{8,4},{9,5},{1... | collective-permute-start | bytes 147464 | tf_op jit(solution)/shard_map/ppermute | solution.py:38
  183.4 18.1 %all-to-all-start.2 = ((f32[32,16,256]{2,1,0:T(8,128)}), f32[32,16,256]{2,1,0:T(8,128)S(1)}, u32[]{:S(2)}, u32[]{:S(2)}) async-start(f32[32,16,256]{2,1,0:T(8,128)} %bitcast.27), calls=%async_computation.2 | async-start | bytes 1048576 | tf_op jit(solution)/shard_map/all_to_all | solution.py:11
  201.7 11.2 %all-to-all-done.2 = f32[32,16,256]{2,1,0:T(8,128)S(1)} async-done(((f32[32,16,256]{2,1,0:T(8,128)}), f32[32,16,256]{2,1,0:T(8,128)S(1)}, u32[]{:S(2)}, u32[]{:S(2)}) %all-to-all-start.2) | async-done | bytes 524320 | tf_op jit(solution)/shard_map/all_to_all | solution.py:11
  213.8 23.5 %all_to_all.20 = f32[4,64,128]{2,1,0:T(8,128)S(1)} all-to-all(f32[4,64,128]{2,1,0:T(8,128)S(1)} %pad_maximum_fusion.5), channel_id=1, replica_groups={{0,1,2,3},{4,5,6,7},{8,9,10,11},{12,13,14,15},{16,17,18,19},{20,21,22,2..., dimensions={0} | all-to-all | bytes 262144 | tf_op jit(solution)/shard_map/all_to_all | solution.py:11
  (87 shorter events, 25.7 us)
Async XLA Ops:
  1.3 19.0 %all-to-all-start = ((bf16[4,64,128]{2,1,0:T(8,128)(2,1)}), bf16[4,64,128]{2,1,0:T(8,128)(2,1)S(1)}, u32[]{:S(2)}, u32[]{:S(2)}) async-start(bf16[4,64,128]{2,1,0:T(8,128)(2,1)} %broadcast_in_dim.22), calls=%async_computation | async-start | bytes 131072 | tf_op jit(solution)/shard_map/all_to_all | solution.py:11
  10.2 26.7 %collective-permute-start.1 = (bf16[64,2304]{1,0:T(8,128)(2,1)S(1)}, bf16[64,2304]{1,0:T(8,128)(2,1)S(1)}, u32[]{:S(2)}, u32[]{:S(2)}) collective-permute-start(bf16[64,2304]{1,0:T(8,128)(2,1)S(1)} %pad_maximum_fusion.1), channel_id=1, source_target_pairs={{0,2},{1,3},{2,0},{3,1},{4,6},{5,7},{6,4},{7,5},{8,10},{9,11},{10,... | collective-permute-start | bytes 884744 | tf_op jit(solution)/shard_map/ppermute | solution.py:43
  14.5 22.4 %collective-permute-start.2 = (bf16[64,2304]{1,0:T(8,128)(2,1)S(1)}, bf16[64,2304]{1,0:T(8,128)(2,1)S(1)}, u32[]{:S(2)}, u32[]{:S(2)}) collective-permute-start(bf16[64,2304]{1,0:T(8,128)(2,1)S(1)} %pad_maximum_fusion.2), channel_id=1, source_target_pairs={{0,3},{1,0},{2,1},{3,2},{4,7},{5,4},{6,5},{7,6},{8,11},{9,8},{10,9... | collective-permute-start | bytes 884744 | tf_op jit(solution)/shard_map/ppermute | solution.py:43
  17.6 19.3 %collective-permute-start = (bf16[64,2304]{1,0:T(8,128)(2,1)S(1)}, bf16[64,2304]{1,0:T(8,128)(2,1)S(1)}, u32[]{:S(2)}, u32[]{:S(2)}) collective-permute-start(bf16[64,2304]{1,0:T(8,128)(2,1)S(1)} %pad_maximum_fusion), channel_id=1, source_target_pairs={{0,1},{1,2},{2,3},{3,0},{4,5},{5,6},{6,7},{7,4},{8,9},{9,10},{10,1... | collective-permute-start | bytes 884744 | tf_op jit(solution)/shard_map/ppermute | solution.py:43
  21.3 24.6 %all-to-all-start.1 = ((bf16[32,16,256]{2,1,0:T(8,128)(2,1)}), bf16[32,16,256]{2,1,0:T(8,128)(2,1)S(1)}, u32[]{:S(2)}, u32[]{:S(2)}) async-start(bf16[32,16,256]{2,1,0:T(8,128)(2,1)} %bitcast.8), calls=%async_computation.1 | async-start | bytes 524288 | tf_op jit(solution)/shard_map/all_to_all | solution.py:11
  36.9 97.5 %copy-start = (bf16[64,2304]{1,0:T(8,128)(2,1)}, bf16[64,2304]{1,0:T(8,128)(2,1)S(1)}, u32[]{:S(2)}) copy-start(bf16[64,2304]{1,0:T(8,128)(2,1)S(1)} %collective-permute-done.1) | copy-start | bytes 884740
  36.9 97.5 %copy-start.1 = (bf16[64,2304]{1,0:T(8,128)(2,1)}, bf16[64,2304]{1,0:T(8,128)(2,1)S(1)}, u32[]{:S(2)}) copy-start(bf16[64,2304]{1,0:T(8,128)(2,1)S(1)} %collective-permute-done.2) | copy-start | bytes 884740
  46.5 13.6 %collective-permute-start.3 = (bf16[32,1536]{1,0:T(8,128)(2,1)S(1)}, bf16[32,1536]{1,0:T(8,128)(2,1)S(1)}, u32[]{:S(2)}, u32[]{:S(2)}) collective-permute-start(bf16[32,1536]{1,0:T(8,128)(2,1)S(1)} %get-tuple-element.11), channel_id=1, source_target_pairs={{0,4},{1,5},{2,6},{3,7},{4,8},{5,9},{6,10},{7,11},{8,12},{9,13},{1... | collective-permute-start | bytes 294920 | tf_op jit(solution)/shard_map/ppermute | solution.py:38
  48.8 12.2 %collective-permute-start.7 = (bf16[32,1536]{1,0:T(8,128)(2,1)S(1)}, bf16[32,1536]{1,0:T(8,128)(2,1)S(1)}, u32[]{:S(2)}, u32[]{:S(2)}) collective-permute-start(bf16[32,1536]{1,0:T(8,128)(2,1)S(1)} %get-tuple-element.12), channel_id=1, source_target_pairs={{0,28},{1,29},{2,30},{3,31},{4,0},{5,1},{6,2},{7,3},{8,4},{9,5},{1... | collective-permute-start | bytes 294920 | tf_op jit(solution)/shard_map/ppermute | solution.py:38
  61.1 12.6 %collective-permute-start.4 = (bf16[64,1536]{1,0:T(8,128)(2,1)S(1)}, bf16[64,1536]{1,0:T(8,128)(2,1)S(1)}, u32[]{:S(2)}, u32[]{:S(2)}) collective-permute-start(bf16[64,1536]{1,0:T(8,128)(2,1)S(1)} %pad_maximum_fusion.3), channel_id=1, source_target_pairs={{0,4},{1,5},{2,6},{3,7},{4,8},{5,9},{6,10},{7,11},{8,12},{9,13},{1... | collective-permute-start | bytes 589832 | tf_op jit(solution)/shard_map/ppermute | solution.py:38
  69.3 10.4 %collective-permute-start.8 = (bf16[64,1536]{1,0:T(8,128)(2,1)S(1)}, bf16[64,1536]{1,0:T(8,128)(2,1)S(1)}, u32[]{:S(2)}, u32[]{:S(2)}) collective-permute-start(bf16[64,1536]{1,0:T(8,128)(2,1)S(1)} %pad_maximum_fusion.4), channel_id=1, source_target_pairs={{0,28},{1,29},{2,30},{3,31},{4,0},{5,1},{6,2},{7,3},{8,4},{9,5},{1... | collective-permute-start | bytes 589832 | tf_op jit(solution)/shard_map/ppermute | solution.py:38
  73.7 22.7 %collective-permute-start.5 = (bf16[64,1536]{1,0:T(8,128)(2,1)S(1)}, bf16[64,1536]{1,0:T(8,128)(2,1)S(1)}, u32[]{:S(2)}, u32[]{:S(2)}) collective-permute-start(bf16[64,1536]{1,0:T(8,128)(2,1)S(1)} %fusion.13), channel_id=1, source_target_pairs={{0,4},{1,5},{2,6},{3,7},{4,8},{5,9},{6,10},{7,11},{8,12},{9,13},{1... | collective-permute-start | bytes 589832 | tf_op jit(solution)/shard_map/ppermute | solution.py:38
  96.5 13.7 %collective-permute-start.9 = (bf16[64,1536]{1,0:T(8,128)(2,1)S(1)}, bf16[64,1536]{1,0:T(8,128)(2,1)S(1)}, u32[]{:S(2)}, u32[]{:S(2)}) collective-permute-start(bf16[64,1536]{1,0:T(8,128)(2,1)S(1)} %get-tuple-element.8), channel_id=1, source_target_pairs={{0,28},{1,29},{2,30},{3,31},{4,0},{5,1},{6,2},{7,3},{8,4},{9,5},{1... | collective-permute-start | bytes 589832 | tf_op jit(solution)/shard_map/ppermute | solution.py:38
  106.7 11.6 %collective-permute-start.6 = (bf16[64,1536]{1,0:T(8,128)(2,1)S(1)}, bf16[64,1536]{1,0:T(8,128)(2,1)S(1)}, u32[]{:S(2)}, u32[]{:S(2)}) collective-permute-start(bf16[64,1536]{1,0:T(8,128)(2,1)S(1)} %get-tuple-element.7), channel_id=1, source_target_pairs={{0,4},{1,5},{2,6},{3,7},{4,8},{5,9},{6,10},{7,11},{8,12},{9,13},{1... | collective-permute-start | bytes 589832 | tf_op jit(solution)/shard_map/ppermute | solution.py:38
  110.3 14.7 %collective-permute-start.10 = (bf16[64,1536]{1,0:T(8,128)(2,1)S(1)}, bf16[64,1536]{1,0:T(8,128)(2,1)S(1)}, u32[]{:S(2)}, u32[]{:S(2)}) collective-permute-start(bf16[64,1536]{1,0:T(8,128)(2,1)S(1)} %fusion.12), channel_id=1, source_target_pairs={{0,28},{1,29},{2,30},{3,31},{4,0},{5,1},{6,2},{7,3},{8,4},{9,5},{1... | collective-permute-start | bytes 589832 | tf_op jit(solution)/shard_map/ppermute | solution.py:38
  125.1 9.4 %collective-permute-start.14 = (bf16[64,768]{1,0:T(8,128)(2,1)S(1)}, bf16[64,768]{1,0:T(8,128)(2,1)S(1)}, u32[]{:S(2)}, u32[]{:S(2)}) collective-permute-start(bf16[64,768]{1,0:T(8,128)(2,1)S(1)} %get-tuple-element.6), channel_id=1, source_target_pairs={{0,4},{1,5},{2,6},{3,7},{4,8},{5,9},{6,10},{7,11},{8,12},{9,13},{1... | collective-permute-start | bytes 294920 | tf_op jit(solution)/shard_map/ppermute | solution.py:38
  127.1 13.0 %collective-permute-start.11 = (bf16[64,768]{1,0:T(8,128)(2,1)S(1)}, bf16[64,768]{1,0:T(8,128)(2,1)S(1)}, u32[]{:S(2)}, u32[]{:S(2)}) collective-permute-start(bf16[64,768]{1,0:T(8,128)(2,1)S(1)} %get-tuple-element.6), channel_id=1, source_target_pairs={{0,28},{1,29},{2,30},{3,31},{4,0},{5,1},{6,2},{7,3},{8,4},{9,5},{1... | collective-permute-start | bytes 294920 | tf_op jit(solution)/shard_map/ppermute | solution.py:38
  134.5 22.2 %collective-permute-start.15 = (bf16[64,768]{1,0:T(8,128)(2,1)S(1)}, bf16[64,768]{1,0:T(8,128)(2,1)S(1)}, u32[]{:S(2)}, u32[]{:S(2)}) collective-permute-start(bf16[64,768]{1,0:T(8,128)(2,1)S(1)} %collective-permute-done.14), channel_id=1, source_target_pairs={{0,4},{1,5},{2,6},{3,7},{4,8},{5,9},{6,10},{7,11},{8,12},{9,13},{1... | collective-permute-start | bytes 294920 | tf_op jit(solution)/shard_map/ppermute | solution.py:38
  140.1 18.5 %collective-permute-start.12 = (bf16[64,768]{1,0:T(8,128)(2,1)S(1)}, bf16[64,768]{1,0:T(8,128)(2,1)S(1)}, u32[]{:S(2)}, u32[]{:S(2)}) collective-permute-start(bf16[64,768]{1,0:T(8,128)(2,1)S(1)} %collective-permute-done.11), channel_id=1, source_target_pairs={{0,28},{1,29},{2,30},{3,31},{4,0},{5,1},{6,2},{7,3},{8,4},{9,5},{1... | collective-permute-start | bytes 294920 | tf_op jit(solution)/shard_map/ppermute | solution.py:38
  156.7 13.3 %collective-permute-start.16 = (bf16[64,768]{1,0:T(8,128)(2,1)S(1)}, bf16[64,768]{1,0:T(8,128)(2,1)S(1)}, u32[]{:S(2)}, u32[]{:S(2)}) collective-permute-start(bf16[64,768]{1,0:T(8,128)(2,1)S(1)} %collective-permute-done.15), channel_id=1, source_target_pairs={{0,4},{1,5},{2,6},{3,7},{4,8},{5,9},{6,10},{7,11},{8,12},{9,13},{1... | collective-permute-start | bytes 294920 | tf_op jit(solution)/shard_map/ppermute | solution.py:38
  158.6 14.6 %collective-permute-start.13 = (bf16[64,768]{1,0:T(8,128)(2,1)S(1)}, bf16[64,768]{1,0:T(8,128)(2,1)S(1)}, u32[]{:S(2)}, u32[]{:S(2)}) collective-permute-start(bf16[64,768]{1,0:T(8,128)(2,1)S(1)} %collective-permute-done.12), channel_id=1, source_target_pairs={{0,28},{1,29},{2,30},{3,31},{4,0},{5,1},{6,2},{7,3},{8,4},{9,5},{1... | collective-permute-start | bytes 294920 | tf_op jit(solution)/shard_map/ppermute | solution.py:38
  170.0 11.3 %collective-permute-start.17 = (bf16[32,768]{1,0:T(8,128)(2,1)S(1)}, bf16[32,768]{1,0:T(8,128)(2,1)S(1)}, u32[]{:S(2)}, u32[]{:S(2)}) collective-permute-start(bf16[32,768]{1,0:T(8,128)(2,1)S(1)} %slice.119), channel_id=1, source_target_pairs={{0,4},{1,5},{2,6},{3,7},{4,8},{5,9},{6,10},{7,11},{8,12},{9,13},{1... | collective-permute-start | bytes 147464 | tf_op jit(solution)/shard_map/ppermute | solution.py:38
  173.2 8.8 %collective-permute-start.18 = (bf16[32,768]{1,0:T(8,128)(2,1)S(1)}, bf16[32,768]{1,0:T(8,128)(2,1)S(1)}, u32[]{:S(2)}, u32[]{:S(2)}) collective-permute-start(bf16[32,768]{1,0:T(8,128)(2,1)S(1)} %slice.120), channel_id=1, source_target_pairs={{0,28},{1,29},{2,30},{3,31},{4,0},{5,1},{6,2},{7,3},{8,4},{9,5},{1... | collective-permute-start | bytes 147464 | tf_op jit(solution)/shard_map/ppermute | solution.py:38
  183.4 29.5 %all-to-all-start.2 = ((f32[32,16,256]{2,1,0:T(8,128)}), f32[32,16,256]{2,1,0:T(8,128)S(1)}, u32[]{:S(2)}, u32[]{:S(2)}) async-start(f32[32,16,256]{2,1,0:T(8,128)} %bitcast.27), calls=%async_computation.2 | async-start | bytes 1048576 | tf_op jit(solution)/shard_map/all_to_all | solution.py:11
  (6 other events, 270.7 us)

commit v3 on v2

v3 whole, which is shorter than its diff:
```python
import jax
import jax.numpy as jnp
from jax import lax
from jax.sharding import PartitionSpec as P

F32 = jnp.float32
BF16 = jnp.bfloat16


def exchange(x, axis, groups=None):
    return lax.all_to_all(
        x, axis, split_axis=0, concat_axis=0, tiled=True, axis_index_groups=groups
    )


def picked(x, places):
    return [lax.dynamic_index_in_dim(x, i, 0, keepdims=False) for i in places]


def rows_dot(a, b):
    return lax.dot_general(a, b, (((1,), (1,)), ((), ())), preferred_element_type=F32)


def on_device(tokens, routing, gate_fixed, gate_weight, up_weight, down_weight):
    ep = lax.axis_size("ep")
    tp = lax.axis_size("tp")
    local, share, units = gate_weight.shape
    rows, top = routing.shape
    capacity = max(2, rows * top * 2 // (local * ep))
    ring = tp // local
    slots = ep * capacity
    chunk = slots // ring
    part_units = units // 2
    near = [[p * local + r for r in range(local)] for p in range(ring)]
    z = lax.axis_index("tp")
    me = lax.rem(z, local)
    here = lax.div(z, local)

    def sign_of(p, r):
        return 1 if (p % 2 == 0) == (r < local // 2) else -1

    sign = jnp.where((lax.rem(here, 2) == 0) == (me < local // 2), 1, -1)

    def swap(x, side):
        pairs = [
            (p * local + r, (p + side * sign_of(p, r)) % ring * local + r)
            for p in range(ring)
            for r in range(local)
        ]
        return lax.ppermute(x, "tp", pairs)

    def beside(x, k):
        return lax.ppermute(
            x, "tp", [(g[i], g[(i + k) % local]) for g in near for i in range(local)]
        )

    chunk_at = [lax.rem(here + k * sign + ring, ring) for k in range(ring)]
    chunk_of = [lax.rem((c - here) * sign + 2 * ring, ring) for c in range(ring)]

    xt = exchange(jnp.broadcast_to(tokens.T[None], (local, share, rows)), "tp", near)
    order = [lax.rem(me - k + local, local) for k in range(local)]
    xt = jnp.concatenate(picked(xt, order), axis=0)

    def in_block(k):
        e = lax.rem(me + k, local)
        g = lax.dynamic_index_in_dim(gate_weight, e, 0, keepdims=False)
        u = lax.dynamic_index_in_dim(up_weight, e, 0, keepdims=False)
        return jnp.concatenate(
            [g[:, :part_units], u[:, :part_units], g[:, part_units:], u[:, part_units:]],
            axis=1,
        )

    def down_block(k):
        return lax.dynamic_index_in_dim(
            down_weight, lax.rem(me + k, local), 0, keepdims=False
        )

    w_in = [in_block(0)] + [beside(in_block(k), k) for k in range(1, local)]

    rt = routing.T
    expert = jnp.arange(ep, dtype=jnp.int32) * local + me
    hit = rt[:, None, :] == expert[None, :, None]
    named = jnp.any(hit, axis=0)
    scale = jnp.sum(jnp.where(hit, gate_fixed.T[:, None, :], 0), axis=0)
    t = jnp.arange(rows)
    before = (t[:, None] < t[None, :]).astype(BF16)
    position = jnp.dot(named.astype(BF16), before, preferred_element_type=F32)
    slot = jnp.arange(capacity).astype(F32)[None, :, None]
    pick = named[:, None, :] & (position[:, None, :] == slot)
    place = pick.astype(BF16).reshape(slots, rows)
    factor = scale.astype(F32) / 65536.0
    mix = jnp.where(pick, factor[:, None, :], 0.0).reshape(slots, rows)

    outgoing = rows_dot(place, xt).astype(BF16)
    sent = [down_block(k) for k in range(1, local)]
    outgoing, sent = lax.optimization_barrier((outgoing, sent))
    x = exchange(outgoing.reshape(ep, capacity, -1), "ep")
    w_down = [down_block(0)] + [beside(b, k + 1) for k, b in enumerate(sent)]
    w_down = jnp.concatenate(w_down, axis=0)

    x = jnp.concatenate(picked(x.reshape(ring, chunk, -1), chunk_at), axis=0)
    width = 2 * part_units
    streams = []
    for h in range(2):
        w = jnp.concatenate([b[:, h * width : (h + 1) * width] for b in w_in], axis=0)
        streams.append(
            jnp.dot(x, w, preferred_element_type=F32).reshape(ring, chunk, width)
        )

    def both(a, b):
        return jnp.stack([a, b]).astype(BF16)

    def summed(part):
        r = swap(both(part[5], part[4]), -1).astype(F32)
        yield
        r = swap(both(part[2] + r[0], part[3] + r[1]), 1).astype(F32)
        yield
        r = swap(both(part[7] + r[0], part[6] + r[1]), -1).astype(F32)
        yield
        r0, r1 = part[0] + r[0], part[1] + r[1]
        acts = r0 + swap(r1.astype(BF16), 1).astype(F32)
        own = jax.nn.silu(acts[:, :part_units]) * acts[:, part_units:]
        yield own.astype(BF16)

    def shared(own):
        first = jnp.stack([own, swap(own, 1)])
        yield
        second = swap(first, -1)
        yield
        third = swap(second, 1)
        yield
        fourth = swap(third, -1)
        yield [first[0], first[1], third[0], third[1], fourth[1], fourth[0], second[1], second[0]]

    def run(steps):
        value = None
        while True:
            got = []
            for s in steps:
                got.append(next(s))
            if got[0] is not None:
                return got

    own = run([summed(p) for p in streams])
    blocks = run([shared(o) for o in own])
    result = rows_dot(jnp.concatenate(blocks[0], axis=0), w_down[:, :part_units]) + rows_dot(
        jnp.concatenate(blocks[1], axis=0), w_down[:, part_units:]
    )
    result = jnp.concatenate(picked(result.reshape(ring, chunk, -1), chunk_of), axis=0)
    back = exchange(result.reshape(ep, capacity, -1), "ep").reshape(slots, -1)

    mixed = lax.dot_general(
        back,
        mix,
        (((0,), (0,)), ((), ())),
        precision=lax.Precision.HIGHEST,
        preferred_element_type=F32,
    ).reshape(local, share, rows)
    parts = exchange(jnp.stack(picked(mixed, order)), "tp", near)
    return jnp.sum(parts, axis=0).astype(BF16).T


def solution(mesh):
    in_specs = (
        P("ep", "tp"),
        P("ep", None),
        P("ep", None),
        P("ep", "tp", None),
        P("ep", "tp", None),
        P("ep", "tp", None),
    )
    return jax.shard_map(
        on_device, mesh=mesh, in_specs=in_specs, out_specs=P("ep", "tp"), check_vma=False
    )
```

time: 239 us -> 278 us (1.16)
  waiting for transfers between devices: 54.5 us -> 109 us
  starting transfers between devices: 150 us -> 140 us
  blocking collectives: 23.5 us -> 13.7 us
  local copies, waits for them, and re-layouts: 4.18 us -> 7.79 us
    ppermute x16, waiting for transfers between devices: 34.5 us -> 89 us  [swap(): return lax.ppermute(x, 'tp', pairs)]
    all_to_all x3, starting transfers between devices: 40.1 us -> 27.5 us  [exchange(): lax.all_to_all(x, axis, split_axis=0, concat_axis=0, tiled=True, axis_ind...]
    ppermute x3 -> x6, starting transfers between devices: 9.55 us -> 21 us  [beside(): lax.ppermute(x, 'tp', [(g[i], g[(i + k) % local]) for g in near for i in...]
    all_to_all x1, blocking collectives: 23.5 us -> 13.7 us  [exchange(): lax.all_to_all(x, axis, split_axis=0, concat_axis=0, tiled=True, axis_ind...]
    ppermute x16, starting transfers between devices: 100 us -> 91.6 us  [swap(): return lax.ppermute(x, 'tp', pairs)]
    ppermute x3 -> x6, waiting for transfers between devices: 0.01 us -> 5.3 us  [beside(): lax.ppermute(x, 'tp', [(g[i], g[(i + k) % local]) for g in near for i in...]
    all_to_all x3, waiting for transfers between devices: 20 us -> 14.9 us  [exchange(): lax.all_to_all(x, axis, split_axis=0, concat_axis=0, tiled=True, axis_ind...]
    unnamed x17 -> x34, local copies, waits for them, and re-layouts: 0.08 us -> 4.7 us
  transfers between devices with their start and end apart: 22 -> 25, of which waited for: 12 -> 14; matrix products, arithmetic and copies ran while one was open for 2% -> 1% of each run, Pallas kernels for 0% -> 0%
where the time goes in v3:
time: 278 us; the launch traced here: 277 us
  starting transfers between devices  140 us (50%)
  waiting for transfers between devices  109 us (39%)
  blocking collectives  13.7 us (5%)
  local copies, waits for them, and re-layouts  7.79 us (3%)
  matrix products  3.05 us (1%)
    ppermute x16, starting transfers between devices, swap(): return lax.ppermute(x, 'tp', pairs)  91.6 us
    ppermute x16, waiting for transfers between devices, swap(): return lax.ppermute(x, 'tp', pairs)  89 us
    all_to_all x3, starting transfers between devices, exchange(): lax.all_to_all(x, axis, split_axis=0, concat_axis=0, tiled=True, axis_ind...  27.5 us
    ppermute x6, starting transfers between devices, beside(): lax.ppermute(x, 'tp', [(g[i], g[(i + k) % local]) for g in near for i in...  21 us
    all_to_all x3, waiting for transfers between devices, exchange(): lax.all_to_all(x, axis, split_axis=0, concat_axis=0, tiled=True, axis_ind...  14.9 us
    all_to_all x1, blocking collectives, exchange(): lax.all_to_all(x, axis, split_axis=0, concat_axis=0, tiled=True, axis_ind...  13.7 us
  transfers between devices with their start and end apart: 25, of which 14 were waited for; matrix products, arithmetic and copies ran while one was open for 1% of the time, Pallas kernels for 0%

profile of v3, /device:TPU:1, one launch (start us, length us, event | category | flops | bytes accessed | tf_op | source)
XLA Modules:
  0.0 276.8 jit_solution(11534213326587897345)
XLA Ops:
  1.4 4.5 %collective-permute-start = (bf16[64,1536]{1,0:T(8,128)(2,1)S(1)}, bf16[64,1536]{1,0:T(8,128)(2,1)S(1)}, u32[]{:S(2)}, u32[]{:S(2)}) collective-permute-start(bf16[64,1536]{1,0:T(8,128)(2,1)S(1)} %pad_maximum_fusion.1), channel_id=1, source_target_pairs={{0,1},{1,2},{2,3},{3,0},{4,5},{5,6},{6,7},{7,4},{8,9},{9,10},{10,1... | collective-permute-start | bytes 589832 | tf_op jit(solution)/shard_map/ppermute | solution.py:53
  5.9 4.9 %collective-permute-start.1 = (bf16[64,1536]{1,0:T(8,128)(2,1)S(1)}, bf16[64,1536]{1,0:T(8,128)(2,1)S(1)}, u32[]{:S(2)}, u32[]{:S(2)}) collective-permute-start(bf16[64,1536]{1,0:T(8,128)(2,1)S(1)} %pad_maximum_fusion.2), channel_id=1, source_target_pairs={{0,2},{1,3},{2,0},{3,1},{4,6},{5,7},{6,4},{7,5},{8,10},{9,11},{10,... | collective-permute-start | bytes 589832 | tf_op jit(solution)/shard_map/ppermute | solution.py:53
  18.5 3.6 %all-to-all-done = bf16[4,64,128]{2,1,0:T(8,128)(2,1)S(1)} async-done(((bf16[4,64,128]{2,1,0:T(8,128)(2,1)}), bf16[4,64,128]{2,1,0:T(8,128)(2,1)S(1)}, u32[]{:S(2)}, u32[]{:S(2)}) %all-to-all-start) | async-done | bytes 65568 | tf_op jit(solution)/shard_map/all_to_all | solution.py:11
  23.0 16.5 %all-to-all-start.1 = ((bf16[32,16,256]{2,1,0:T(8,128)(2,1)}), bf16[32,16,256]{2,1,0:T(8,128)(2,1)S(1)}, u32[]{:S(2)}, u32[]{:S(2)}) async-start(bf16[32,16,256]{2,1,0:T(8,128)(2,1)} %bitcast.11), calls=%async_computation.1 | async-start | bytes 524288 | tf_op jit(solution)/shard_map/all_to_all | solution.py:11
  44.1 4.4 %collective-permute-start.13 = (bf16[64,768]{1,0:T(8,128)(2,1)S(1)}, bf16[64,768]{1,0:T(8,128)(2,1)S(1)}, u32[]{:S(2)}, u32[]{:S(2)}) collective-permute-start(bf16[64,768]{1,0:T(8,128)(2,1)S(1)} %get-tuple-element.12), channel_id=1, source_target_pairs={{0,3},{1,0},{2,1},{3,2},{4,7},{5,4},{6,5},{7,6},{8,11},{9,8},{10,9... | collective-permute-start | bytes 294920 | tf_op jit(solution)/shard_map/ppermute | solution.py:53
  48.6 3.6 %collective-permute-done.12 = bf16[64,768]{1,0:T(8,128)(2,1)S(1)} collective-permute-done((bf16[64,768]{1,0:T(8,128)(2,1)S(1)}, bf16[64,768]{1,0:T(8,128)(2,1)S(1)}, u32[]{:S(2)}, u32[]{:S(2)}) %collective-permute-start.12) | collective-permute-done | bytes 98336 | tf_op jit(solution)/shard_map/ppermute | solution.py:53
  54.5 15.7 %collective-permute-start.3 = (bf16[2,64,768]{2,1,0:T(8,128)(2,1)S(1)}, bf16[2,64,768]{2,1,0:T(8,128)(2,1)S(1)}, u32[]{:S(2)}, u32[]{:S(2)}) collective-permute-start(bf16[2,64,768]{2,1,0:T(8,128)(2,1)S(1)} %pad_maximum_fusion.4), channel_id=1, source_target_pairs={{0,28},{1,29},{2,6},{3,7},{4,8},{5,9},{6,2},{7,3},{8,4},{9,5},{10,... | collective-permute-start | bytes 589832 | tf_op jit(solution)/shard_map/ppermute | solution.py:50
  72.5 19.1 %collective-permute-done.3 = bf16[2,64,768]{2,1,0:T(8,128)(2,1)S(1)} collective-permute-done((bf16[2,64,768]{2,1,0:T(8,128)(2,1)S(1)}, bf16[2,64,768]{2,1,0:T(8,128)(2,1)S(1)}, u32[]{:S(2)}, u32[]{:S(2)}) %collective-permute-start.3) | collective-permute-done | bytes 196640 | tf_op jit(solution)/shard_map/ppermute | solution.py:50
  96.0 5.1 %collective-permute-start.15 = (bf16[2,64,768]{2,1,0:T(8,128)(2,1)S(1)}, bf16[2,64,768]{2,1,0:T(8,128)(2,1)S(1)}, u32[]{:S(2)}, u32[]{:S(2)}) collective-permute-start(bf16[2,64,768]{2,1,0:T(8,128)(2,1)S(1)} %pad_maximum_fusion.8), channel_id=1, source_target_pairs={{0,4},{1,5},{2,30},{3,31},{4,0},{5,1},{6,10},{7,11},{8,12},{9,13},... | collective-permute-start | bytes 589832 | tf_op jit(solution)/shard_map/ppermute | solution.py:50
  101.1 19.9 %collective-permute-done.4 = bf16[2,64,768]{2,1,0:T(8,128)(2,1)S(1)} collective-permute-done((bf16[2,64,768]{2,1,0:T(8,128)(2,1)S(1)}, bf16[2,64,768]{2,1,0:T(8,128)(2,1)S(1)}, u32[]{:S(2)}, u32[]{:S(2)}) %collective-permute-start.4) | collective-permute-done | bytes 196640 | tf_op jit(solution)/shard_map/ppermute | solution.py:50
  121.1 12.6 %collective-permute-start.5 = (bf16[2,64,768]{2,1,0:T(8,128)(2,1)S(1)}, bf16[2,64,768]{2,1,0:T(8,128)(2,1)S(1)}, u32[]{:S(2)}, u32[]{:S(2)}) collective-permute-start(bf16[2,64,768]{2,1,0:T(8,128)(2,1)S(1)} %pad_maximum_fusion.6), channel_id=1, source_target_pairs={{0,28},{1,29},{2,6},{3,7},{4,8},{5,9},{6,2},{7,3},{8,4},{9,5},{10,... | collective-permute-start | bytes 589832 | tf_op jit(solution)/shard_map/ppermute | solution.py:50
  133.8 4.1 %collective-permute-start.16 = (bf16[2,64,768]{2,1,0:T(8,128)(2,1)S(1)}, bf16[2,64,768]{2,1,0:T(8,128)(2,1)S(1)}, u32[]{:S(2)}, u32[]{:S(2)}) collective-permute-start(bf16[2,64,768]{2,1,0:T(8,128)(2,1)S(1)} %pad_maximum_fusion.9), channel_id=1, source_target_pairs={{0,28},{1,29},{2,6},{3,7},{4,8},{5,9},{6,2},{7,3},{8,4},{9,5},{10,... | collective-permute-start | bytes 589832 | tf_op jit(solution)/shard_map/ppermute | solution.py:50
  140.0 24.0 %collective-permute-done.16 = bf16[2,64,768]{2,1,0:T(8,128)(2,1)S(1)} collective-permute-done((bf16[2,64,768]{2,1,0:T(8,128)(2,1)S(1)}, bf16[2,64,768]{2,1,0:T(8,128)(2,1)S(1)}, u32[]{:S(2)}, u32[]{:S(2)}) %collective-permute-start.16) | collective-permute-done | bytes 196640 | tf_op jit(solution)/shard_map/ppermute | solution.py:50
  166.1 7.3 %collective-permute-start.7 = (bf16[64,384]{1,0:T(8,128)(2,1)S(1)}, bf16[64,384]{1,0:T(8,128)(2,1)S(1)}, u32[]{:S(2)}, u32[]{:S(2)}) collective-permute-start(bf16[64,384]{1,0:T(8,128)(2,1)S(1)} %get-tuple-element.14), channel_id=1, source_target_pairs={{0,4},{1,5},{2,30},{3,31},{4,0},{5,1},{6,10},{7,11},{8,12},{9,13},... | collective-permute-start | bytes 147464 | tf_op jit(solution)/shard_map/ppermute | solution.py:50
  173.3 8.5 %collective-permute-done.17 = bf16[64,768]{1,0:T(8,128)(2,1)S(1)} collective-permute-done((bf16[64,768]{1,0:T(8,128)(2,1)S(1)}, bf16[64,768]{1,0:T(8,128)(2,1)S(1)}, u32[]{:S(2)}, u32[]{:S(2)}) %collective-permute-start.17) | collective-permute-done | bytes 98336 | tf_op jit(solution)/shard_map/ppermute | solution.py:50
  181.9 8.0 %collective-permute-start.18 = (bf16[64,384]{1,0:T(8,128)(2,1)S(1)}, bf16[64,384]{1,0:T(8,128)(2,1)S(1)}, u32[]{:S(2)}, u32[]{:S(2)}) collective-permute-start(bf16[64,384]{1,0:T(8,128)(2,1)S(1)} %get-tuple-element.16), channel_id=1, source_target_pairs={{0,4},{1,5},{2,30},{3,31},{4,0},{5,1},{6,10},{7,11},{8,12},{9,13},... | collective-permute-start | bytes 147464 | tf_op jit(solution)/shard_map/ppermute | solution.py:50
  193.4 6.8 %collective-permute-start.19 = (bf16[2,64,384]{2,1,0:T(8,128)(2,1)S(1)}, bf16[2,64,384]{2,1,0:T(8,128)(2,1)S(1)}, u32[]{:S(2)}, u32[]{:S(2)}) collective-permute-start(bf16[2,64,384]{2,1,0:T(8,128)(2,1)S(1)} %pad_maximum_fusion.12), channel_id=1, source_target_pairs={{0,28},{1,29},{2,6},{3,7},{4,8},{5,9},{6,2},{7,3},{8,4},{9,5},{10,... | collective-permute-start | bytes 294920 | tf_op jit(solution)/shard_map/ppermute | solution.py:50
  202.8 6.8 %collective-permute-done.19 = bf16[2,64,384]{2,1,0:T(8,128)(2,1)S(1)} collective-permute-done((bf16[2,64,384]{2,1,0:T(8,128)(2,1)S(1)}, bf16[2,64,384]{2,1,0:T(8,128)(2,1)S(1)}, u32[]{:S(2)}, u32[]{:S(2)}) %collective-permute-start.19) | collective-permute-done | bytes 98336 | tf_op jit(solution)/shard_map/ppermute | solution.py:50
  211.6 10.2 %collective-permute-start.10 = (bf16[2,64,384]{2,1,0:T(8,128)(2,1)S(1)}, bf16[2,64,384]{2,1,0:T(8,128)(2,1)S(1)}, u32[]{:S(2)}, u32[]{:S(2)}) collective-permute-start(bf16[2,64,384]{2,1,0:T(8,128)(2,1)S(1)} %collective-permute-done.9), channel_id=1, source_target_pairs={{0,28},{1,29},{2,6},{3,7},{4,8},{5,9},{6,2},{7,3},{8,4},{9,5},{10,... | collective-permute-start | bytes 294920 | tf_op jit(solution)/shard_map/ppermute | solution.py:50
  221.9 7.0 %collective-permute-start.21 = (bf16[2,64,384]{2,1,0:T(8,128)(2,1)S(1)}, bf16[2,64,384]{2,1,0:T(8,128)(2,1)S(1)}, u32[]{:S(2)}, u32[]{:S(2)}) collective-permute-start(bf16[2,64,384]{2,1,0:T(8,128)(2,1)S(1)} %collective-permute-done.20), channel_id=1, source_target_pairs={{0,28},{1,29},{2,6},{3,7},{4,8},{5,9},{6,2},{7,3},{8,4},{9,5},{10,... | collective-permute-start | bytes 294920 | tf_op jit(solution)/shard_map/ppermute | solution.py:50
  228.9 7.6 %collective-permute-done.21 = bf16[2,64,384]{2,1,0:T(8,128)(2,1)S(1)} collective-permute-done((bf16[2,64,384]{2,1,0:T(8,128)(2,1)S(1)}, bf16[2,64,384]{2,1,0:T(8,128)(2,1)S(1)}, u32[]{:S(2)}, u32[]{:S(2)}) %collective-permute-start.21) | collective-permute-done | bytes 98336 | tf_op jit(solution)/shard_map/ppermute | solution.py:50
  242.4 7.7 %all-to-all-start.2 = ((f32[32,16,256]{2,1,0:T(8,128)}), f32[32,16,256]{2,1,0:T(8,128)S(1)}, u32[]{:S(2)}, u32[]{:S(2)}) async-start(f32[32,16,256]{2,1,0:T(8,128)} %bitcast.71), calls=%async_computation.2 | async-start | bytes 1048576 | tf_op jit(solution)/shard_map/all_to_all | solution.py:11
  250.4 11.3 %all-to-all-done.2 = f32[32,16,256]{2,1,0:T(8,128)S(1)} async-done(((f32[32,16,256]{2,1,0:T(8,128)}), f32[32,16,256]{2,1,0:T(8,128)S(1)}, u32[]{:S(2)}, u32[]{:S(2)}) %all-to-all-start.2) | async-done | bytes 524320 | tf_op jit(solution)/shard_map/all_to_all | solution.py:11
  262.5 13.7 %all_to_all.20 = f32[4,64,128]{2,1,0:T(8,128)S(1)} all-to-all(f32[4,64,128]{2,1,0:T(8,128)S(1)} %pad_maximum_fusion.10), channel_id=1, replica_groups={{0,1,2,3},{4,5,6,7},{8,9,10,11},{12,13,14,15},{16,17,18,19},{20,21,22,2..., dimensions={0} | all-to-all | bytes 262144 | tf_op jit(solution)/shard_map/all_to_all | solution.py:11
  (130 shorter events, 42.9 us)
Async XLA Ops:
  1.4 17.1 %collective-permute-start = (bf16[64,1536]{1,0:T(8,128)(2,1)S(1)}, bf16[64,1536]{1,0:T(8,128)(2,1)S(1)}, u32[]{:S(2)}, u32[]{:S(2)}) collective-permute-start(bf16[64,1536]{1,0:T(8,128)(2,1)S(1)} %pad_maximum_fusion.1), channel_id=1, source_target_pairs={{0,1},{1,2},{2,3},{3,0},{4,5},{5,6},{6,7},{7,4},{8,9},{9,10},{10,1... | collective-permute-start | bytes 589832 | tf_op jit(solution)/shard_map/ppermute | solution.py:53
  5.9 12.5 %collective-permute-start.1 = (bf16[64,1536]{1,0:T(8,128)(2,1)S(1)}, bf16[64,1536]{1,0:T(8,128)(2,1)S(1)}, u32[]{:S(2)}, u32[]{:S(2)}) collective-permute-start(bf16[64,1536]{1,0:T(8,128)(2,1)S(1)} %pad_maximum_fusion.2), channel_id=1, source_target_pairs={{0,2},{1,3},{2,0},{3,1},{4,6},{5,7},{6,4},{7,5},{8,10},{9,11},{10,... | collective-permute-start | bytes 589832 | tf_op jit(solution)/shard_map/ppermute | solution.py:53
  10.9 37.6 %collective-permute-start.2 = (bf16[64,1536]{1,0:T(8,128)(2,1)S(1)}, bf16[64,1536]{1,0:T(8,128)(2,1)S(1)}, u32[]{:S(2)}, u32[]{:S(2)}) collective-permute-start(bf16[64,1536]{1,0:T(8,128)(2,1)S(1)} %pad_maximum_fusion.3), channel_id=1, source_target_pairs={{0,3},{1,0},{2,1},{3,2},{4,7},{5,4},{6,5},{7,6},{8,11},{9,8},{10,9... | collective-permute-start | bytes 589832 | tf_op jit(solution)/shard_map/ppermute | solution.py:53
  23.0 30.9 %all-to-all-start.1 = ((bf16[32,16,256]{2,1,0:T(8,128)(2,1)}), bf16[32,16,256]{2,1,0:T(8,128)(2,1)S(1)}, u32[]{:S(2)}, u32[]{:S(2)}) async-start(bf16[32,16,256]{2,1,0:T(8,128)(2,1)} %bitcast.11), calls=%async_computation.1 | async-start | bytes 524288 | tf_op jit(solution)/shard_map/all_to_all | solution.py:11
  39.5 9.1 %collective-permute-start.11 = (bf16[64,768]{1,0:T(8,128)(2,1)S(1)}, bf16[64,768]{1,0:T(8,128)(2,1)S(1)}, u32[]{:S(2)}, u32[]{:S(2)}) collective-permute-start(bf16[64,768]{1,0:T(8,128)(2,1)S(1)} %get-tuple-element.10), channel_id=1, source_target_pairs={{0,1},{1,2},{2,3},{3,0},{4,5},{5,6},{6,7},{7,4},{8,9},{9,10},{10,1... | collective-permute-start | bytes 294920 | tf_op jit(solution)/shard_map/ppermute | solution.py:53
  42.0 10.1 %collective-permute-start.12 = (bf16[64,768]{1,0:T(8,128)(2,1)S(1)}, bf16[64,768]{1,0:T(8,128)(2,1)S(1)}, u32[]{:S(2)}, u32[]{:S(2)}) collective-permute-start(bf16[64,768]{1,0:T(8,128)(2,1)S(1)} %get-tuple-element.11), channel_id=1, source_target_pairs={{0,2},{1,3},{2,0},{3,1},{4,6},{5,7},{6,4},{7,5},{8,10},{9,11},{10,... | collective-permute-start | bytes 294920 | tf_op jit(solution)/shard_map/ppermute | solution.py:53
  44.1 9.8 %collective-permute-start.13 = (bf16[64,768]{1,0:T(8,128)(2,1)S(1)}, bf16[64,768]{1,0:T(8,128)(2,1)S(1)}, u32[]{:S(2)}, u32[]{:S(2)}) collective-permute-start(bf16[64,768]{1,0:T(8,128)(2,1)S(1)} %get-tuple-element.12), channel_id=1, source_target_pairs={{0,3},{1,0},{2,1},{3,2},{4,7},{5,4},{6,5},{7,6},{8,11},{9,8},{10,9... | collective-permute-start | bytes 294920 | tf_op jit(solution)/shard_map/ppermute | solution.py:53
  54.5 37.2 %collective-permute-start.3 = (bf16[2,64,768]{2,1,0:T(8,128)(2,1)S(1)}, bf16[2,64,768]{2,1,0:T(8,128)(2,1)S(1)}, u32[]{:S(2)}, u32[]{:S(2)}) collective-permute-start(bf16[2,64,768]{2,1,0:T(8,128)(2,1)S(1)} %pad_maximum_fusion.4), channel_id=1, source_target_pairs={{0,28},{1,29},{2,6},{3,7},{4,8},{5,9},{6,2},{7,3},{8,4},{9,5},{10,... | collective-permute-start | bytes 589832 | tf_op jit(solution)/shard_map/ppermute | solution.py:50
  70.6 25.3 %collective-permute-start.14 = (bf16[2,64,768]{2,1,0:T(8,128)(2,1)S(1)}, bf16[2,64,768]{2,1,0:T(8,128)(2,1)S(1)}, u32[]{:S(2)}, u32[]{:S(2)}) collective-permute-start(bf16[2,64,768]{2,1,0:T(8,128)(2,1)S(1)} %pad_maximum_fusion.7), channel_id=1, source_target_pairs={{0,28},{1,29},{2,6},{3,7},{4,8},{5,9},{6,2},{7,3},{8,4},{9,5},{10,... | collective-permute-start | bytes 589832 | tf_op jit(solution)/shard_map/ppermute | solution.py:50
  91.8 29.2 %collective-permute-start.4 = (bf16[2,64,768]{2,1,0:T(8,128)(2,1)S(1)}, bf16[2,64,768]{2,1,0:T(8,128)(2,1)S(1)}, u32[]{:S(2)}, u32[]{:S(2)}) collective-permute-start(bf16[2,64,768]{2,1,0:T(8,128)(2,1)S(1)} %pad_maximum_fusion.5), channel_id=1, source_target_pairs={{0,4},{1,5},{2,30},{3,31},{4,0},{5,1},{6,10},{7,11},{8,12},{9,13},... | collective-permute-start | bytes 589832 | tf_op jit(solution)/shard_map/ppermute | solution.py:50
  96.0 37.7 %collective-permute-start.15 = (bf16[2,64,768]{2,1,0:T(8,128)(2,1)S(1)}, bf16[2,64,768]{2,1,0:T(8,128)(2,1)S(1)}, u32[]{:S(2)}, u32[]{:S(2)}) collective-permute-start(bf16[2,64,768]{2,1,0:T(8,128)(2,1)S(1)} %pad_maximum_fusion.8), channel_id=1, source_target_pairs={{0,4},{1,5},{2,30},{3,31},{4,0},{5,1},{6,10},{7,11},{8,12},{9,13},... | collective-permute-start | bytes 589832 | tf_op jit(solution)/shard_map/ppermute | solution.py:50
  121.1 16.8 %collective-permute-start.5 = (bf16[2,64,768]{2,1,0:T(8,128)(2,1)S(1)}, bf16[2,64,768]{2,1,0:T(8,128)(2,1)S(1)}, u32[]{:S(2)}, u32[]{:S(2)}) collective-permute-start(bf16[2,64,768]{2,1,0:T(8,128)(2,1)S(1)} %pad_maximum_fusion.6), channel_id=1, source_target_pairs={{0,28},{1,29},{2,6},{3,7},{4,8},{5,9},{6,2},{7,3},{8,4},{9,5},{10,... | collective-permute-start | bytes 589832 | tf_op jit(solution)/shard_map/ppermute | solution.py:50
  133.8 30.2 %collective-permute-start.16 = (bf16[2,64,768]{2,1,0:T(8,128)(2,1)S(1)}, bf16[2,64,768]{2,1,0:T(8,128)(2,1)S(1)}, u32[]{:S(2)}, u32[]{:S(2)}) collective-permute-start(bf16[2,64,768]{2,1,0:T(8,128)(2,1)S(1)} %pad_maximum_fusion.9), channel_id=1, source_target_pairs={{0,28},{1,29},{2,6},{3,7},{4,8},{5,9},{6,2},{7,3},{8,4},{9,5},{10,... | collective-permute-start | bytes 589832 | tf_op jit(solution)/shard_map/ppermute | solution.py:50
  138.0 28.0 %collective-permute-start.6 = (bf16[64,768]{1,0:T(8,128)(2,1)S(1)}, bf16[64,768]{1,0:T(8,128)(2,1)S(1)}, u32[]{:S(2)}, u32[]{:S(2)}) collective-permute-start(bf16[64,768]{1,0:T(8,128)(2,1)S(1)} %fusion.33), channel_id=1, source_target_pairs={{0,4},{1,5},{2,30},{3,31},{4,0},{5,1},{6,10},{7,11},{8,12},{9,13},... | collective-permute-start | bytes 294920 | tf_op jit(solution)/shard_map/ppermute | solution.py:50
  164.0 17.8 %collective-permute-start.17 = (bf16[64,768]{1,0:T(8,128)(2,1)S(1)}, bf16[64,768]{1,0:T(8,128)(2,1)S(1)}, u32[]{:S(2)}, u32[]{:S(2)}) collective-permute-start(bf16[64,768]{1,0:T(8,128)(2,1)S(1)} %fusion.24), channel_id=1, source_target_pairs={{0,4},{1,5},{2,30},{3,31},{4,0},{5,1},{6,10},{7,11},{8,12},{9,13},... | collective-permute-start | bytes 294920 | tf_op jit(solution)/shard_map/ppermute | solution.py:50
  166.1 23.9 %collective-permute-start.7 = (bf16[64,384]{1,0:T(8,128)(2,1)S(1)}, bf16[64,384]{1,0:T(8,128)(2,1)S(1)}, u32[]{:S(2)}, u32[]{:S(2)}) collective-permute-start(bf16[64,384]{1,0:T(8,128)(2,1)S(1)} %get-tuple-element.14), channel_id=1, source_target_pairs={{0,4},{1,5},{2,30},{3,31},{4,0},{5,1},{6,10},{7,11},{8,12},{9,13},... | collective-permute-start | bytes 147464 | tf_op jit(solution)/shard_map/ppermute | solution.py:50
  181.9 11.4 %collective-permute-start.18 = (bf16[64,384]{1,0:T(8,128)(2,1)S(1)}, bf16[64,384]{1,0:T(8,128)(2,1)S(1)}, u32[]{:S(2)}, u32[]{:S(2)}) collective-permute-start(bf16[64,384]{1,0:T(8,128)(2,1)S(1)} %get-tuple-element.16), channel_id=1, source_target_pairs={{0,4},{1,5},{2,30},{3,31},{4,0},{5,1},{6,10},{7,11},{8,12},{9,13},... | collective-permute-start | bytes 147464 | tf_op jit(solution)/shard_map/ppermute | solution.py:50
  190.0 10.9 %collective-permute-start.8 = (bf16[2,64,384]{2,1,0:T(8,128)(2,1)S(1)}, bf16[2,64,384]{2,1,0:T(8,128)(2,1)S(1)}, u32[]{:S(2)}, u32[]{:S(2)}) collective-permute-start(bf16[2,64,384]{2,1,0:T(8,128)(2,1)S(1)} %pad_maximum_fusion.11), channel_id=1, source_target_pairs={{0,28},{1,29},{2,6},{3,7},{4,8},{5,9},{6,2},{7,3},{8,4},{9,5},{10,... | collective-permute-start | bytes 294920 | tf_op jit(solution)/shard_map/ppermute | solution.py:50
  193.4 16.2 %collective-permute-start.19 = (bf16[2,64,384]{2,1,0:T(8,128)(2,1)S(1)}, bf16[2,64,384]{2,1,0:T(8,128)(2,1)S(1)}, u32[]{:S(2)}, u32[]{:S(2)}) collective-permute-start(bf16[2,64,384]{2,1,0:T(8,128)(2,1)S(1)} %pad_maximum_fusion.12), channel_id=1, source_target_pairs={{0,28},{1,29},{2,6},{3,7},{4,8},{5,9},{6,2},{7,3},{8,4},{9,5},{10,... | collective-permute-start | bytes 294920 | tf_op jit(solution)/shard_map/ppermute | solution.py:50
  200.9 10.7 %collective-permute-start.9 = (bf16[2,64,384]{2,1,0:T(8,128)(2,1)S(1)}, bf16[2,64,384]{2,1,0:T(8,128)(2,1)S(1)}, u32[]{:S(2)}, u32[]{:S(2)}) collective-permute-start(bf16[2,64,384]{2,1,0:T(8,128)(2,1)S(1)} %collective-permute-done.8), channel_id=1, source_target_pairs={{0,4},{1,5},{2,30},{3,31},{4,0},{5,1},{6,10},{7,11},{8,12},{9,13},... | collective-permute-start | bytes 294920 | tf_op jit(solution)/shard_map/ppermute | solution.py:50
  209.6 12.3 %collective-permute-start.20 = (bf16[2,64,384]{2,1,0:T(8,128)(2,1)S(1)}, bf16[2,64,384]{2,1,0:T(8,128)(2,1)S(1)}, u32[]{:S(2)}, u32[]{:S(2)}) collective-permute-start(bf16[2,64,384]{2,1,0:T(8,128)(2,1)S(1)} %collective-permute-done.19), channel_id=1, source_target_pairs={{0,4},{1,5},{2,30},{3,31},{4,0},{5,1},{6,10},{7,11},{8,12},{9,13},... | collective-permute-start | bytes 294920 | tf_op jit(solution)/shard_map/ppermute | solution.py:50
  211.6 25.4 %collective-permute-start.10 = (bf16[2,64,384]{2,1,0:T(8,128)(2,1)S(1)}, bf16[2,64,384]{2,1,0:T(8,128)(2,1)S(1)}, u32[]{:S(2)}, u32[]{:S(2)}) collective-permute-start(bf16[2,64,384]{2,1,0:T(8,128)(2,1)S(1)} %collective-permute-done.9), channel_id=1, source_target_pairs={{0,28},{1,29},{2,6},{3,7},{4,8},{5,9},{6,2},{7,3},{8,4},{9,5},{10,... | collective-permute-start | bytes 294920 | tf_op jit(solution)/shard_map/ppermute | solution.py:50
  221.9 14.7 %collective-permute-start.21 = (bf16[2,64,384]{2,1,0:T(8,128)(2,1)S(1)}, bf16[2,64,384]{2,1,0:T(8,128)(2,1)S(1)}, u32[]{:S(2)}, u32[]{:S(2)}) collective-permute-start(bf16[2,64,384]{2,1,0:T(8,128)(2,1)S(1)} %collective-permute-done.20), channel_id=1, source_target_pairs={{0,28},{1,29},{2,6},{3,7},{4,8},{5,9},{6,2},{7,3},{8,4},{9,5},{10,... | collective-permute-start | bytes 294920 | tf_op jit(solution)/shard_map/ppermute | solution.py:50
  242.4 19.3 %all-to-all-start.2 = ((f32[32,16,256]{2,1,0:T(8,128)}), f32[32,16,256]{2,1,0:T(8,128)S(1)}, u32[]{:S(2)}, u32[]{:S(2)}) async-start(f32[32,16,256]{2,1,0:T(8,128)} %bitcast.71), calls=%async_computation.2 | async-start | bytes 1048576 | tf_op jit(solution)/shard_map/all_to_all | solution.py:11
  (5 other events, 66.2 us)

commit v4 on v3

v4 whole, which is shorter than its diff:
```python
import jax
import jax.numpy as jnp
from jax import lax
from jax.sharding import PartitionSpec as P

F32 = jnp.float32
BF16 = jnp.bfloat16


def exchange(x, axis, groups=None):
    return lax.all_to_all(
        x, axis, split_axis=0, concat_axis=0, tiled=True, axis_index_groups=groups
    )


def picked(x, places):
    return [lax.dynamic_index_in_dim(x, i, 0, keepdims=False) for i in places]


def rows_dot(a, b):
    return lax.dot_general(a, b, (((1,), (1,)), ((), ())), preferred_element_type=F32)


def layer(tokens, routing, gate_fixed, gate_weight, up_weight, down_weight):
    ep = lax.axis_size("ep")
    tp = lax.axis_size("tp")
    local, share, units = gate_weight.shape
    rows, top = routing.shape
    capacity = max(2, rows * top * 2 // (local * ep))
    ring = tp // local
    slots = ep * capacity
    chunk = slots // ring
    near = [[p * local + r for r in range(local)] for p in range(ring)]
    z = lax.axis_index("tp")
    me = lax.rem(z, local)
    here = lax.div(z, local)

    def sign_of(r):
        return 1 if r < local // 2 else -1

    sign = jnp.where(me < local // 2, 1, -1)

    def ship(x, side):
        pairs = [
            (p * local + r, (p + side * sign_of(r)) % ring * local + r)
            for p in range(ring)
            for r in range(local)
        ]
        return lax.ppermute(x, "tp", pairs)

    def beside(x, k):
        return lax.ppermute(
            x, "tp", [(g[i], g[(i + k) % local]) for g in near for i in range(local)]
        )

    chunk_at = [lax.rem(here + k * sign + ring, ring) for k in range(ring)]

    xt = exchange(jnp.broadcast_to(tokens.T[None], (local, share, rows)), "tp", near)
    order = [lax.rem(me - k + local, local) for k in range(local)]
    xt = jnp.concatenate(picked(xt, order), axis=0)

    def in_block(k):
        e = lax.rem(me + k, local)
        g = lax.dynamic_index_in_dim(gate_weight, e, 0, keepdims=False)
        u = lax.dynamic_index_in_dim(up_weight, e, 0, keepdims=False)
        return jnp.concatenate([g, u], axis=1)

    def down_block(k):
        return lax.dynamic_index_in_dim(
            down_weight, lax.rem(me + k, local), 0, keepdims=False
        )

    w_in = [in_block(0)] + [beside(in_block(k), k) for k in range(1, local)]

    rt = routing.T
    expert = jnp.arange(ep, dtype=jnp.int32) * local + me
    hit = rt[:, None, :] == expert[None, :, None]
    named = jnp.any(hit, axis=0)
    scale = jnp.sum(jnp.where(hit, gate_fixed.T[:, None, :], 0), axis=0)
    t = jnp.arange(rows)
    before = (t[:, None] < t[None, :]).astype(BF16)
    position = jnp.dot(named.astype(BF16), before, preferred_element_type=F32)
    slot = jnp.arange(capacity).astype(F32)[None, :, None]
    pick = named[:, None, :] & (position[:, None, :] == slot)
    place = pick.astype(BF16).reshape(slots, rows)
    factor = scale.astype(F32) / 65536.0
    mix = jnp.where(pick, factor[:, None, :], 0.0).reshape(slots, rows)

    outgoing = rows_dot(place, xt).astype(BF16)
    sent = [down_block(k) for k in range(1, local)]
    outgoing, sent = lax.optimization_barrier((outgoing, sent))
    x = exchange(outgoing.reshape(ep, capacity, -1), "ep")
    w_down = [down_block(0)] + [beside(b, k + 1) for k, b in enumerate(sent)]
    w_down = jnp.concatenate(w_down, axis=0)

    x = x.reshape(ring, chunk, -1)
    w_in = jnp.concatenate(w_in, axis=0)

    def term(k):
        rows_of = lax.dynamic_index_in_dim(x, chunk_at[k % ring], 0, keepdims=False)
        return jnp.dot(rows_of, w_in, preferred_element_type=F32)

    steps = ring // 2
    ahead = ship(term(steps).astype(BF16), 1)
    behind = ship(term(1 - steps).astype(BF16), -1)
    for k in range(steps - 1, 0, -1):
        ahead = ship((term(k) + ahead.astype(F32)).astype(BF16), 1)
        if k > 1:
            behind = ship((term(1 - k) + behind.astype(F32)).astype(BF16), -1)
    acts = term(0) + ahead.astype(F32) + behind.astype(F32)
    own = (jax.nn.silu(acts[:, :units]) * acts[:, units:]).astype(BF16)

    result = jnp.zeros((ring, chunk, local * share), F32)

    def put(result, hidden, k):
        return lax.dynamic_update_index_in_dim(
            result, rows_dot(hidden, w_down), chunk_at[k % ring], 0
        )

    ahead = behind = own
    result = put(result, own, 0)
    for k in range(1, steps + 1):
        ahead = ship(ahead, 1)
        result = put(result, ahead, -k)
        if k < steps:
            behind = ship(behind, -1)
            result = put(result, behind, k)
    back = exchange(result.reshape(ep, capacity, -1), "ep").reshape(slots, -1)

    mixed = lax.dot_general(
        back,
        mix,
        (((0,), (0,)), ((), ())),
        precision=lax.Precision.HIGHEST,
        preferred_element_type=F32,
    ).reshape(local, share, rows)
    parts = exchange(jnp.stack(picked(mixed, order)), "tp", near)
    return jnp.sum(parts, axis=0).astype(BF16).T


def solution(mesh):
    in_specs = (
        P("ep", "tp"),
        P("ep", None),
        P("ep", None),
        P("ep", "tp", None),
        P("ep", "tp", None),
        P("ep", "tp", None),
    )
    return jax.shard_map(
        layer, mesh=mesh, in_specs=in_specs, out_specs=P("ep", "tp"), check_vma=False
    )
```

time: 278 us -> 218 us (0.78)
  waiting for transfers between devices: 109 us -> 37.6 us
  starting transfers between devices: 140 us -> 155 us
  matrix products: 3.05 us -> 10.9 us
  blocking collectives: 13.7 us -> 7.43 us
  local copies, waits for them, and re-layouts: 7.79 us -> 3.84 us
    ppermute x16 -> x14, waiting for transfers between devices: 89 us -> 17.5 us  [ship(): return lax.ppermute(x, 'tp', pairs)]
    all_to_all x3, starting transfers between devices: 27.5 us -> 41.4 us  [exchange(): lax.all_to_all(x, axis, split_axis=0, concat_axis=0, tiled=True, axis_ind...]
    ppermute x6, starting transfers between devices: 21 us -> 32.4 us  [beside(): lax.ppermute(x, 'tp', [(g[i], g[(i + k) % local]) for g in near for i in...]
    ppermute x16 -> x14, starting transfers between devices: 91.6 us -> 81.4 us  [ship(): return lax.ppermute(x, 'tp', pairs)]
    dot_general x3 -> x9, matrix products: 1.59 us -> 8.15 us  [rows_dot(): lax.dot_general(a, b, (((1,), (1,)), ((), ())), preferred_element_type=F32)]
    all_to_all x1, blocking collectives: 13.7 us -> 7.43 us  [exchange(): lax.all_to_all(x, axis, split_axis=0, concat_axis=0, tiled=True, axis_ind...]
    ppermute x6, waiting for transfers between devices: 5.3 us -> 0.02 us  [beside(): lax.ppermute(x, 'tp', [(g[i], g[(i + k) % local]) for g in near for i in...]
    all_to_all x3, waiting for transfers between devices: 14.9 us -> 20.1 us  [exchange(): lax.all_to_all(x, axis, split_axis=0, concat_axis=0, tiled=True, axis_ind...]
  transfers between devices with their start and end apart: 25 -> 23, of which waited for: 14 -> 7; matrix products, arithmetic and copies ran while one was open for 1% -> 6% of each run, Pallas kernels for 0% -> 0%
where the time goes in v4:
time: 218 us; the launch traced here: 217 us
  starting transfers between devices  155 us (71%)
  waiting for transfers between devices  37.6 us (17%)
  matrix products  10.9 us (5%)
  blocking collectives  7.43 us (3%)
  local copies, waits for them, and re-layouts  3.84 us (2%)
    ppermute x14, starting transfers between devices, ship(): return lax.ppermute(x, 'tp', pairs)  81.4 us
    all_to_all x3, starting transfers between devices, exchange(): lax.all_to_all(x, axis, split_axis=0, concat_axis=0, tiled=True, axis_ind...  41.4 us
    ppermute x6, starting transfers between devices, beside(): lax.ppermute(x, 'tp', [(g[i], g[(i + k) % local]) for g in near for i in...  32.4 us
    all_to_all x3, waiting for transfers between devices, exchange(): lax.all_to_all(x, axis, split_axis=0, concat_axis=0, tiled=True, axis_ind...  20.1 us
    ppermute x14, waiting for transfers between devices, ship(): return lax.ppermute(x, 'tp', pairs)  17.5 us
    dot_general x9, matrix products, rows_dot(): lax.dot_general(a, b, (((1,), (1,)), ((), ())), preferred_element_type=F32)  8.15 us
    all_to_all x1, blocking collectives, exchange(): lax.all_to_all(x, axis, split_axis=0, concat_axis=0, tiled=True, axis_ind...  7.43 us
  transfers between devices with their start and end apart: 23, of which 7 were waited for; matrix products, arithmetic and copies ran while one was open for 6% of the time, Pallas kernels for 0%

profile of v4, /device:TPU:1, one launch (start us, length us, event | category | flops | bytes accessed | tf_op | source)
XLA Modules:
  0.0 216.8 jit_solution(10089450491016724603)
XLA Ops:
  1.3 6.4 %all-to-all-start = ((bf16[4,64,128]{2,1,0:T(8,128)(2,1)}), bf16[4,64,128]{2,1,0:T(8,128)(2,1)S(1)}, u32[]{:S(2)}, u32[]{:S(2)}) async-start(bf16[4,64,128]{2,1,0:T(8,128)(2,1)} %broadcast_in_dim.68), calls=%async_computation | async-start | bytes 131072 | tf_op jit(solution)/shard_map/all_to_all | solution.py:11
  9.1 3.5 %collective-permute-start = (bf16[64,1536]{1,0:T(8,128)(2,1)S(1)}, bf16[64,1536]{1,0:T(8,128)(2,1)S(1)}, u32[]{:S(2)}, u32[]{:S(2)}) collective-permute-start(bf16[64,1536]{1,0:T(8,128)(2,1)S(1)} %pad_maximum_fusion.2), channel_id=1, source_target_pairs={{0,1},{1,2},{2,3},{3,0},{4,5},{5,6},{6,7},{7,4},{8,9},{9,10},{10,1... | collective-permute-start | bytes 589832 | tf_op jit(solution)/shard_map/ppermute | solution.py:52
  12.6 4.0 %collective-permute-start.1 = (bf16[64,1536]{1,0:T(8,128)(2,1)S(1)}, bf16[64,1536]{1,0:T(8,128)(2,1)S(1)}, u32[]{:S(2)}, u32[]{:S(2)}) collective-permute-start(bf16[64,1536]{1,0:T(8,128)(2,1)S(1)} %pad_maximum_fusion.3), channel_id=1, source_target_pairs={{0,2},{1,3},{2,0},{3,1},{4,6},{5,7},{6,4},{7,5},{8,10},{9,11},{10,... | collective-permute-start | bytes 589832 | tf_op jit(solution)/shard_map/ppermute | solution.py:52
  16.7 3.1 %collective-permute-start.2 = (bf16[64,1536]{1,0:T(8,128)(2,1)S(1)}, bf16[64,1536]{1,0:T(8,128)(2,1)S(1)}, u32[]{:S(2)}, u32[]{:S(2)}) collective-permute-start(bf16[64,1536]{1,0:T(8,128)(2,1)S(1)} %pad_maximum_fusion.4), channel_id=1, source_target_pairs={{0,3},{1,0},{2,1},{3,2},{4,7},{5,4},{6,5},{7,6},{8,11},{9,8},{10,9... | collective-permute-start | bytes 589832 | tf_op jit(solution)/shard_map/ppermute | solution.py:52
  21.3 15.6 %all-to-all-start.1 = ((bf16[32,16,256]{2,1,0:T(8,128)(2,1)}), bf16[32,16,256]{2,1,0:T(8,128)(2,1)S(1)}, u32[]{:S(2)}, u32[]{:S(2)}) async-start(bf16[32,16,256]{2,1,0:T(8,128)(2,1)} %bitcast.11), calls=%async_computation.1 | async-start | bytes 524288 | tf_op jit(solution)/shard_map/all_to_all | solution.py:11
  37.1 8.8 %all-to-all-done.1 = bf16[32,16,256]{2,1,0:T(8,128)(2,1)S(1)} async-done(((bf16[32,16,256]{2,1,0:T(8,128)(2,1)}), bf16[32,16,256]{2,1,0:T(8,128)(2,1)S(1)}, u32[]{:S(2)}, u32[]{:S(2)}) %all-to-all-start.1) | async-done | bytes 262176 | tf_op jit(solution)/shard_map/all_to_all | solution.py:11
  48.7 10.2 %collective-permute-start.7 = (bf16[64,1536]{1,0:T(8,128)(2,1)S(1)}, bf16[64,1536]{1,0:T(8,128)(2,1)S(1)}, u32[]{:S(2)}, u32[]{:S(2)}) collective-permute-start(bf16[64,1536]{1,0:T(8,128)(2,1)S(1)} %convolution_convert_fusion), channel_id=1, source_target_pairs={{0,28},{1,29},{2,6},{3,7},{4,0},{5,1},{6,10},{7,11},{8,4},{9,5},{1... | collective-permute-start | bytes 589832 | tf_op jit(solution)/shard_map/ppermute | solution.py:49
  62.1 11.2 %collective-permute-start.4 = (bf16[64,1536]{1,0:T(8,128)(2,1)S(1)}, bf16[64,1536]{1,0:T(8,128)(2,1)S(1)}, u32[]{:S(2)}, u32[]{:S(2)}) collective-permute-start(bf16[64,1536]{1,0:T(8,128)(2,1)S(1)} %fusion.3), channel_id=1, source_target_pairs={{0,4},{1,5},{2,30},{3,31},{4,8},{5,9},{6,2},{7,3},{8,12},{9,13},{1... | collective-permute-start | bytes 589832 | tf_op jit(solution)/shard_map/ppermute | solution.py:49
  73.7 4.9 %collective-permute-start.8 = (bf16[64,1536]{1,0:T(8,128)(2,1)S(1)}, bf16[64,1536]{1,0:T(8,128)(2,1)S(1)}, u32[]{:S(2)}, u32[]{:S(2)}) collective-permute-start(bf16[64,1536]{1,0:T(8,128)(2,1)S(1)} %fusion.5), channel_id=1, source_target_pairs={{0,28},{1,29},{2,6},{3,7},{4,0},{5,1},{6,10},{7,11},{8,4},{9,5},{1... | collective-permute-start | bytes 589832 | tf_op jit(solution)/shard_map/ppermute | solution.py:49
  78.6 4.7 %collective-permute-done.4 = bf16[64,1536]{1,0:T(8,128)(2,1)S(1)} collective-permute-done((bf16[64,1536]{1,0:T(8,128)(2,1)S(1)}, bf16[64,1536]{1,0:T(8,128)(2,1)S(1)}, u32[]{:S(2)}, u32[]{:S(2)}) %collective-permute-start.4) | collective-permute-done | bytes 196640 | tf_op jit(solution)/shard_map/ppermute | solution.py:49
  83.6 16.5 %collective-permute-start.5 = (bf16[64,1536]{1,0:T(8,128)(2,1)S(1)}, bf16[64,1536]{1,0:T(8,128)(2,1)S(1)}, u32[]{:S(2)}, u32[]{:S(2)}) collective-permute-start(bf16[64,1536]{1,0:T(8,128)(2,1)S(1)} %fusion.2), channel_id=1, source_target_pairs={{0,4},{1,5},{2,30},{3,31},{4,8},{5,9},{6,2},{7,3},{8,12},{9,13},{1... | collective-permute-start | bytes 589832 | tf_op jit(solution)/shard_map/ppermute | solution.py:49
  100.3 3.2 %collective-permute-start.9 = (bf16[64,1536]{1,0:T(8,128)(2,1)S(1)}, bf16[64,1536]{1,0:T(8,128)(2,1)S(1)}, u32[]{:S(2)}, u32[]{:S(2)}) collective-permute-start(bf16[64,1536]{1,0:T(8,128)(2,1)S(1)} %fusion.4), channel_id=1, source_target_pairs={{0,28},{1,29},{2,6},{3,7},{4,0},{5,1},{6,10},{7,11},{8,4},{9,5},{1... | collective-permute-start | bytes 589832 | tf_op jit(solution)/shard_map/ppermute | solution.py:49
  103.5 4.2 %collective-permute-done.5 = bf16[64,1536]{1,0:T(8,128)(2,1)S(1)} collective-permute-done((bf16[64,1536]{1,0:T(8,128)(2,1)S(1)}, bf16[64,1536]{1,0:T(8,128)(2,1)S(1)}, u32[]{:S(2)}, u32[]{:S(2)}) %collective-permute-start.5) | collective-permute-done | bytes 196640 | tf_op jit(solution)/shard_map/ppermute | solution.py:49
  108.0 3.5 %collective-permute-start.6 = (bf16[64,1536]{1,0:T(8,128)(2,1)S(1)}, bf16[64,1536]{1,0:T(8,128)(2,1)S(1)}, u32[]{:S(2)}, u32[]{:S(2)}) collective-permute-start(bf16[64,1536]{1,0:T(8,128)(2,1)S(1)} %fusion.1), channel_id=1, source_target_pairs={{0,4},{1,5},{2,30},{3,31},{4,8},{5,9},{6,2},{7,3},{8,12},{9,13},{1... | collective-permute-start | bytes 589832 | tf_op jit(solution)/shard_map/ppermute | solution.py:49
  113.4 15.7 %collective-permute-start.11 = (bf16[64,768]{1,0:T(8,128)(2,1)S(1)}, bf16[64,768]{1,0:T(8,128)(2,1)S(1)}, u32[]{:S(2)}, u32[]{:S(2)}) collective-permute-start(bf16[64,768]{1,0:T(8,128)(2,1)S(1)} %get-tuple-element.11), channel_id=1, source_target_pairs={{0,2},{1,3},{2,0},{3,1},{4,6},{5,7},{6,4},{7,5},{8,10},{9,11},{10,... | collective-permute-start | bytes 294920 | tf_op jit(solution)/shard_map/ppermute | solution.py:52
  129.1 4.3 %collective-permute-start.12 = (bf16[64,768]{1,0:T(8,128)(2,1)S(1)}, bf16[64,768]{1,0:T(8,128)(2,1)S(1)}, u32[]{:S(2)}, u32[]{:S(2)}) collective-permute-start(bf16[64,768]{1,0:T(8,128)(2,1)S(1)} %get-tuple-element.12), channel_id=1, source_target_pairs={{0,3},{1,0},{2,1},{3,2},{4,7},{5,4},{6,5},{7,6},{8,11},{9,8},{10,9... | collective-permute-start | bytes 294920 | tf_op jit(solution)/shard_map/ppermute | solution.py:52
  135.6 7.3 %collective-permute-start.14 = (bf16[64,768]{1,0:T(8,128)(2,1)S(1)}, bf16[64,768]{1,0:T(8,128)(2,1)S(1)}, u32[]{:S(2)}, u32[]{:S(2)}) collective-permute-start(bf16[64,768]{1,0:T(8,128)(2,1)S(1)} %fusion.15), channel_id=1, source_target_pairs={{0,28},{1,29},{2,6},{3,7},{4,0},{5,1},{6,10},{7,11},{8,4},{9,5},{1... | collective-permute-start | bytes 294920 | tf_op jit(solution)/shard_map/ppermute | solution.py:49
  147.5 7.3 %collective-permute-start.16 = (bf16[64,768]{1,0:T(8,128)(2,1)S(1)}, bf16[64,768]{1,0:T(8,128)(2,1)S(1)}, u32[]{:S(2)}, u32[]{:S(2)}) collective-permute-start(bf16[64,768]{1,0:T(8,128)(2,1)S(1)} %collective-permute-done.14), channel_id=1, source_target_pairs={{0,28},{1,29},{2,6},{3,7},{4,0},{5,1},{6,10},{7,11},{8,4},{9,5},{1... | collective-permute-start | bytes 294920 | tf_op jit(solution)/shard_map/ppermute | solution.py:49
  159.8 6.0 %collective-permute-start.18 = (bf16[64,768]{1,0:T(8,128)(2,1)S(1)}, bf16[64,768]{1,0:T(8,128)(2,1)S(1)}, u32[]{:S(2)}, u32[]{:S(2)}) collective-permute-start(bf16[64,768]{1,0:T(8,128)(2,1)S(1)} %collective-permute-done.16), channel_id=1, source_target_pairs={{0,28},{1,29},{2,6},{3,7},{4,0},{5,1},{6,10},{7,11},{8,4},{9,5},{1... | collective-permute-start | bytes 294920 | tf_op jit(solution)/shard_map/ppermute | solution.py:49
  166.7 3.2 %collective-permute-start.19 = (bf16[64,768]{1,0:T(8,128)(2,1)S(1)}, bf16[64,768]{1,0:T(8,128)(2,1)S(1)}, u32[]{:S(2)}, u32[]{:S(2)}) collective-permute-start(bf16[64,768]{1,0:T(8,128)(2,1)S(1)} %collective-permute-done.17), channel_id=1, source_target_pairs={{0,4},{1,5},{2,30},{3,31},{4,8},{5,9},{6,2},{7,3},{8,12},{9,13},{1... | collective-permute-start | bytes 294920 | tf_op jit(solution)/shard_map/ppermute | solution.py:49
  171.7 4.4 %collective-permute-done.19 = bf16[64,768]{1,0:T(8,128)(2,1)S(1)} collective-permute-done((bf16[64,768]{1,0:T(8,128)(2,1)S(1)}, bf16[64,768]{1,0:T(8,128)(2,1)S(1)}, u32[]{:S(2)}, u32[]{:S(2)}) %collective-permute-start.19) | collective-permute-done | bytes 98336 | tf_op jit(solution)/shard_map/ppermute | solution.py:49
  177.0 19.4 %all-to-all-start.2 = ((f32[32,16,256]{2,1,0:T(8,128)}), f32[32,16,256]{2,1,0:T(8,128)S(1)}, u32[]{:S(2)}, u32[]{:S(2)}) async-start(f32[32,16,256]{2,1,0:T(8,128)} %bitcast.38), calls=%async_computation.2 | async-start | bytes 1048576 | tf_op jit(solution)/shard_map/all_to_all | solution.py:11
  196.6 11.3 %all-to-all-done.2 = f32[32,16,256]{2,1,0:T(8,128)S(1)} async-done(((f32[32,16,256]{2,1,0:T(8,128)}), f32[32,16,256]{2,1,0:T(8,128)S(1)}, u32[]{:S(2)}, u32[]{:S(2)}) %all-to-all-start.2) | async-done | bytes 524320 | tf_op jit(solution)/shard_map/all_to_all | solution.py:11
  208.7 7.4 %all_to_all.20 = f32[4,64,128]{2,1,0:T(8,128)S(1)} all-to-all(f32[4,64,128]{2,1,0:T(8,128)S(1)} %pad_maximum_fusion.5), channel_id=1, replica_groups={{0,1,2,3},{4,5,6,7},{8,9,10,11},{12,13,14,15},{16,17,18,19},{20,21,22,2..., dimensions={0} | all-to-all | bytes 262144 | tf_op jit(solution)/shard_map/all_to_all | solution.py:11
  (71 shorter events, 30.2 us)
Async XLA Ops:
  1.3 19.0 %all-to-all-start = ((bf16[4,64,128]{2,1,0:T(8,128)(2,1)}), bf16[4,64,128]{2,1,0:T(8,128)(2,1)S(1)}, u32[]{:S(2)}, u32[]{:S(2)}) async-start(bf16[4,64,128]{2,1,0:T(8,128)(2,1)} %broadcast_in_dim.68), calls=%async_computation | async-start | bytes 131072 | tf_op jit(solution)/shard_map/all_to_all | solution.py:11
  9.1 27.9 %collective-permute-start = (bf16[64,1536]{1,0:T(8,128)(2,1)S(1)}, bf16[64,1536]{1,0:T(8,128)(2,1)S(1)}, u32[]{:S(2)}, u32[]{:S(2)}) collective-permute-start(bf16[64,1536]{1,0:T(8,128)(2,1)S(1)} %pad_maximum_fusion.2), channel_id=1, source_target_pairs={{0,1},{1,2},{2,3},{3,0},{4,5},{5,6},{6,7},{7,4},{8,9},{9,10},{10,1... | collective-permute-start | bytes 589832 | tf_op jit(solution)/shard_map/ppermute | solution.py:52
  12.6 24.4 %collective-permute-start.1 = (bf16[64,1536]{1,0:T(8,128)(2,1)S(1)}, bf16[64,1536]{1,0:T(8,128)(2,1)S(1)}, u32[]{:S(2)}, u32[]{:S(2)}) collective-permute-start(bf16[64,1536]{1,0:T(8,128)(2,1)S(1)} %pad_maximum_fusion.3), channel_id=1, source_target_pairs={{0,2},{1,3},{2,0},{3,1},{4,6},{5,7},{6,4},{7,5},{8,10},{9,11},{10,... | collective-permute-start | bytes 589832 | tf_op jit(solution)/shard_map/ppermute | solution.py:52
  16.7 20.4 %collective-permute-start.2 = (bf16[64,1536]{1,0:T(8,128)(2,1)S(1)}, bf16[64,1536]{1,0:T(8,128)(2,1)S(1)}, u32[]{:S(2)}, u32[]{:S(2)}) collective-permute-start(bf16[64,1536]{1,0:T(8,128)(2,1)S(1)} %pad_maximum_fusion.4), channel_id=1, source_target_pairs={{0,3},{1,0},{2,1},{3,2},{4,7},{5,4},{6,5},{7,6},{8,11},{9,8},{10,9... | collective-permute-start | bytes 589832 | tf_op jit(solution)/shard_map/ppermute | solution.py:52
  21.3 24.6 %all-to-all-start.1 = ((bf16[32,16,256]{2,1,0:T(8,128)(2,1)}), bf16[32,16,256]{2,1,0:T(8,128)(2,1)S(1)}, u32[]{:S(2)}, u32[]{:S(2)}) async-start(bf16[32,16,256]{2,1,0:T(8,128)(2,1)} %bitcast.11), calls=%async_computation.1 | async-start | bytes 524288 | tf_op jit(solution)/shard_map/all_to_all | solution.py:11
  46.2 15.7 %collective-permute-start.3 = (bf16[64,1536]{1,0:T(8,128)(2,1)S(1)}, bf16[64,1536]{1,0:T(8,128)(2,1)S(1)}, u32[]{:S(2)}, u32[]{:S(2)}) collective-permute-start(bf16[64,1536]{1,0:T(8,128)(2,1)S(1)} %convolution_convert_fusion.1), channel_id=1, source_target_pairs={{0,4},{1,5},{2,30},{3,31},{4,8},{5,9},{6,2},{7,3},{8,12},{9,13},{1... | collective-permute-start | bytes 589832 | tf_op jit(solution)/shard_map/ppermute | solution.py:49
  48.7 24.7 %collective-permute-start.7 = (bf16[64,1536]{1,0:T(8,128)(2,1)S(1)}, bf16[64,1536]{1,0:T(8,128)(2,1)S(1)}, u32[]{:S(2)}, u32[]{:S(2)}) collective-permute-start(bf16[64,1536]{1,0:T(8,128)(2,1)S(1)} %convolution_convert_fusion), channel_id=1, source_target_pairs={{0,28},{1,29},{2,6},{3,7},{4,0},{5,1},{6,10},{7,11},{8,4},{9,5},{1... | collective-permute-start | bytes 589832 | tf_op jit(solution)/shard_map/ppermute | solution.py:49
  62.1 21.1 %collective-permute-start.4 = (bf16[64,1536]{1,0:T(8,128)(2,1)S(1)}, bf16[64,1536]{1,0:T(8,128)(2,1)S(1)}, u32[]{:S(2)}, u32[]{:S(2)}) collective-permute-start(bf16[64,1536]{1,0:T(8,128)(2,1)S(1)} %fusion.3), channel_id=1, source_target_pairs={{0,4},{1,5},{2,30},{3,31},{4,8},{5,9},{6,2},{7,3},{8,12},{9,13},{1... | collective-permute-start | bytes 589832 | tf_op jit(solution)/shard_map/ppermute | solution.py:49
  73.7 26.4 %collective-permute-start.8 = (bf16[64,1536]{1,0:T(8,128)(2,1)S(1)}, bf16[64,1536]{1,0:T(8,128)(2,1)S(1)}, u32[]{:S(2)}, u32[]{:S(2)}) collective-permute-start(bf16[64,1536]{1,0:T(8,128)(2,1)S(1)} %fusion.5), channel_id=1, source_target_pairs={{0,28},{1,29},{2,6},{3,7},{4,0},{5,1},{6,10},{7,11},{8,4},{9,5},{1... | collective-permute-start | bytes 589832 | tf_op jit(solution)/shard_map/ppermute | solution.py:49
  83.6 24.2 %collective-permute-start.5 = (bf16[64,1536]{1,0:T(8,128)(2,1)S(1)}, bf16[64,1536]{1,0:T(8,128)(2,1)S(1)}, u32[]{:S(2)}, u32[]{:S(2)}) collective-permute-start(bf16[64,1536]{1,0:T(8,128)(2,1)S(1)} %fusion.2), channel_id=1, source_target_pairs={{0,4},{1,5},{2,30},{3,31},{4,8},{5,9},{6,2},{7,3},{8,12},{9,13},{1... | collective-permute-start | bytes 589832 | tf_op jit(solution)/shard_map/ppermute | solution.py:49
  100.3 33.0 %collective-permute-start.9 = (bf16[64,1536]{1,0:T(8,128)(2,1)S(1)}, bf16[64,1536]{1,0:T(8,128)(2,1)S(1)}, u32[]{:S(2)}, u32[]{:S(2)}) collective-permute-start(bf16[64,1536]{1,0:T(8,128)(2,1)S(1)} %fusion.4), channel_id=1, source_target_pairs={{0,28},{1,29},{2,6},{3,7},{4,0},{5,1},{6,10},{7,11},{8,4},{9,5},{1... | collective-permute-start | bytes 589832 | tf_op jit(solution)/shard_map/ppermute | solution.py:49
  108.0 25.4 %collective-permute-start.6 = (bf16[64,1536]{1,0:T(8,128)(2,1)S(1)}, bf16[64,1536]{1,0:T(8,128)(2,1)S(1)}, u32[]{:S(2)}, u32[]{:S(2)}) collective-permute-start(bf16[64,1536]{1,0:T(8,128)(2,1)S(1)} %fusion.1), channel_id=1, source_target_pairs={{0,4},{1,5},{2,30},{3,31},{4,8},{5,9},{6,2},{7,3},{8,12},{9,13},{1... | collective-permute-start | bytes 589832 | tf_op jit(solution)/shard_map/ppermute | solution.py:49
  111.5 31.4 %collective-permute-start.10 = (bf16[64,768]{1,0:T(8,128)(2,1)S(1)}, bf16[64,768]{1,0:T(8,128)(2,1)S(1)}, u32[]{:S(2)}, u32[]{:S(2)}) collective-permute-start(bf16[64,768]{1,0:T(8,128)(2,1)S(1)} %get-tuple-element.10), channel_id=1, source_target_pairs={{0,1},{1,2},{2,3},{3,0},{4,5},{5,6},{6,7},{7,4},{8,9},{9,10},{10,1... | collective-permute-start | bytes 294920 | tf_op jit(solution)/shard_map/ppermute | solution.py:52
  113.4 29.5 %collective-permute-start.11 = (bf16[64,768]{1,0:T(8,128)(2,1)S(1)}, bf16[64,768]{1,0:T(8,128)(2,1)S(1)}, u32[]{:S(2)}, u32[]{:S(2)}) collective-permute-start(bf16[64,768]{1,0:T(8,128)(2,1)S(1)} %get-tuple-element.11), channel_id=1, source_target_pairs={{0,2},{1,3},{2,0},{3,1},{4,6},{5,7},{6,4},{7,5},{8,10},{9,11},{10,... | collective-permute-start | bytes 294920 | tf_op jit(solution)/shard_map/ppermute | solution.py:52
  129.1 13.9 %collective-permute-start.12 = (bf16[64,768]{1,0:T(8,128)(2,1)S(1)}, bf16[64,768]{1,0:T(8,128)(2,1)S(1)}, u32[]{:S(2)}, u32[]{:S(2)}) collective-permute-start(bf16[64,768]{1,0:T(8,128)(2,1)S(1)} %get-tuple-element.12), channel_id=1, source_target_pairs={{0,3},{1,0},{2,1},{3,2},{4,7},{5,4},{6,5},{7,6},{8,11},{9,8},{10,9... | collective-permute-start | bytes 294920 | tf_op jit(solution)/shard_map/ppermute | solution.py:52
  133.7 11.0 %collective-permute-start.13 = (bf16[64,768]{1,0:T(8,128)(2,1)S(1)}, bf16[64,768]{1,0:T(8,128)(2,1)S(1)}, u32[]{:S(2)}, u32[]{:S(2)}) collective-permute-start(bf16[64,768]{1,0:T(8,128)(2,1)S(1)} %fusion.15), channel_id=1, source_target_pairs={{0,4},{1,5},{2,30},{3,31},{4,8},{5,9},{6,2},{7,3},{8,12},{9,13},{1... | collective-permute-start | bytes 294920 | tf_op jit(solution)/shard_map/ppermute | solution.py:49
  135.6 11.9 %collective-permute-start.14 = (bf16[64,768]{1,0:T(8,128)(2,1)S(1)}, bf16[64,768]{1,0:T(8,128)(2,1)S(1)}, u32[]{:S(2)}, u32[]{:S(2)}) collective-permute-start(bf16[64,768]{1,0:T(8,128)(2,1)S(1)} %fusion.15), channel_id=1, source_target_pairs={{0,28},{1,29},{2,6},{3,7},{4,0},{5,1},{6,10},{7,11},{8,4},{9,5},{1... | collective-permute-start | bytes 294920 | tf_op jit(solution)/shard_map/ppermute | solution.py:49
  144.7 11.0 %collective-permute-start.15 = (bf16[64,768]{1,0:T(8,128)(2,1)S(1)}, bf16[64,768]{1,0:T(8,128)(2,1)S(1)}, u32[]{:S(2)}, u32[]{:S(2)}) collective-permute-start(bf16[64,768]{1,0:T(8,128)(2,1)S(1)} %collective-permute-done.13), channel_id=1, source_target_pairs={{0,4},{1,5},{2,30},{3,31},{4,8},{5,9},{6,2},{7,3},{8,12},{9,13},{1... | collective-permute-start | bytes 294920 | tf_op jit(solution)/shard_map/ppermute | solution.py:49
  147.5 12.3 %collective-permute-start.16 = (bf16[64,768]{1,0:T(8,128)(2,1)S(1)}, bf16[64,768]{1,0:T(8,128)(2,1)S(1)}, u32[]{:S(2)}, u32[]{:S(2)}) collective-permute-start(bf16[64,768]{1,0:T(8,128)(2,1)S(1)} %collective-permute-done.14), channel_id=1, source_target_pairs={{0,28},{1,29},{2,6},{3,7},{4,0},{5,1},{6,10},{7,11},{8,4},{9,5},{1... | collective-permute-start | bytes 294920 | tf_op jit(solution)/shard_map/ppermute | solution.py:49
  155.7 11.0 %collective-permute-start.17 = (bf16[64,768]{1,0:T(8,128)(2,1)S(1)}, bf16[64,768]{1,0:T(8,128)(2,1)S(1)}, u32[]{:S(2)}, u32[]{:S(2)}) collective-permute-start(bf16[64,768]{1,0:T(8,128)(2,1)S(1)} %collective-permute-done.15), channel_id=1, source_target_pairs={{0,4},{1,5},{2,30},{3,31},{4,8},{5,9},{6,2},{7,3},{8,12},{9,13},{1... | collective-permute-start | bytes 294920 | tf_op jit(solution)/shard_map/ppermute | solution.py:49
  159.8 11.0 %collective-permute-start.18 = (bf16[64,768]{1,0:T(8,128)(2,1)S(1)}, bf16[64,768]{1,0:T(8,128)(2,1)S(1)}, u32[]{:S(2)}, u32[]{:S(2)}) collective-permute-start(bf16[64,768]{1,0:T(8,128)(2,1)S(1)} %collective-permute-done.16), channel_id=1, source_target_pairs={{0,28},{1,29},{2,6},{3,7},{4,0},{5,1},{6,10},{7,11},{8,4},{9,5},{1... | collective-permute-start | bytes 294920 | tf_op jit(solution)/shard_map/ppermute | solution.py:49
  166.7 9.4 %collective-permute-start.19 = (bf16[64,768]{1,0:T(8,128)(2,1)S(1)}, bf16[64,768]{1,0:T(8,128)(2,1)S(1)}, u32[]{:S(2)}, u32[]{:S(2)}) collective-permute-start(bf16[64,768]{1,0:T(8,128)(2,1)S(1)} %collective-permute-done.17), channel_id=1, source_target_pairs={{0,4},{1,5},{2,30},{3,31},{4,8},{5,9},{6,2},{7,3},{8,12},{9,13},{1... | collective-permute-start | bytes 294920 | tf_op jit(solution)/shard_map/ppermute | solution.py:49
  177.0 19.4 %copy-start.2 = (s32[128,8]{0,1:T(8,128)S(1)}, s32[128,8]{0,1:T(8,128)}, u32[]{:S(2)}) copy-start(s32[128,8]{0,1:T(8,128)} %param.8) | copy-start | bytes 12292
  177.0 30.9 %all-to-all-start.2 = ((f32[32,16,256]{2,1,0:T(8,128)}), f32[32,16,256]{2,1,0:T(8,128)S(1)}, u32[]{:S(2)}, u32[]{:S(2)}) async-start(f32[32,16,256]{2,1,0:T(8,128)} %bitcast.38), calls=%async_computation.2 | async-start | bytes 1048576 | tf_op jit(solution)/shard_map/all_to_all | solution.py:11
  (2 other events, 21.9 us)

commit v5 on v4

--- a/solution.py
+++ b/solution.py
@@ -76,22 +76,18 @@
     expert = jnp.arange(ep, dtype=jnp.int32) * local + me
     hit = rt[:, None, :] == expert[None, :, None]
     named = jnp.any(hit, axis=0)
-    scale = jnp.sum(jnp.where(hit, gate_fixed.T[:, None, :], 0), axis=0)
     t = jnp.arange(rows)
     before = (t[:, None] < t[None, :]).astype(BF16)
     position = jnp.dot(named.astype(BF16), before, preferred_element_type=F32)
     slot = jnp.arange(capacity).astype(F32)[None, :, None]
     pick = named[:, None, :] & (position[:, None, :] == slot)
     place = pick.astype(BF16).reshape(slots, rows)
-    factor = scale.astype(F32) / 65536.0
-    mix = jnp.where(pick, factor[:, None, :], 0.0).reshape(slots, rows)
-
     outgoing = rows_dot(place, xt).astype(BF16)
     sent = [down_block(k) for k in range(1, local)]
     outgoing, sent = lax.optimization_barrier((outgoing, sent))
     x = exchange(outgoing.reshape(ep, capacity, -1), "ep")
     w_down = [down_block(0)] + [beside(b, k + 1) for k, b in enumerate(sent)]
-    w_down = jnp.concatenate(w_down, axis=0)
+    w_down = jnp.stack(picked(jnp.stack(w_down), order))
 
     x = x.reshape(ring, chunk, -1)
     w_in = jnp.concatenate(w_in, axis=0)
@@ -110,12 +106,21 @@
     acts = term(0) + ahead.astype(F32) + behind.astype(F32)
     own = (jax.nn.silu(acts[:, :units]) * acts[:, units:]).astype(BF16)
 
-    result = jnp.zeros((ring, chunk, local * share), F32)
+    low = capacity // 2
+    empty = jnp.zeros_like(w_down)
+    w_down = jnp.stack(
+        [jnp.concatenate([w_down, empty], axis=2), jnp.concatenate([empty, w_down], axis=2)],
+        axis=1,
+    ).reshape(local * 2 * share, 2 * units)
+    sources = chunk // capacity
+    result = jnp.zeros((ring, sources, local, low, 2 * share), F32)
 
     def put(result, hidden, k):
-        return lax.dynamic_update_index_in_dim(
-            result, rows_dot(hidden, w_down), chunk_at[k % ring], 0
-        )
+        pair = hidden.reshape(sources, 2, low, units)
+        pair = jnp.concatenate([pair[:, 0], pair[:, 1]], axis=2)
+        tile = rows_dot(pair.reshape(sources * low, 2 * units), w_down)
+        tile = tile.reshape(sources, low, local, 2 * share).transpose(0, 2, 1, 3)
+        return lax.dynamic_update_index_in_dim(result, tile, chunk_at[k % ring], 0)
 
     ahead = behind = own
     result = put(result, own, 0)
@@ -125,17 +130,42 @@
         if k < steps:
             behind = ship(behind, -1)
             result = put(result, behind, k)
-    back = exchange(result.reshape(ep, capacity, -1), "ep").reshape(slots, -1)
 
+    groups = [
+        [e * tp + p * local + r for e in range(ep) for r in range(local)] for p in range(ring)
+    ]
+    back = lax.all_to_all(
+        result.reshape(ep * local, low, 2 * share),
+        ("ep", "tp"),
+        split_axis=0,
+        concat_axis=0,
+        tiled=True,
+        axis_index_groups=groups,
+    )
+
+    each = jnp.arange(ep * local, dtype=jnp.int32)
+    hit = rt[:, None, :] == each[None, :, None]
+    named = jnp.any(hit, axis=0)
+    scale = jnp.sum(jnp.where(hit, gate_fixed.T[:, None, :], 0), axis=0)
+    position = jnp.dot(named.astype(BF16), before, preferred_element_type=F32)
+    position = jnp.where(named, position, -1.0)[:, None, :]
+    factor = (scale.astype(F32) / 65536.0)[:, None, :]
+    slot = jnp.arange(low).astype(F32)[None, :, None]
+    mix = jnp.concatenate(
+        [
+            jnp.where(position == slot, factor, 0.0),
+            jnp.where(position == slot + low, factor, 0.0),
+        ],
+        axis=2,
+    ).reshape(ep * local * low, 2 * rows)
     mixed = lax.dot_general(
-        back,
+        back.reshape(ep * local * low, 2 * share),
         mix,
         (((0,), (0,)), ((), ())),
         precision=lax.Precision.HIGHEST,
         preferred_element_type=F32,
-    ).reshape(local, share, rows)
-    parts = exchange(jnp.stack(picked(mixed, order)), "tp", near)
-    return jnp.sum(parts, axis=0).astype(BF16).T
+    )
+    return (mixed[:share, :rows] + mixed[share:, rows:]).astype(BF16).T
 
 
 def solution(mesh):

time: 218 us -> 253 us (1.16)
  waiting for transfers between devices: 37.6 us -> 81.9 us
  blocking collectives: 7.43 us -> 0 us
  starting transfers between devices: 155 us -> 151 us
  matrix products: 10.9 us -> 13.7 us
    ppermute x14, waiting for transfers between devices: 17.5 us -> 51.1 us  [ship(): return lax.ppermute(x, 'tp', pairs)]
    all_to_all x3 -> x2, starting transfers between devices: 41.4 us -> 20.7 us  [exchange(): lax.all_to_all(x, axis, split_axis=0, concat_axis=0, tiled=True, axis_ind...]
    all_to_all x0 -> x1, starting transfers between devices: none -> 19.2 us  [layer(): lax.all_to_all(result.reshape(ep * local, low, 2 * share), ('ep', 'tp'),...]
    all_to_all x0 -> x1, waiting for transfers between devices: none -> 18.3 us  [layer(): lax.all_to_all(result.reshape(ep * local, low, 2 * share), ('ep', 'tp'),...]
    ppermute x6, starting transfers between devices: 32.4 us -> 20.9 us  [beside(): lax.ppermute(x, 'tp', [(g[i], g[(i + k) % local]) for g in near for i in...]
    ppermute x14, starting transfers between devices: 81.4 us -> 90.6 us  [ship(): return lax.ppermute(x, 'tp', pairs)]
    all_to_all x3 -> x2, waiting for transfers between devices: 20.1 us -> 12.5 us  [exchange(): lax.all_to_all(x, axis, split_axis=0, concat_axis=0, tiled=True, axis_ind...]
    all_to_all x1 -> x0, blocking collectives: 7.43 us -> none  [exchange(): lax.all_to_all(x, axis, split_axis=0, concat_axis=0, tiled=True, axis_ind...]
  transfers between devices with their start and end apart: 23 -> 23, of which waited for: 7 -> 12; matrix products, arithmetic and copies ran while one was open for 6% -> 4% of each run, Pallas kernels for 0% -> 0%
where the time goes in v5:
time: 253 us
  starting transfers between devices  151 us (60%)
  waiting for transfers between devices  81.9 us (32%)
  matrix products  13.7 us (5%)
  local copies, waits for them, and re-layouts  3.25 us (1%)
    ppermute x14, starting transfers between devices, ship(): return lax.ppermute(x, 'tp', pairs)  90.6 us
    ppermute x14, waiting for transfers between devices, ship(): return lax.ppermute(x, 'tp', pairs)  51.1 us
    ppermute x6, starting transfers between devices, beside(): lax.ppermute(x, 'tp', [(g[i], g[(i + k) % local]) for g in near for i in...  20.9 us
    all_to_all x2, starting transfers between devices, exchange(): lax.all_to_all(x, axis, split_axis=0, concat_axis=0, tiled=True, axis_ind...  20.7 us
    all_to_all x1, starting transfers between devices, layer(): lax.all_to_all(result.reshape(ep * local, low, 2 * share), ('ep', 'tp'),...  19.2 us
    all_to_all x1, waiting for transfers between devices, layer(): lax.all_to_all(result.reshape(ep * local, low, 2 * share), ('ep', 'tp'),...  18.3 us
    all_to_all x2, waiting for transfers between devices, exchange(): lax.all_to_all(x, axis, split_axis=0, concat_axis=0, tiled=True, axis_ind...  12.5 us
    dot_general x9, matrix products, rows_dot(): lax.dot_general(a, b, (((1,), (1,)), ((), ())), preferred_element_type=F32)  10.4 us
  transfers between devices with their start and end apart: 23, of which 12 were waited for; matrix products, arithmetic and copies ran while one was open for 4% of the time, Pallas kernels for 0%

profile of v5, /device:TPU:1, one launch (start us, length us, event | category | flops | bytes accessed | tf_op | source)
XLA Modules:
  0.0 252.5 jit_solution(16876503686298215225)
XLA Ops:
  1.4 4.4 %collective-permute-start = (bf16[64,1536]{1,0:T(8,128)(2,1)S(1)}, bf16[64,1536]{1,0:T(8,128)(2,1)S(1)}, u32[]{:S(2)}, u32[]{:S(2)}) collective-permute-start(bf16[64,1536]{1,0:T(8,128)(2,1)S(1)} %pad_maximum_fusion.4), channel_id=1, source_target_pairs={{0,1},{1,2},{2,3},{3,0},{4,5},{5,6},{6,7},{7,4},{8,9},{9,10},{10,1... | collective-permute-start | bytes 589832 | tf_op jit(solution)/shard_map/ppermute | solution.py:52
  5.8 4.9 %collective-permute-start.1 = (bf16[64,1536]{1,0:T(8,128)(2,1)S(1)}, bf16[64,1536]{1,0:T(8,128)(2,1)S(1)}, u32[]{:S(2)}, u32[]{:S(2)}) collective-permute-start(bf16[64,1536]{1,0:T(8,128)(2,1)S(1)} %pad_maximum_fusion.5), channel_id=1, source_target_pairs={{0,2},{1,3},{2,0},{3,1},{4,6},{5,7},{6,4},{7,5},{8,10},{9,11},{10,... | collective-permute-start | bytes 589832 | tf_op jit(solution)/shard_map/ppermute | solution.py:52
  27.7 4.1 %collective-permute-start.12 = (bf16[64,768]{1,0:T(8,128)(2,1)S(1)}, bf16[64,768]{1,0:T(8,128)(2,1)S(1)}, u32[]{:S(2)}, u32[]{:S(2)}) collective-permute-start(bf16[64,768]{1,0:T(8,128)(2,1)S(1)} %get-tuple-element.12), channel_id=1, source_target_pairs={{0,3},{1,0},{2,1},{3,2},{4,7},{5,4},{6,5},{7,6},{8,11},{9,8},{10,9... | collective-permute-start | bytes 294920 | tf_op jit(solution)/shard_map/ppermute | solution.py:52
  31.9 17.4 %all-to-all-start.1 = ((bf16[32,16,256]{2,1,0:T(8,128)(2,1)}), bf16[32,16,256]{2,1,0:T(8,128)(2,1)S(1)}, u32[]{:S(2)}, u32[]{:S(2)}) async-start(bf16[32,16,256]{2,1,0:T(8,128)(2,1)} %bitcast.11), calls=%async_computation.1 | async-start | bytes 524288 | tf_op jit(solution)/shard_map/all_to_all | solution.py:11
  49.6 8.7 %all-to-all-done.1 = bf16[32,16,256]{2,1,0:T(8,128)(2,1)S(1)} async-done(((bf16[32,16,256]{2,1,0:T(8,128)(2,1)}), bf16[32,16,256]{2,1,0:T(8,128)(2,1)S(1)}, u32[]{:S(2)}, u32[]{:S(2)}) %all-to-all-start.1) | async-done | bytes 262176 | tf_op jit(solution)/shard_map/all_to_all | solution.py:11
  58.5 5.5 %collective-permute-start.3 = (bf16[64,1536]{1,0:T(8,128)(2,1)S(1)}, bf16[64,1536]{1,0:T(8,128)(2,1)S(1)}, u32[]{:S(2)}, u32[]{:S(2)}) collective-permute-start(bf16[64,1536]{1,0:T(8,128)(2,1)S(1)} %convolution_convert_fusion.1), channel_id=1, source_target_pairs={{0,4},{1,5},{2,30},{3,31},{4,8},{5,9},{6,2},{7,3},{8,12},{9,13},{1... | collective-permute-start | bytes 589832 | tf_op jit(solution)/shard_map/ppermute | solution.py:49
  64.3 11.7 %collective-permute-start.7 = (bf16[64,1536]{1,0:T(8,128)(2,1)S(1)}, bf16[64,1536]{1,0:T(8,128)(2,1)S(1)}, u32[]{:S(2)}, u32[]{:S(2)}) collective-permute-start(bf16[64,1536]{1,0:T(8,128)(2,1)S(1)} %convolution_convert_fusion), channel_id=1, source_target_pairs={{0,28},{1,29},{2,6},{3,7},{4,0},{5,1},{6,10},{7,11},{8,4},{9,5},{1... | collective-permute-start | bytes 589832 | tf_op jit(solution)/shard_map/ppermute | solution.py:49
  85.2 7.3 %collective-permute-start.8 = (bf16[64,1536]{1,0:T(8,128)(2,1)S(1)}, bf16[64,1536]{1,0:T(8,128)(2,1)S(1)}, u32[]{:S(2)}, u32[]{:S(2)}) collective-permute-start(bf16[64,1536]{1,0:T(8,128)(2,1)S(1)} %fusion.5), channel_id=1, source_target_pairs={{0,28},{1,29},{2,6},{3,7},{4,0},{5,1},{6,10},{7,11},{8,4},{9,5},{1... | collective-permute-start | bytes 589832 | tf_op jit(solution)/shard_map/ppermute | solution.py:49
  92.5 7.9 %collective-permute-done.4 = bf16[64,1536]{1,0:T(8,128)(2,1)S(1)} collective-permute-done((bf16[64,1536]{1,0:T(8,128)(2,1)S(1)}, bf16[64,1536]{1,0:T(8,128)(2,1)S(1)}, u32[]{:S(2)}, u32[]{:S(2)}) %collective-permute-start.4) | collective-permute-done | bytes 196640 | tf_op jit(solution)/shard_map/ppermute | solution.py:49
  100.7 21.9 %collective-permute-start.5 = (bf16[64,1536]{1,0:T(8,128)(2,1)S(1)}, bf16[64,1536]{1,0:T(8,128)(2,1)S(1)}, u32[]{:S(2)}, u32[]{:S(2)}) collective-permute-start(bf16[64,1536]{1,0:T(8,128)(2,1)S(1)} %fusion.2), channel_id=1, source_target_pairs={{0,4},{1,5},{2,30},{3,31},{4,8},{5,9},{6,2},{7,3},{8,12},{9,13},{1... | collective-permute-start | bytes 589832 | tf_op jit(solution)/shard_map/ppermute | solution.py:49
  124.7 11.6 %collective-permute-done.5 = bf16[64,1536]{1,0:T(8,128)(2,1)S(1)} collective-permute-done((bf16[64,1536]{1,0:T(8,128)(2,1)S(1)}, bf16[64,1536]{1,0:T(8,128)(2,1)S(1)}, u32[]{:S(2)}, u32[]{:S(2)}) %collective-permute-start.5) | collective-permute-done | bytes 196640 | tf_op jit(solution)/shard_map/ppermute | solution.py:49
  136.6 8.0 %collective-permute-start.6 = (bf16[64,1536]{1,0:T(8,128)(2,1)S(1)}, bf16[64,1536]{1,0:T(8,128)(2,1)S(1)}, u32[]{:S(2)}, u32[]{:S(2)}) collective-permute-start(bf16[64,1536]{1,0:T(8,128)(2,1)S(1)} %fusion.1), channel_id=1, source_target_pairs={{0,4},{1,5},{2,30},{3,31},{4,8},{5,9},{6,2},{7,3},{8,12},{9,13},{1... | collective-permute-start | bytes 589832 | tf_op jit(solution)/shard_map/ppermute | solution.py:49
  144.9 4.4 %collective-permute-done.6 = bf16[64,1536]{1,0:T(8,128)(2,1)S(1)} collective-permute-done((bf16[64,1536]{1,0:T(8,128)(2,1)S(1)}, bf16[64,1536]{1,0:T(8,128)(2,1)S(1)}, u32[]{:S(2)}, u32[]{:S(2)}) %collective-permute-start.6) | collective-permute-done | bytes 196640 | tf_op jit(solution)/shard_map/ppermute | solution.py:49
  149.6 7.9 %collective-permute-start.13 = (bf16[64,768]{1,0:T(8,128)(2,1)S(1)}, bf16[64,768]{1,0:T(8,128)(2,1)S(1)}, u32[]{:S(2)}, u32[]{:S(2)}) collective-permute-start(bf16[64,768]{1,0:T(8,128)(2,1)S(1)} %fusion.19), channel_id=1, source_target_pairs={{0,4},{1,5},{2,30},{3,31},{4,8},{5,9},{6,2},{7,3},{8,12},{9,13},{1... | collective-permute-start | bytes 294920 | tf_op jit(solution)/shard_map/ppermute | solution.py:49
  161.5 5.7 %collective-permute-done.14 = bf16[64,768]{1,0:T(8,128)(2,1)S(1)} collective-permute-done((bf16[64,768]{1,0:T(8,128)(2,1)S(1)}, bf16[64,768]{1,0:T(8,128)(2,1)S(1)}, u32[]{:S(2)}, u32[]{:S(2)}) %collective-permute-start.14) | collective-permute-done | bytes 98336 | tf_op jit(solution)/shard_map/ppermute | solution.py:49
  168.4 4.1 %collective-permute-start.15 = (bf16[64,768]{1,0:T(8,128)(2,1)S(1)}, bf16[64,768]{1,0:T(8,128)(2,1)S(1)}, u32[]{:S(2)}, u32[]{:S(2)}) collective-permute-start(bf16[64,768]{1,0:T(8,128)(2,1)S(1)} %collective-permute-done.13), channel_id=1, source_target_pairs={{0,4},{1,5},{2,30},{3,31},{4,8},{5,9},{6,2},{7,3},{8,12},{9,13},{1... | collective-permute-start | bytes 294920 | tf_op jit(solution)/shard_map/ppermute | solution.py:49
  173.7 5.0 %collective-permute-start.16 = (bf16[64,768]{1,0:T(8,128)(2,1)S(1)}, bf16[64,768]{1,0:T(8,128)(2,1)S(1)}, u32[]{:S(2)}, u32[]{:S(2)}) collective-permute-start(bf16[64,768]{1,0:T(8,128)(2,1)S(1)} %collective-permute-done.14), channel_id=1, source_target_pairs={{0,28},{1,29},{2,6},{3,7},{4,0},{5,1},{6,10},{7,11},{8,4},{9,5},{1... | collective-permute-start | bytes 294920 | tf_op jit(solution)/shard_map/ppermute | solution.py:49
  178.8 4.2 %collective-permute-done.16 = bf16[64,768]{1,0:T(8,128)(2,1)S(1)} collective-permute-done((bf16[64,768]{1,0:T(8,128)(2,1)S(1)}, bf16[64,768]{1,0:T(8,128)(2,1)S(1)}, u32[]{:S(2)}, u32[]{:S(2)}) %collective-permute-start.16) | collective-permute-done | bytes 98336 | tf_op jit(solution)/shard_map/ppermute | solution.py:49
  184.2 6.2 %collective-permute-start.17 = (bf16[64,768]{1,0:T(8,128)(2,1)S(1)}, bf16[64,768]{1,0:T(8,128)(2,1)S(1)}, u32[]{:S(2)}, u32[]{:S(2)}) collective-permute-start(bf16[64,768]{1,0:T(8,128)(2,1)S(1)} %collective-permute-done.15), channel_id=1, source_target_pairs={{0,4},{1,5},{2,30},{3,31},{4,8},{5,9},{6,2},{7,3},{8,12},{9,13},{1... | collective-permute-start | bytes 294920 | tf_op jit(solution)/shard_map/ppermute | solution.py:49
  194.6 6.7 %collective-permute-done.18 = bf16[64,768]{1,0:T(8,128)(2,1)S(1)} collective-permute-done((bf16[64,768]{1,0:T(8,128)(2,1)S(1)}, bf16[64,768]{1,0:T(8,128)(2,1)S(1)}, u32[]{:S(2)}, u32[]{:S(2)}) %collective-permute-start.18) | collective-permute-done | bytes 98336 | tf_op jit(solution)/shard_map/ppermute | solution.py:49
  202.5 4.2 %collective-permute-start.19 = (bf16[64,768]{1,0:T(8,128)(2,1)S(1)}, bf16[64,768]{1,0:T(8,128)(2,1)S(1)}, u32[]{:S(2)}, u32[]{:S(2)}) collective-permute-start(bf16[64,768]{1,0:T(8,128)(2,1)S(1)} %collective-permute-done.17), channel_id=1, source_target_pairs={{0,4},{1,5},{2,30},{3,31},{4,8},{5,9},{6,2},{7,3},{8,12},{9,13},{1... | collective-permute-start | bytes 294920 | tf_op jit(solution)/shard_map/ppermute | solution.py:49
  207.8 3.9 %collective-permute-done.19 = bf16[64,768]{1,0:T(8,128)(2,1)S(1)} collective-permute-done((bf16[64,768]{1,0:T(8,128)(2,1)S(1)}, bf16[64,768]{1,0:T(8,128)(2,1)S(1)}, u32[]{:S(2)}, u32[]{:S(2)}) %collective-permute-start.19) | collective-permute-done | bytes 98336 | tf_op jit(solution)/shard_map/ppermute | solution.py:49
  212.9 19.2 %all-to-all-start.2 = ((f32[128,8,128]{2,1,0:T(8,128)}), f32[128,8,128]{2,1,0:T(8,128)S(1)}, u32[]{:S(2)}, u32[]{:S(2)}) async-start(f32[128,8,128]{2,1,0:T(8,128)} %bitcast.93), calls=%async_computation.2 | async-start | bytes 1048576 | tf_op jit(solution)/shard_map/all_to_all | solution.py:137
  232.6 18.3 %all-to-all-done.2 = f32[128,8,128]{2,1,0:T(8,128)S(1)} async-done(((f32[128,8,128]{2,1,0:T(8,128)}), f32[128,8,128]{2,1,0:T(8,128)S(1)}, u32[]{:S(2)}, u32[]{:S(2)}) %all-to-all-start.2) | async-done | bytes 524320 | tf_op jit(solution)/shard_map/all_to_all | solution.py:137
  (87 shorter events, 48.7 us)
Async XLA Ops:
  1.4 26.3 %collective-permute-start = (bf16[64,1536]{1,0:T(8,128)(2,1)S(1)}, bf16[64,1536]{1,0:T(8,128)(2,1)S(1)}, u32[]{:S(2)}, u32[]{:S(2)}) collective-permute-start(bf16[64,1536]{1,0:T(8,128)(2,1)S(1)} %pad_maximum_fusion.4), channel_id=1, source_target_pairs={{0,1},{1,2},{2,3},{3,0},{4,5},{5,6},{6,7},{7,4},{8,9},{9,10},{10,1... | collective-permute-start | bytes 589832 | tf_op jit(solution)/shard_map/ppermute | solution.py:52
  5.8 26.0 %collective-permute-start.1 = (bf16[64,1536]{1,0:T(8,128)(2,1)S(1)}, bf16[64,1536]{1,0:T(8,128)(2,1)S(1)}, u32[]{:S(2)}, u32[]{:S(2)}) collective-permute-start(bf16[64,1536]{1,0:T(8,128)(2,1)S(1)} %pad_maximum_fusion.5), channel_id=1, source_target_pairs={{0,2},{1,3},{2,0},{3,1},{4,6},{5,7},{6,4},{7,5},{8,10},{9,11},{10,... | collective-permute-start | bytes 589832 | tf_op jit(solution)/shard_map/ppermute | solution.py:52
  10.7 21.1 %collective-permute-start.2 = (bf16[64,1536]{1,0:T(8,128)(2,1)S(1)}, bf16[64,1536]{1,0:T(8,128)(2,1)S(1)}, u32[]{:S(2)}, u32[]{:S(2)}) collective-permute-start(bf16[64,1536]{1,0:T(8,128)(2,1)S(1)} %pad_maximum_fusion.6), channel_id=1, source_target_pairs={{0,3},{1,0},{2,1},{3,2},{4,7},{5,4},{6,5},{7,6},{8,11},{9,8},{10,9... | collective-permute-start | bytes 589832 | tf_op jit(solution)/shard_map/ppermute | solution.py:52
  14.0 7.9 %all-to-all-start = ((bf16[4,64,128]{2,1,0:T(8,128)(2,1)}), bf16[4,64,128]{2,1,0:T(8,128)(2,1)S(1)}, u32[]{:S(2)}, u32[]{:S(2)}) async-start(bf16[4,64,128]{2,1,0:T(8,128)(2,1)} %broadcast_in_dim.81), calls=%async_computation | async-start | bytes 131072 | tf_op jit(solution)/shard_map/all_to_all | solution.py:11
  22.8 26.5 %collective-permute-start.10 = (bf16[64,768]{1,0:T(8,128)(2,1)S(1)}, bf16[64,768]{1,0:T(8,128)(2,1)S(1)}, u32[]{:S(2)}, u32[]{:S(2)}) collective-permute-start(bf16[64,768]{1,0:T(8,128)(2,1)S(1)} %get-tuple-element.10), channel_id=1, source_target_pairs={{0,1},{1,2},{2,3},{3,0},{4,5},{5,6},{6,7},{7,4},{8,9},{9,10},{10,1... | collective-permute-start | bytes 294920 | tf_op jit(solution)/shard_map/ppermute | solution.py:52
  25.4 23.9 %collective-permute-start.11 = (bf16[64,768]{1,0:T(8,128)(2,1)S(1)}, bf16[64,768]{1,0:T(8,128)(2,1)S(1)}, u32[]{:S(2)}, u32[]{:S(2)}) collective-permute-start(bf16[64,768]{1,0:T(8,128)(2,1)S(1)} %get-tuple-element.11), channel_id=1, source_target_pairs={{0,2},{1,3},{2,0},{3,1},{4,6},{5,7},{6,4},{7,5},{8,10},{9,11},{10,... | collective-permute-start | bytes 294920 | tf_op jit(solution)/shard_map/ppermute | solution.py:52
  27.7 21.6 %collective-permute-start.12 = (bf16[64,768]{1,0:T(8,128)(2,1)S(1)}, bf16[64,768]{1,0:T(8,128)(2,1)S(1)}, u32[]{:S(2)}, u32[]{:S(2)}) collective-permute-start(bf16[64,768]{1,0:T(8,128)(2,1)S(1)} %get-tuple-element.12), channel_id=1, source_target_pairs={{0,3},{1,0},{2,1},{3,2},{4,7},{5,4},{6,5},{7,6},{8,11},{9,8},{10,9... | collective-permute-start | bytes 294920 | tf_op jit(solution)/shard_map/ppermute | solution.py:52
  31.9 26.4 %all-to-all-start.1 = ((bf16[32,16,256]{2,1,0:T(8,128)(2,1)}), bf16[32,16,256]{2,1,0:T(8,128)(2,1)S(1)}, u32[]{:S(2)}, u32[]{:S(2)}) async-start(bf16[32,16,256]{2,1,0:T(8,128)(2,1)} %bitcast.11), calls=%async_computation.1 | async-start | bytes 524288 | tf_op jit(solution)/shard_map/all_to_all | solution.py:11
  58.5 20.5 %collective-permute-start.3 = (bf16[64,1536]{1,0:T(8,128)(2,1)S(1)}, bf16[64,1536]{1,0:T(8,128)(2,1)S(1)}, u32[]{:S(2)}, u32[]{:S(2)}) collective-permute-start(bf16[64,1536]{1,0:T(8,128)(2,1)S(1)} %convolution_convert_fusion.1), channel_id=1, source_target_pairs={{0,4},{1,5},{2,30},{3,31},{4,8},{5,9},{6,2},{7,3},{8,12},{9,13},{1... | collective-permute-start | bytes 589832 | tf_op jit(solution)/shard_map/ppermute | solution.py:49
  64.3 20.7 %collective-permute-start.7 = (bf16[64,1536]{1,0:T(8,128)(2,1)S(1)}, bf16[64,1536]{1,0:T(8,128)(2,1)S(1)}, u32[]{:S(2)}, u32[]{:S(2)}) collective-permute-start(bf16[64,1536]{1,0:T(8,128)(2,1)S(1)} %convolution_convert_fusion), channel_id=1, source_target_pairs={{0,28},{1,29},{2,6},{3,7},{4,0},{5,1},{6,10},{7,11},{8,4},{9,5},{1... | collective-permute-start | bytes 589832 | tf_op jit(solution)/shard_map/ppermute | solution.py:49
  79.3 21.1 %collective-permute-start.4 = (bf16[64,1536]{1,0:T(8,128)(2,1)S(1)}, bf16[64,1536]{1,0:T(8,128)(2,1)S(1)}, u32[]{:S(2)}, u32[]{:S(2)}) collective-permute-start(bf16[64,1536]{1,0:T(8,128)(2,1)S(1)} %fusion.3), channel_id=1, source_target_pairs={{0,4},{1,5},{2,30},{3,31},{4,8},{5,9},{6,2},{7,3},{8,12},{9,13},{1... | collective-permute-start | bytes 589832 | tf_op jit(solution)/shard_map/ppermute | solution.py:49
  85.2 37.3 %collective-permute-start.8 = (bf16[64,1536]{1,0:T(8,128)(2,1)S(1)}, bf16[64,1536]{1,0:T(8,128)(2,1)S(1)}, u32[]{:S(2)}, u32[]{:S(2)}) collective-permute-start(bf16[64,1536]{1,0:T(8,128)(2,1)S(1)} %fusion.5), channel_id=1, source_target_pairs={{0,28},{1,29},{2,6},{3,7},{4,0},{5,1},{6,10},{7,11},{8,4},{9,5},{1... | collective-permute-start | bytes 589832 | tf_op jit(solution)/shard_map/ppermute | solution.py:49
  100.7 35.6 %collective-permute-start.5 = (bf16[64,1536]{1,0:T(8,128)(2,1)S(1)}, bf16[64,1536]{1,0:T(8,128)(2,1)S(1)}, u32[]{:S(2)}, u32[]{:S(2)}) collective-permute-start(bf16[64,1536]{1,0:T(8,128)(2,1)S(1)} %fusion.2), channel_id=1, source_target_pairs={{0,4},{1,5},{2,30},{3,31},{4,8},{5,9},{6,2},{7,3},{8,12},{9,13},{1... | collective-permute-start | bytes 589832 | tf_op jit(solution)/shard_map/ppermute | solution.py:49
  122.8 22.0 %collective-permute-start.9 = (bf16[64,1536]{1,0:T(8,128)(2,1)S(1)}, bf16[64,1536]{1,0:T(8,128)(2,1)S(1)}, u32[]{:S(2)}, u32[]{:S(2)}) collective-permute-start(bf16[64,1536]{1,0:T(8,128)(2,1)S(1)} %fusion.4), channel_id=1, source_target_pairs={{0,28},{1,29},{2,6},{3,7},{4,0},{5,1},{6,10},{7,11},{8,4},{9,5},{1... | collective-permute-start | bytes 589832 | tf_op jit(solution)/shard_map/ppermute | solution.py:49
  136.6 12.7 %collective-permute-start.6 = (bf16[64,1536]{1,0:T(8,128)(2,1)S(1)}, bf16[64,1536]{1,0:T(8,128)(2,1)S(1)}, u32[]{:S(2)}, u32[]{:S(2)}) collective-permute-start(bf16[64,1536]{1,0:T(8,128)(2,1)S(1)} %fusion.1), channel_id=1, source_target_pairs={{0,4},{1,5},{2,30},{3,31},{4,8},{5,9},{6,2},{7,3},{8,12},{9,13},{1... | collective-permute-start | bytes 589832 | tf_op jit(solution)/shard_map/ppermute | solution.py:49
  149.6 11.9 %collective-permute-start.13 = (bf16[64,768]{1,0:T(8,128)(2,1)S(1)}, bf16[64,768]{1,0:T(8,128)(2,1)S(1)}, u32[]{:S(2)}, u32[]{:S(2)}) collective-permute-start(bf16[64,768]{1,0:T(8,128)(2,1)S(1)} %fusion.19), channel_id=1, source_target_pairs={{0,4},{1,5},{2,30},{3,31},{4,8},{5,9},{6,2},{7,3},{8,12},{9,13},{1... | collective-permute-start | bytes 294920 | tf_op jit(solution)/shard_map/ppermute | solution.py:49
  157.5 9.7 %collective-permute-start.14 = (bf16[64,768]{1,0:T(8,128)(2,1)S(1)}, bf16[64,768]{1,0:T(8,128)(2,1)S(1)}, u32[]{:S(2)}, u32[]{:S(2)}) collective-permute-start(bf16[64,768]{1,0:T(8,128)(2,1)S(1)} %fusion.19), channel_id=1, source_target_pairs={{0,28},{1,29},{2,6},{3,7},{4,0},{5,1},{6,10},{7,11},{8,4},{9,5},{1... | collective-permute-start | bytes 294920 | tf_op jit(solution)/shard_map/ppermute | solution.py:49
  168.4 10.4 %collective-permute-start.15 = (bf16[64,768]{1,0:T(8,128)(2,1)S(1)}, bf16[64,768]{1,0:T(8,128)(2,1)S(1)}, u32[]{:S(2)}, u32[]{:S(2)}) collective-permute-start(bf16[64,768]{1,0:T(8,128)(2,1)S(1)} %collective-permute-done.13), channel_id=1, source_target_pairs={{0,4},{1,5},{2,30},{3,31},{4,8},{5,9},{6,2},{7,3},{8,12},{9,13},{1... | collective-permute-start | bytes 294920 | tf_op jit(solution)/shard_map/ppermute | solution.py:49
  173.7 9.3 %collective-permute-start.16 = (bf16[64,768]{1,0:T(8,128)(2,1)S(1)}, bf16[64,768]{1,0:T(8,128)(2,1)S(1)}, u32[]{:S(2)}, u32[]{:S(2)}) collective-permute-start(bf16[64,768]{1,0:T(8,128)(2,1)S(1)} %collective-permute-done.14), channel_id=1, source_target_pairs={{0,28},{1,29},{2,6},{3,7},{4,0},{5,1},{6,10},{7,11},{8,4},{9,5},{1... | collective-permute-start | bytes 294920 | tf_op jit(solution)/shard_map/ppermute | solution.py:49
  184.2 10.4 %collective-permute-start.17 = (bf16[64,768]{1,0:T(8,128)(2,1)S(1)}, bf16[64,768]{1,0:T(8,128)(2,1)S(1)}, u32[]{:S(2)}, u32[]{:S(2)}) collective-permute-start(bf16[64,768]{1,0:T(8,128)(2,1)S(1)} %collective-permute-done.15), channel_id=1, source_target_pairs={{0,4},{1,5},{2,30},{3,31},{4,8},{5,9},{6,2},{7,3},{8,12},{9,13},{1... | collective-permute-start | bytes 294920 | tf_op jit(solution)/shard_map/ppermute | solution.py:49
  191.6 9.7 %collective-permute-start.18 = (bf16[64,768]{1,0:T(8,128)(2,1)S(1)}, bf16[64,768]{1,0:T(8,128)(2,1)S(1)}, u32[]{:S(2)}, u32[]{:S(2)}) collective-permute-start(bf16[64,768]{1,0:T(8,128)(2,1)S(1)} %collective-permute-done.16), channel_id=1, source_target_pairs={{0,28},{1,29},{2,6},{3,7},{4,0},{5,1},{6,10},{7,11},{8,4},{9,5},{1... | collective-permute-start | bytes 294920 | tf_op jit(solution)/shard_map/ppermute | solution.py:49
  202.5 9.3 %collective-permute-start.19 = (bf16[64,768]{1,0:T(8,128)(2,1)S(1)}, bf16[64,768]{1,0:T(8,128)(2,1)S(1)}, u32[]{:S(2)}, u32[]{:S(2)}) collective-permute-start(bf16[64,768]{1,0:T(8,128)(2,1)S(1)} %collective-permute-done.17), channel_id=1, source_target_pairs={{0,4},{1,5},{2,30},{3,31},{4,8},{5,9},{6,2},{7,3},{8,12},{9,13},{1... | collective-permute-start | bytes 294920 | tf_op jit(solution)/shard_map/ppermute | solution.py:49
  207.8 24.3 %copy-start.3 = (s32[128,8]{0,1:T(8,128)S(1)}, s32[128,8]{0,1:T(8,128)}, u32[]{:S(2)}) copy-start(s32[128,8]{0,1:T(8,128)} %param.8) | copy-start | bytes 12292
  212.9 38.0 %all-to-all-start.2 = ((f32[128,8,128]{2,1,0:T(8,128)}), f32[128,8,128]{2,1,0:T(8,128)S(1)}, u32[]{:S(2)}, u32[]{:S(2)}) async-start(f32[128,8,128]{2,1,0:T(8,128)} %bitcast.93), calls=%async_computation.2 | async-start | bytes 1048576 | tf_op jit(solution)/shard_map/all_to_all | solution.py:137
  (3 other events, 48.5 us)

commit v6 on v4

--- a/solution.py
+++ b/solution.py
@@ -110,21 +110,20 @@
     acts = term(0) + ahead.astype(F32) + behind.astype(F32)
     own = (jax.nn.silu(acts[:, :units]) * acts[:, units:]).astype(BF16)
 
-    result = jnp.zeros((ring, chunk, local * share), F32)
+    hidden = jnp.zeros((ring, chunk, units), BF16)
 
-    def put(result, hidden, k):
-        return lax.dynamic_update_index_in_dim(
-            result, rows_dot(hidden, w_down), chunk_at[k % ring], 0
-        )
+    def put(hidden, arrived, k):
+        return lax.dynamic_update_index_in_dim(hidden, arrived, chunk_at[k % ring], 0)
 
     ahead = behind = own
-    result = put(result, own, 0)
+    hidden = put(hidden, own, 0)
     for k in range(1, steps + 1):
         ahead = ship(ahead, 1)
-        result = put(result, ahead, -k)
+        hidden = put(hidden, ahead, -k)
         if k < steps:
             behind = ship(behind, -1)
-            result = put(result, behind, k)
+            hidden = put(hidden, behind, k)
+    result = rows_dot(hidden.reshape(slots, units), w_down)
     back = exchange(result.reshape(ep, capacity, -1), "ep").reshape(slots, -1)
 
     mixed = lax.dot_general(

time: 218 us -> 229 us (1.050)
  waiting for transfers between devices: 37.6 us -> 58.6 us
  starting transfers between devices: 155 us -> 144 us
  blocking collectives: 7.43 us -> 15.5 us
  matrix products: 10.9 us -> 4.88 us
    ppermute x14, waiting for transfers between devices: 17.5 us -> 38.6 us  [ship(): return lax.ppermute(x, 'tp', pairs)]
    all_to_all x3, starting transfers between devices: 41.4 us -> 29 us  [exchange(): lax.all_to_all(x, axis, split_axis=0, concat_axis=0, tiled=True, axis_ind...]
    all_to_all x1, blocking collectives: 7.43 us -> 15.5 us  [exchange(): lax.all_to_all(x, axis, split_axis=0, concat_axis=0, tiled=True, axis_ind...]
    dot_general x9 -> x2, matrix products: 8.15 us -> 2.15 us  [rows_dot(): lax.dot_general(a, b, (((1,), (1,)), ((), ())), preferred_element_type=F32)]
    ppermute x14, starting transfers between devices: 81.4 us -> 85.3 us  [ship(): return lax.ppermute(x, 'tp', pairs)]
    ppermute x6, starting transfers between devices: 32.4 us -> 29.7 us  [beside(): lax.ppermute(x, 'tp', [(g[i], g[(i + k) % local]) for g in near for i in...]
  transfers between devices with their start and end apart: 23 -> 23, of which waited for: 7 -> 11; matrix products, arithmetic and copies ran while one was open for 6% -> 2% of each run, Pallas kernels for 0% -> 0%
where the time goes in v6:
time: 229 us; the launch traced here: 228 us
  starting transfers between devices  144 us (63%)
  waiting for transfers between devices  58.6 us (26%)
  blocking collectives  15.5 us (7%)
  matrix products  4.88 us (2%)
  local copies, waits for them, and re-layouts  3.13 us (1%)
    ppermute x14, starting transfers between devices, ship(): return lax.ppermute(x, 'tp', pairs)  85.3 us
    ppermute x14, waiting for transfers between devices, ship(): return lax.ppermute(x, 'tp', pairs)  38.6 us
    ppermute x6, starting transfers between devices, beside(): lax.ppermute(x, 'tp', [(g[i], g[(i + k) % local]) for g in near for i in...  29.7 us
    all_to_all x3, starting transfers between devices, exchange(): lax.all_to_all(x, axis, split_axis=0, concat_axis=0, tiled=True, axis_ind...  29 us
    all_to_all x3, waiting for transfers between devices, exchange(): lax.all_to_all(x, axis, split_axis=0, concat_axis=0, tiled=True, axis_ind...  20 us
    all_to_all x1, blocking collectives, exchange(): lax.all_to_all(x, axis, split_axis=0, concat_axis=0, tiled=True, axis_ind...  15.5 us
  transfers between devices with their start and end apart: 23, of which 11 were waited for; matrix products, arithmetic and copies ran while one was open for 2% of the time, Pallas kernels for 0%

profile of v6, /device:TPU:1, one launch (start us, length us, event | category | flops | bytes accessed | tf_op | source)
XLA Modules:
  0.0 228.1 jit_solution(7971972268784723943)
XLA Ops:
  1.3 6.4 %all-to-all-start = ((bf16[4,64,128]{2,1,0:T(8,128)(2,1)}), bf16[4,64,128]{2,1,0:T(8,128)(2,1)S(1)}, u32[]{:S(2)}, u32[]{:S(2)}) async-start(bf16[4,64,128]{2,1,0:T(8,128)(2,1)} %broadcast_in_dim.68), calls=%async_computation | async-start | bytes 131072 | tf_op jit(solution)/shard_map/all_to_all | solution.py:11
  9.1 3.5 %collective-permute-start = (bf16[64,1536]{1,0:T(8,128)(2,1)S(1)}, bf16[64,1536]{1,0:T(8,128)(2,1)S(1)}, u32[]{:S(2)}, u32[]{:S(2)}) collective-permute-start(bf16[64,1536]{1,0:T(8,128)(2,1)S(1)} %pad_maximum_fusion.1), channel_id=1, source_target_pairs={{0,1},{1,2},{2,3},{3,0},{4,5},{5,6},{6,7},{7,4},{8,9},{9,10},{10,1... | collective-permute-start | bytes 589832 | tf_op jit(solution)/shard_map/ppermute | solution.py:52
  12.6 4.0 %collective-permute-start.1 = (bf16[64,1536]{1,0:T(8,128)(2,1)S(1)}, bf16[64,1536]{1,0:T(8,128)(2,1)S(1)}, u32[]{:S(2)}, u32[]{:S(2)}) collective-permute-start(bf16[64,1536]{1,0:T(8,128)(2,1)S(1)} %pad_maximum_fusion.2), channel_id=1, source_target_pairs={{0,2},{1,3},{2,0},{3,1},{4,6},{5,7},{6,4},{7,5},{8,10},{9,11},{10,... | collective-permute-start | bytes 589832 | tf_op jit(solution)/shard_map/ppermute | solution.py:52
  21.3 15.6 %all-to-all-start.1 = ((bf16[32,16,256]{2,1,0:T(8,128)(2,1)}), bf16[32,16,256]{2,1,0:T(8,128)(2,1)S(1)}, u32[]{:S(2)}, u32[]{:S(2)}) async-start(bf16[32,16,256]{2,1,0:T(8,128)(2,1)} %bitcast.11), calls=%async_computation.1 | async-start | bytes 524288 | tf_op jit(solution)/shard_map/all_to_all | solution.py:11
  37.1 8.8 %all-to-all-done.1 = bf16[32,16,256]{2,1,0:T(8,128)(2,1)S(1)} async-done(((bf16[32,16,256]{2,1,0:T(8,128)(2,1)}), bf16[32,16,256]{2,1,0:T(8,128)(2,1)S(1)}, u32[]{:S(2)}, u32[]{:S(2)}) %all-to-all-start.1) | async-done | bytes 262176 | tf_op jit(solution)/shard_map/all_to_all | solution.py:11
  48.7 10.2 %collective-permute-start.7 = (bf16[64,1536]{1,0:T(8,128)(2,1)S(1)}, bf16[64,1536]{1,0:T(8,128)(2,1)S(1)}, u32[]{:S(2)}, u32[]{:S(2)}) collective-permute-start(bf16[64,1536]{1,0:T(8,128)(2,1)S(1)} %convolution_convert_fusion), channel_id=1, source_target_pairs={{0,28},{1,29},{2,6},{3,7},{4,0},{5,1},{6,10},{7,11},{8,4},{9,5},{1... | collective-permute-start | bytes 589832 | tf_op jit(solution)/shard_map/ppermute | solution.py:49
  62.1 11.2 %collective-permute-start.4 = (bf16[64,1536]{1,0:T(8,128)(2,1)S(1)}, bf16[64,1536]{1,0:T(8,128)(2,1)S(1)}, u32[]{:S(2)}, u32[]{:S(2)}) collective-permute-start(bf16[64,1536]{1,0:T(8,128)(2,1)S(1)} %fusion.3), channel_id=1, source_target_pairs={{0,4},{1,5},{2,30},{3,31},{4,8},{5,9},{6,2},{7,3},{8,12},{9,13},{1... | collective-permute-start | bytes 589832 | tf_op jit(solution)/shard_map/ppermute | solution.py:49
  73.6 4.9 %collective-permute-start.8 = (bf16[64,1536]{1,0:T(8,128)(2,1)S(1)}, bf16[64,1536]{1,0:T(8,128)(2,1)S(1)}, u32[]{:S(2)}, u32[]{:S(2)}) collective-permute-start(bf16[64,1536]{1,0:T(8,128)(2,1)S(1)} %fusion.5), channel_id=1, source_target_pairs={{0,28},{1,29},{2,6},{3,7},{4,0},{5,1},{6,10},{7,11},{8,4},{9,5},{1... | collective-permute-start | bytes 589832 | tf_op jit(solution)/shard_map/ppermute | solution.py:49
  78.6 4.7 %collective-permute-done.4 = bf16[64,1536]{1,0:T(8,128)(2,1)S(1)} collective-permute-done((bf16[64,1536]{1,0:T(8,128)(2,1)S(1)}, bf16[64,1536]{1,0:T(8,128)(2,1)S(1)}, u32[]{:S(2)}, u32[]{:S(2)}) %collective-permute-start.4) | collective-permute-done | bytes 196640 | tf_op jit(solution)/shard_map/ppermute | solution.py:49
  83.5 16.5 %collective-permute-start.5 = (bf16[64,1536]{1,0:T(8,128)(2,1)S(1)}, bf16[64,1536]{1,0:T(8,128)(2,1)S(1)}, u32[]{:S(2)}, u32[]{:S(2)}) collective-permute-start(bf16[64,1536]{1,0:T(8,128)(2,1)S(1)} %fusion.2), channel_id=1, source_target_pairs={{0,4},{1,5},{2,30},{3,31},{4,8},{5,9},{6,2},{7,3},{8,12},{9,13},{1... | collective-permute-start | bytes 589832 | tf_op jit(solution)/shard_map/ppermute | solution.py:49
  103.5 4.2 %collective-permute-done.5 = bf16[64,1536]{1,0:T(8,128)(2,1)S(1)} collective-permute-done((bf16[64,1536]{1,0:T(8,128)(2,1)S(1)}, bf16[64,1536]{1,0:T(8,128)(2,1)S(1)}, u32[]{:S(2)}, u32[]{:S(2)}) %collective-permute-start.5) | collective-permute-done | bytes 196640 | tf_op jit(solution)/shard_map/ppermute | solution.py:49
  108.0 3.4 %collective-permute-start.6 = (bf16[64,1536]{1,0:T(8,128)(2,1)S(1)}, bf16[64,1536]{1,0:T(8,128)(2,1)S(1)}, u32[]{:S(2)}, u32[]{:S(2)}) collective-permute-start(bf16[64,1536]{1,0:T(8,128)(2,1)S(1)} %fusion.1), channel_id=1, source_target_pairs={{0,4},{1,5},{2,30},{3,31},{4,8},{5,9},{6,2},{7,3},{8,12},{9,13},{1... | collective-permute-start | bytes 589832 | tf_op jit(solution)/shard_map/ppermute | solution.py:49
  111.4 3.5 %collective-permute-done.9 = bf16[64,1536]{1,0:T(8,128)(2,1)S(1)} collective-permute-done((bf16[64,1536]{1,0:T(8,128)(2,1)S(1)}, bf16[64,1536]{1,0:T(8,128)(2,1)S(1)}, u32[]{:S(2)}, u32[]{:S(2)}) %collective-permute-start.9) | collective-permute-done | bytes 196640 | tf_op jit(solution)/shard_map/ppermute | solution.py:49
  114.9 12.5 %collective-permute-done.6 = bf16[64,1536]{1,0:T(8,128)(2,1)S(1)} collective-permute-done((bf16[64,1536]{1,0:T(8,128)(2,1)S(1)}, bf16[64,1536]{1,0:T(8,128)(2,1)S(1)}, u32[]{:S(2)}, u32[]{:S(2)}) %collective-permute-start.6) | collective-permute-done | bytes 196640 | tf_op jit(solution)/shard_map/ppermute | solution.py:49
  132.2 12.4 %collective-permute-start.18 = (bf16[64,768]{1,0:T(8,128)(2,1)S(1)}, bf16[64,768]{1,0:T(8,128)(2,1)S(1)}, u32[]{:S(2)}, u32[]{:S(2)}) collective-permute-start(bf16[64,768]{1,0:T(8,128)(2,1)S(1)} %get-tuple-element.11), channel_id=1, source_target_pairs={{0,2},{1,3},{2,0},{3,1},{4,6},{5,7},{6,4},{7,5},{8,10},{9,11},{10,... | collective-permute-start | bytes 294920 | tf_op jit(solution)/shard_map/ppermute | solution.py:52
  144.6 4.3 %collective-permute-start.19 = (bf16[64,768]{1,0:T(8,128)(2,1)S(1)}, bf16[64,768]{1,0:T(8,128)(2,1)S(1)}, u32[]{:S(2)}, u32[]{:S(2)}) collective-permute-start(bf16[64,768]{1,0:T(8,128)(2,1)S(1)} %get-tuple-element.12), channel_id=1, source_target_pairs={{0,3},{1,0},{2,1},{3,2},{4,7},{5,4},{6,5},{7,6},{8,11},{9,8},{10,9... | collective-permute-start | bytes 294920 | tf_op jit(solution)/shard_map/ppermute | solution.py:52
  148.9 7.2 %collective-permute-start.11 = (bf16[64,768]{1,0:T(8,128)(2,1)S(1)}, bf16[64,768]{1,0:T(8,128)(2,1)S(1)}, u32[]{:S(2)}, u32[]{:S(2)}) collective-permute-start(bf16[64,768]{1,0:T(8,128)(2,1)S(1)} %get-tuple-element.14), channel_id=1, source_target_pairs={{0,28},{1,29},{2,6},{3,7},{4,0},{5,1},{6,10},{7,11},{8,4},{9,5},{1... | collective-permute-start | bytes 294920 | tf_op jit(solution)/shard_map/ppermute | solution.py:49
  158.3 10.5 %collective-permute-start.13 = (bf16[64,768]{1,0:T(8,128)(2,1)S(1)}, bf16[64,768]{1,0:T(8,128)(2,1)S(1)}, u32[]{:S(2)}, u32[]{:S(2)}) collective-permute-start(bf16[64,768]{1,0:T(8,128)(2,1)S(1)} %collective-permute-done.11), channel_id=1, source_target_pairs={{0,28},{1,29},{2,6},{3,7},{4,0},{5,1},{6,10},{7,11},{8,4},{9,5},{1... | collective-permute-start | bytes 294920 | tf_op jit(solution)/shard_map/ppermute | solution.py:49
  170.8 3.3 %collective-permute-done.13 = bf16[64,768]{1,0:T(8,128)(2,1)S(1)} collective-permute-done((bf16[64,768]{1,0:T(8,128)(2,1)S(1)}, bf16[64,768]{1,0:T(8,128)(2,1)S(1)}, u32[]{:S(2)}, u32[]{:S(2)}) %collective-permute-start.13) | collective-permute-done | bytes 98336 | tf_op jit(solution)/shard_map/ppermute | solution.py:49
  174.1 8.0 %collective-permute-start.15 = (bf16[64,768]{1,0:T(8,128)(2,1)S(1)}, bf16[64,768]{1,0:T(8,128)(2,1)S(1)}, u32[]{:S(2)}, u32[]{:S(2)}) collective-permute-start(bf16[64,768]{1,0:T(8,128)(2,1)S(1)} %collective-permute-done.13), channel_id=1, source_target_pairs={{0,28},{1,29},{2,6},{3,7},{4,0},{5,1},{6,10},{7,11},{8,4},{9,5},{1... | collective-permute-start | bytes 294920 | tf_op jit(solution)/shard_map/ppermute | solution.py:49
  186.1 5.3 %collective-permute-done.16 = bf16[64,768]{1,0:T(8,128)(2,1)S(1)} collective-permute-done((bf16[64,768]{1,0:T(8,128)(2,1)S(1)}, bf16[64,768]{1,0:T(8,128)(2,1)S(1)}, u32[]{:S(2)}, u32[]{:S(2)}) %collective-permute-start.16) | collective-permute-done | bytes 98336 | tf_op jit(solution)/shard_map/ppermute | solution.py:49
  192.7 7.0 %all-to-all-start.2 = ((f32[32,16,256]{2,1,0:T(8,128)}), f32[32,16,256]{2,1,0:T(8,128)S(1)}, u32[]{:S(2)}, u32[]{:S(2)}) async-start(f32[32,16,256]{2,1,0:T(8,128)} %fusion.6), calls=%async_computation.2 | async-start | bytes 1048576 | tf_op jit(solution)/shard_map/all_to_all | solution.py:11
  199.9 11.2 %all-to-all-done.2 = f32[32,16,256]{2,1,0:T(8,128)S(1)} async-done(((f32[32,16,256]{2,1,0:T(8,128)}), f32[32,16,256]{2,1,0:T(8,128)S(1)}, u32[]{:S(2)}, u32[]{:S(2)}) %all-to-all-start.2) | async-done | bytes 524320 | tf_op jit(solution)/shard_map/all_to_all | solution.py:11
  211.9 15.5 %all_to_all.20 = f32[4,64,128]{2,1,0:T(8,128)S(1)} all-to-all(f32[4,64,128]{2,1,0:T(8,128)S(1)} %pad_maximum_fusion.4), channel_id=1, replica_groups={{0,1,2,3},{4,5,6,7},{8,9,10,11},{12,13,14,15},{16,17,18,19},{20,21,22,2..., dimensions={0} | all-to-all | bytes 262144 | tf_op jit(solution)/shard_map/all_to_all | solution.py:11
  (71 shorter events, 33.2 us)
Async XLA Ops:
  1.3 19.0 %all-to-all-start = ((bf16[4,64,128]{2,1,0:T(8,128)(2,1)}), bf16[4,64,128]{2,1,0:T(8,128)(2,1)S(1)}, u32[]{:S(2)}, u32[]{:S(2)}) async-start(bf16[4,64,128]{2,1,0:T(8,128)(2,1)} %broadcast_in_dim.68), calls=%async_computation | async-start | bytes 131072 | tf_op jit(solution)/shard_map/all_to_all | solution.py:11
  9.1 11.2 %copy-start = (bf16[4,64,768]{2,1,0:T(8,128)(2,1)S(1)}, bf16[4,64,768]{2,1,0:T(8,128)(2,1)}, u32[]{:S(2)}) copy-start(bf16[4,64,768]{2,1,0:T(8,128)(2,1)} %param.11) | copy-start | bytes 1179652
  9.1 27.9 %collective-permute-start = (bf16[64,1536]{1,0:T(8,128)(2,1)S(1)}, bf16[64,1536]{1,0:T(8,128)(2,1)S(1)}, u32[]{:S(2)}, u32[]{:S(2)}) collective-permute-start(bf16[64,1536]{1,0:T(8,128)(2,1)S(1)} %pad_maximum_fusion.1), channel_id=1, source_target_pairs={{0,1},{1,2},{2,3},{3,0},{4,5},{5,6},{6,7},{7,4},{8,9},{9,10},{10,1... | collective-permute-start | bytes 589832 | tf_op jit(solution)/shard_map/ppermute | solution.py:52
  12.6 24.4 %collective-permute-start.1 = (bf16[64,1536]{1,0:T(8,128)(2,1)S(1)}, bf16[64,1536]{1,0:T(8,128)(2,1)S(1)}, u32[]{:S(2)}, u32[]{:S(2)}) collective-permute-start(bf16[64,1536]{1,0:T(8,128)(2,1)S(1)} %pad_maximum_fusion.2), channel_id=1, source_target_pairs={{0,2},{1,3},{2,0},{3,1},{4,6},{5,7},{6,4},{7,5},{8,10},{9,11},{10,... | collective-permute-start | bytes 589832 | tf_op jit(solution)/shard_map/ppermute | solution.py:52
  16.7 20.4 %collective-permute-start.2 = (bf16[64,1536]{1,0:T(8,128)(2,1)S(1)}, bf16[64,1536]{1,0:T(8,128)(2,1)S(1)}, u32[]{:S(2)}, u32[]{:S(2)}) collective-permute-start(bf16[64,1536]{1,0:T(8,128)(2,1)S(1)} %pad_maximum_fusion.3), channel_id=1, source_target_pairs={{0,3},{1,0},{2,1},{3,2},{4,7},{5,4},{6,5},{7,6},{8,11},{9,8},{10,9... | collective-permute-start | bytes 589832 | tf_op jit(solution)/shard_map/ppermute | solution.py:52
  21.3 24.6 %all-to-all-start.1 = ((bf16[32,16,256]{2,1,0:T(8,128)(2,1)}), bf16[32,16,256]{2,1,0:T(8,128)(2,1)S(1)}, u32[]{:S(2)}, u32[]{:S(2)}) async-start(bf16[32,16,256]{2,1,0:T(8,128)(2,1)} %bitcast.11), calls=%async_computation.1 | async-start | bytes 524288 | tf_op jit(solution)/shard_map/all_to_all | solution.py:11
  46.1 15.7 %collective-permute-start.3 = (bf16[64,1536]{1,0:T(8,128)(2,1)S(1)}, bf16[64,1536]{1,0:T(8,128)(2,1)S(1)}, u32[]{:S(2)}, u32[]{:S(2)}) collective-permute-start(bf16[64,1536]{1,0:T(8,128)(2,1)S(1)} %convolution_convert_fusion.1), channel_id=1, source_target_pairs={{0,4},{1,5},{2,30},{3,31},{4,8},{5,9},{6,2},{7,3},{8,12},{9,13},{1... | collective-permute-start | bytes 589832 | tf_op jit(solution)/shard_map/ppermute | solution.py:49
  48.7 24.7 %collective-permute-start.7 = (bf16[64,1536]{1,0:T(8,128)(2,1)S(1)}, bf16[64,1536]{1,0:T(8,128)(2,1)S(1)}, u32[]{:S(2)}, u32[]{:S(2)}) collective-permute-start(bf16[64,1536]{1,0:T(8,128)(2,1)S(1)} %convolution_convert_fusion), channel_id=1, source_target_pairs={{0,28},{1,29},{2,6},{3,7},{4,0},{5,1},{6,10},{7,11},{8,4},{9,5},{1... | collective-permute-start | bytes 589832 | tf_op jit(solution)/shard_map/ppermute | solution.py:49
  62.1 21.1 %collective-permute-start.4 = (bf16[64,1536]{1,0:T(8,128)(2,1)S(1)}, bf16[64,1536]{1,0:T(8,128)(2,1)S(1)}, u32[]{:S(2)}, u32[]{:S(2)}) collective-permute-start(bf16[64,1536]{1,0:T(8,128)(2,1)S(1)} %fusion.3), channel_id=1, source_target_pairs={{0,4},{1,5},{2,30},{3,31},{4,8},{5,9},{6,2},{7,3},{8,12},{9,13},{1... | collective-permute-start | bytes 589832 | tf_op jit(solution)/shard_map/ppermute | solution.py:49
  73.6 26.4 %collective-permute-start.8 = (bf16[64,1536]{1,0:T(8,128)(2,1)S(1)}, bf16[64,1536]{1,0:T(8,128)(2,1)S(1)}, u32[]{:S(2)}, u32[]{:S(2)}) collective-permute-start(bf16[64,1536]{1,0:T(8,128)(2,1)S(1)} %fusion.5), channel_id=1, source_target_pairs={{0,28},{1,29},{2,6},{3,7},{4,0},{5,1},{6,10},{7,11},{8,4},{9,5},{1... | collective-permute-start | bytes 589832 | tf_op jit(solution)/shard_map/ppermute | solution.py:49
  83.5 24.2 %collective-permute-start.5 = (bf16[64,1536]{1,0:T(8,128)(2,1)S(1)}, bf16[64,1536]{1,0:T(8,128)(2,1)S(1)}, u32[]{:S(2)}, u32[]{:S(2)}) collective-permute-start(bf16[64,1536]{1,0:T(8,128)(2,1)S(1)} %fusion.2), channel_id=1, source_target_pairs={{0,4},{1,5},{2,30},{3,31},{4,8},{5,9},{6,2},{7,3},{8,12},{9,13},{1... | collective-permute-start | bytes 589832 | tf_op jit(solution)/shard_map/ppermute | solution.py:49
  100.3 14.6 %collective-permute-start.9 = (bf16[64,1536]{1,0:T(8,128)(2,1)S(1)}, bf16[64,1536]{1,0:T(8,128)(2,1)S(1)}, u32[]{:S(2)}, u32[]{:S(2)}) collective-permute-start(bf16[64,1536]{1,0:T(8,128)(2,1)S(1)} %fusion.4), channel_id=1, source_target_pairs={{0,28},{1,29},{2,6},{3,7},{4,0},{5,1},{6,10},{7,11},{8,4},{9,5},{1... | collective-permute-start | bytes 589832 | tf_op jit(solution)/shard_map/ppermute | solution.py:49
  108.0 19.4 %collective-permute-start.6 = (bf16[64,1536]{1,0:T(8,128)(2,1)S(1)}, bf16[64,1536]{1,0:T(8,128)(2,1)S(1)}, u32[]{:S(2)}, u32[]{:S(2)}) collective-permute-start(bf16[64,1536]{1,0:T(8,128)(2,1)S(1)} %fusion.1), channel_id=1, source_target_pairs={{0,4},{1,5},{2,30},{3,31},{4,8},{5,9},{6,2},{7,3},{8,12},{9,13},{1... | collective-permute-start | bytes 589832 | tf_op jit(solution)/shard_map/ppermute | solution.py:49
  127.8 28.3 %collective-permute-start.10 = (bf16[64,768]{1,0:T(8,128)(2,1)S(1)}, bf16[64,768]{1,0:T(8,128)(2,1)S(1)}, u32[]{:S(2)}, u32[]{:S(2)}) collective-permute-start(bf16[64,768]{1,0:T(8,128)(2,1)S(1)} %get-tuple-element.14), channel_id=1, source_target_pairs={{0,4},{1,5},{2,30},{3,31},{4,8},{5,9},{6,2},{7,3},{8,12},{9,13},{1... | collective-permute-start | bytes 294920 | tf_op jit(solution)/shard_map/ppermute | solution.py:49
  129.7 61.7 %collective-permute-start.17 = (bf16[64,768]{1,0:T(8,128)(2,1)S(1)}, bf16[64,768]{1,0:T(8,128)(2,1)S(1)}, u32[]{:S(2)}, u32[]{:S(2)}) collective-permute-start(bf16[64,768]{1,0:T(8,128)(2,1)S(1)} %get-tuple-element.10), channel_id=1, source_target_pairs={{0,1},{1,2},{2,3},{3,0},{4,5},{5,6},{6,7},{7,4},{8,9},{9,10},{10,1... | collective-permute-start | bytes 294920 | tf_op jit(solution)/shard_map/ppermute | solution.py:52
  132.2 59.2 %collective-permute-start.18 = (bf16[64,768]{1,0:T(8,128)(2,1)S(1)}, bf16[64,768]{1,0:T(8,128)(2,1)S(1)}, u32[]{:S(2)}, u32[]{:S(2)}) collective-permute-start(bf16[64,768]{1,0:T(8,128)(2,1)S(1)} %get-tuple-element.11), channel_id=1, source_target_pairs={{0,2},{1,3},{2,0},{3,1},{4,6},{5,7},{6,4},{7,5},{8,10},{9,11},{10,... | collective-permute-start | bytes 294920 | tf_op jit(solution)/shard_map/ppermute | solution.py:52
  144.6 46.8 %collective-permute-start.19 = (bf16[64,768]{1,0:T(8,128)(2,1)S(1)}, bf16[64,768]{1,0:T(8,128)(2,1)S(1)}, u32[]{:S(2)}, u32[]{:S(2)}) collective-permute-start(bf16[64,768]{1,0:T(8,128)(2,1)S(1)} %get-tuple-element.12), channel_id=1, source_target_pairs={{0,3},{1,0},{2,1},{3,2},{4,7},{5,4},{6,5},{7,6},{8,11},{9,8},{10,9... | collective-permute-start | bytes 294920 | tf_op jit(solution)/shard_map/ppermute | solution.py:52
  148.9 9.4 %collective-permute-start.11 = (bf16[64,768]{1,0:T(8,128)(2,1)S(1)}, bf16[64,768]{1,0:T(8,128)(2,1)S(1)}, u32[]{:S(2)}, u32[]{:S(2)}) collective-permute-start(bf16[64,768]{1,0:T(8,128)(2,1)S(1)} %get-tuple-element.14), channel_id=1, source_target_pairs={{0,28},{1,29},{2,6},{3,7},{4,0},{5,1},{6,10},{7,11},{8,4},{9,5},{1... | collective-permute-start | bytes 294920 | tf_op jit(solution)/shard_map/ppermute | solution.py:49
  156.1 12.7 %collective-permute-start.12 = (bf16[64,768]{1,0:T(8,128)(2,1)S(1)}, bf16[64,768]{1,0:T(8,128)(2,1)S(1)}, u32[]{:S(2)}, u32[]{:S(2)}) collective-permute-start(bf16[64,768]{1,0:T(8,128)(2,1)S(1)} %collective-permute-done.10), channel_id=1, source_target_pairs={{0,4},{1,5},{2,30},{3,31},{4,8},{5,9},{6,2},{7,3},{8,12},{9,13},{1... | collective-permute-start | bytes 294920 | tf_op jit(solution)/shard_map/ppermute | solution.py:49
  158.3 15.8 %collective-permute-start.13 = (bf16[64,768]{1,0:T(8,128)(2,1)S(1)}, bf16[64,768]{1,0:T(8,128)(2,1)S(1)}, u32[]{:S(2)}, u32[]{:S(2)}) collective-permute-start(bf16[64,768]{1,0:T(8,128)(2,1)S(1)} %collective-permute-done.11), channel_id=1, source_target_pairs={{0,28},{1,29},{2,6},{3,7},{4,0},{5,1},{6,10},{7,11},{8,4},{9,5},{1... | collective-permute-start | bytes 294920 | tf_op jit(solution)/shard_map/ppermute | solution.py:49
  168.9 13.3 %collective-permute-start.14 = (bf16[64,768]{1,0:T(8,128)(2,1)S(1)}, bf16[64,768]{1,0:T(8,128)(2,1)S(1)}, u32[]{:S(2)}, u32[]{:S(2)}) collective-permute-start(bf16[64,768]{1,0:T(8,128)(2,1)S(1)} %collective-permute-done.12), channel_id=1, source_target_pairs={{0,4},{1,5},{2,30},{3,31},{4,8},{5,9},{6,2},{7,3},{8,12},{9,13},{1... | collective-permute-start | bytes 294920 | tf_op jit(solution)/shard_map/ppermute | solution.py:49
  174.1 12.0 %collective-permute-start.15 = (bf16[64,768]{1,0:T(8,128)(2,1)S(1)}, bf16[64,768]{1,0:T(8,128)(2,1)S(1)}, u32[]{:S(2)}, u32[]{:S(2)}) collective-permute-start(bf16[64,768]{1,0:T(8,128)(2,1)S(1)} %collective-permute-done.13), channel_id=1, source_target_pairs={{0,28},{1,29},{2,6},{3,7},{4,0},{5,1},{6,10},{7,11},{8,4},{9,5},{1... | collective-permute-start | bytes 294920 | tf_op jit(solution)/shard_map/ppermute | solution.py:49
  182.1 9.3 %collective-permute-start.16 = (bf16[64,768]{1,0:T(8,128)(2,1)S(1)}, bf16[64,768]{1,0:T(8,128)(2,1)S(1)}, u32[]{:S(2)}, u32[]{:S(2)}) collective-permute-start(bf16[64,768]{1,0:T(8,128)(2,1)S(1)} %collective-permute-done.14), channel_id=1, source_target_pairs={{0,4},{1,5},{2,30},{3,31},{4,8},{5,9},{6,2},{7,3},{8,12},{9,13},{1... | collective-permute-start | bytes 294920 | tf_op jit(solution)/shard_map/ppermute | solution.py:49
  192.7 18.4 %all-to-all-start.2 = ((f32[32,16,256]{2,1,0:T(8,128)}), f32[32,16,256]{2,1,0:T(8,128)S(1)}, u32[]{:S(2)}, u32[]{:S(2)}) async-start(f32[32,16,256]{2,1,0:T(8,128)} %fusion.6), calls=%async_computation.2 | async-start | bytes 1048576 | tf_op jit(solution)/shard_map/all_to_all | solution.py:11
  (2 other events, 17.7 us)

commit v7 on v6

--- a/solution.py
+++ b/solution.py
@@ -63,14 +63,12 @@
         e = lax.rem(me + k, local)
         g = lax.dynamic_index_in_dim(gate_weight, e, 0, keepdims=False)
         u = lax.dynamic_index_in_dim(up_weight, e, 0, keepdims=False)
-        return jnp.concatenate([g, u], axis=1)
+        d = lax.dynamic_index_in_dim(down_weight, e, 0, keepdims=False)
+        return jnp.concatenate([g, u, d], axis=1)
 
-    def down_block(k):
-        return lax.dynamic_index_in_dim(
-            down_weight, lax.rem(me + k, local), 0, keepdims=False
-        )
-
-    w_in = [in_block(0)] + [beside(in_block(k), k) for k in range(1, local)]
+    blocks = [in_block(0)] + [beside(in_block(k), k) for k in range(1, local)]
+    w_in = jnp.concatenate([b[:, : 2 * units] for b in blocks], axis=0)
+    w_down = jnp.concatenate([b[:, 2 * units :] for b in blocks], axis=0)
 
     rt = routing.T
     expert = jnp.arange(ep, dtype=jnp.int32) * local + me
@@ -87,14 +85,8 @@
     mix = jnp.where(pick, factor[:, None, :], 0.0).reshape(slots, rows)
 
     outgoing = rows_dot(place, xt).astype(BF16)
-    sent = [down_block(k) for k in range(1, local)]
-    outgoing, sent = lax.optimization_barrier((outgoing, sent))
     x = exchange(outgoing.reshape(ep, capacity, -1), "ep")
-    w_down = [down_block(0)] + [beside(b, k + 1) for k, b in enumerate(sent)]
-    w_down = jnp.concatenate(w_down, axis=0)
-
     x = x.reshape(ring, chunk, -1)
-    w_in = jnp.concatenate(w_in, axis=0)
 
     def term(k):
         rows_of = lax.dynamic_index_in_dim(x, chunk_at[k % ring], 0, keepdims=False)
@@ -116,7 +108,7 @@
         return lax.dynamic_update_index_in_dim(hidden, arrived, chunk_at[k % ring], 0)
 
     ahead = behind = own
-    hidden = put(hidden, own, 0)
+    hidden = put(hidden, lax.optimization_barrier(own), 0)
     for k in range(1, steps + 1):
         ahead = ship(ahead, 1)
         hidden = put(hidden, ahead, -k)

time: 229 us -> 218 us (0.952)
  starting transfers between devices: 144 us -> 137 us
  blocking collectives: 15.5 us -> 10.3 us
    ppermute x6 -> x3, starting transfers between devices: 29.7 us -> 10.5 us  [beside(): lax.ppermute(x, 'tp', [(g[i], g[(i + k) % local]) for g in near for i in...]
    ppermute x14, starting transfers between devices: 85.3 us -> 92.9 us  [ship(): return lax.ppermute(x, 'tp', pairs)]
    all_to_all x1, blocking collectives: 15.5 us -> 10.3 us  [exchange(): lax.all_to_all(x, axis, split_axis=0, concat_axis=0, tiled=True, axis_ind...]
    all_to_all x3, starting transfers between devices: 29 us -> 33.6 us  [exchange(): lax.all_to_all(x, axis, split_axis=0, concat_axis=0, tiled=True, axis_ind...]
  transfers between devices with their start and end apart: 23 -> 20, of which waited for: 11 -> 10; matrix products, arithmetic and copies ran while one was open for 2% -> 2% of each run, Pallas kernels for 0% -> 0%
where the time goes in v7:
time: 218 us; the launch traced here: 216 us
  starting transfers between devices  137 us (63%)
  waiting for transfers between devices  59.2 us (27%)
  blocking collectives  10.3 us (5%)
  matrix products  4.9 us (2%)
  local copies, waits for them, and re-layouts  3.13 us (1%)
    ppermute x14, starting transfers between devices, ship(): return lax.ppermute(x, 'tp', pairs)  92.9 us
    ppermute x14, waiting for transfers between devices, ship(): return lax.ppermute(x, 'tp', pairs)  39.3 us
    all_to_all x3, starting transfers between devices, exchange(): lax.all_to_all(x, axis, split_axis=0, concat_axis=0, tiled=True, axis_ind...  33.6 us
    all_to_all x3, waiting for transfers between devices, exchange(): lax.all_to_all(x, axis, split_axis=0, concat_axis=0, tiled=True, axis_ind...  19.9 us
    ppermute x3, starting transfers between devices, beside(): lax.ppermute(x, 'tp', [(g[i], g[(i + k) % local]) for g in near for i in...  10.5 us
    all_to_all x1, blocking collectives, exchange(): lax.all_to_all(x, axis, split_axis=0, concat_axis=0, tiled=True, axis_ind...  10.3 us
  transfers between devices with their start and end apart: 20, of which 10 were waited for; matrix products, arithmetic and copies ran while one was open for 2% of the time, Pallas kernels for 0%

profile of v7, /device:TPU:1, one launch (start us, length us, event | category | flops | bytes accessed | tf_op | source)
XLA Modules:
  0.0 216.5 jit_solution(1135699568187805727)
XLA Ops:
  1.4 6.4 %all-to-all-start = ((bf16[4,64,128]{2,1,0:T(8,128)(2,1)}), bf16[4,64,128]{2,1,0:T(8,128)(2,1)S(1)}, u32[]{:S(2)}, u32[]{:S(2)}) async-start(bf16[4,64,128]{2,1,0:T(8,128)(2,1)} %broadcast_in_dim.68), calls=%async_computation | async-start | bytes 131072 | tf_op jit(solution)/shard_map/all_to_all | solution.py:11
  9.1 3.4 %collective-permute-start = (bf16[64,2304]{1,0:T(8,128)(2,1)S(1)}, bf16[64,2304]{1,0:T(8,128)(2,1)S(1)}, u32[]{:S(2)}, u32[]{:S(2)}) collective-permute-start(bf16[64,2304]{1,0:T(8,128)(2,1)S(1)} %pad_maximum_fusion.1), channel_id=1, source_target_pairs={{0,1},{1,2},{2,3},{3,0},{4,5},{5,6},{6,7},{7,4},{8,9},{9,10},{10,1... | collective-permute-start | bytes 884744 | tf_op jit(solution)/shard_map/ppermute | solution.py:52
  12.5 4.0 %collective-permute-start.1 = (bf16[64,2304]{1,0:T(8,128)(2,1)S(1)}, bf16[64,2304]{1,0:T(8,128)(2,1)S(1)}, u32[]{:S(2)}, u32[]{:S(2)}) collective-permute-start(bf16[64,2304]{1,0:T(8,128)(2,1)S(1)} %pad_maximum_fusion.2), channel_id=1, source_target_pairs={{0,2},{1,3},{2,0},{3,1},{4,6},{5,7},{6,4},{7,5},{8,10},{9,11},{10,... | collective-permute-start | bytes 884744 | tf_op jit(solution)/shard_map/ppermute | solution.py:52
  21.1 15.6 %all-to-all-start.1 = ((bf16[32,16,256]{2,1,0:T(8,128)(2,1)}), bf16[32,16,256]{2,1,0:T(8,128)(2,1)S(1)}, u32[]{:S(2)}, u32[]{:S(2)}) async-start(bf16[32,16,256]{2,1,0:T(8,128)(2,1)} %bitcast.8), calls=%async_computation.1 | async-start | bytes 524288 | tf_op jit(solution)/shard_map/all_to_all | solution.py:11
  37.0 8.7 %all-to-all-done.1 = bf16[32,16,256]{2,1,0:T(8,128)(2,1)S(1)} async-done(((bf16[32,16,256]{2,1,0:T(8,128)(2,1)}), bf16[32,16,256]{2,1,0:T(8,128)(2,1)S(1)}, u32[]{:S(2)}, u32[]{:S(2)}) %all-to-all-start.1) | async-done | bytes 262176 | tf_op jit(solution)/shard_map/all_to_all | solution.py:11
  48.5 10.2 %collective-permute-start.7 = (bf16[64,1536]{1,0:T(8,128)(2,1)S(1)}, bf16[64,1536]{1,0:T(8,128)(2,1)S(1)}, u32[]{:S(2)}, u32[]{:S(2)}) collective-permute-start(bf16[64,1536]{1,0:T(8,128)(2,1)S(1)} %convolution_convert_fusion), channel_id=1, source_target_pairs={{0,28},{1,29},{2,6},{3,7},{4,0},{5,1},{6,10},{7,11},{8,4},{9,5},{1... | collective-permute-start | bytes 589832 | tf_op jit(solution)/shard_map/ppermute | solution.py:49
  61.9 3.6 %collective-permute-start.4 = (bf16[64,1536]{1,0:T(8,128)(2,1)S(1)}, bf16[64,1536]{1,0:T(8,128)(2,1)S(1)}, u32[]{:S(2)}, u32[]{:S(2)}) collective-permute-start(bf16[64,1536]{1,0:T(8,128)(2,1)S(1)} %fusion.3), channel_id=1, source_target_pairs={{0,4},{1,5},{2,30},{3,31},{4,8},{5,9},{6,2},{7,3},{8,12},{9,13},{1... | collective-permute-start | bytes 589832 | tf_op jit(solution)/shard_map/ppermute | solution.py:49
  65.5 5.4 %collective-permute-done.7 = bf16[64,1536]{1,0:T(8,128)(2,1)S(1)} collective-permute-done((bf16[64,1536]{1,0:T(8,128)(2,1)S(1)}, bf16[64,1536]{1,0:T(8,128)(2,1)S(1)}, u32[]{:S(2)}, u32[]{:S(2)}) %collective-permute-start.7) | collective-permute-done | bytes 196640 | tf_op jit(solution)/shard_map/ppermute | solution.py:49
  71.2 7.1 %collective-permute-start.8 = (bf16[64,1536]{1,0:T(8,128)(2,1)S(1)}, bf16[64,1536]{1,0:T(8,128)(2,1)S(1)}, u32[]{:S(2)}, u32[]{:S(2)}) collective-permute-start(bf16[64,1536]{1,0:T(8,128)(2,1)S(1)} %fusion.5), channel_id=1, source_target_pairs={{0,28},{1,29},{2,6},{3,7},{4,0},{5,1},{6,10},{7,11},{8,4},{9,5},{1... | collective-permute-start | bytes 589832 | tf_op jit(solution)/shard_map/ppermute | solution.py:49
  78.3 5.6 %collective-permute-done.4 = bf16[64,1536]{1,0:T(8,128)(2,1)S(1)} collective-permute-done((bf16[64,1536]{1,0:T(8,128)(2,1)S(1)}, bf16[64,1536]{1,0:T(8,128)(2,1)S(1)}, u32[]{:S(2)}, u32[]{:S(2)}) %collective-permute-start.4) | collective-permute-done | bytes 196640 | tf_op jit(solution)/shard_map/ppermute | solution.py:49
  84.2 17.8 %collective-permute-start.5 = (bf16[64,1536]{1,0:T(8,128)(2,1)S(1)}, bf16[64,1536]{1,0:T(8,128)(2,1)S(1)}, u32[]{:S(2)}, u32[]{:S(2)}) collective-permute-start(bf16[64,1536]{1,0:T(8,128)(2,1)S(1)} %fusion.2), channel_id=1, source_target_pairs={{0,4},{1,5},{2,30},{3,31},{4,8},{5,9},{6,2},{7,3},{8,12},{9,13},{1... | collective-permute-start | bytes 589832 | tf_op jit(solution)/shard_map/ppermute | solution.py:49
  104.2 14.5 %collective-permute-done.5 = bf16[64,1536]{1,0:T(8,128)(2,1)S(1)} collective-permute-done((bf16[64,1536]{1,0:T(8,128)(2,1)S(1)}, bf16[64,1536]{1,0:T(8,128)(2,1)S(1)}, u32[]{:S(2)}, u32[]{:S(2)}) %collective-permute-start.5) | collective-permute-done | bytes 196640 | tf_op jit(solution)/shard_map/ppermute | solution.py:49
  119.0 12.3 %collective-permute-start.6 = (bf16[64,1536]{1,0:T(8,128)(2,1)S(1)}, bf16[64,1536]{1,0:T(8,128)(2,1)S(1)}, u32[]{:S(2)}, u32[]{:S(2)}) collective-permute-start(bf16[64,1536]{1,0:T(8,128)(2,1)S(1)} %fusion.1), channel_id=1, source_target_pairs={{0,4},{1,5},{2,30},{3,31},{4,8},{5,9},{6,2},{7,3},{8,12},{9,13},{1... | collective-permute-start | bytes 589832 | tf_op jit(solution)/shard_map/ppermute | solution.py:49
  131.3 3.4 %collective-permute-done.6 = bf16[64,1536]{1,0:T(8,128)(2,1)S(1)} collective-permute-done((bf16[64,1536]{1,0:T(8,128)(2,1)S(1)}, bf16[64,1536]{1,0:T(8,128)(2,1)S(1)}, u32[]{:S(2)}, u32[]{:S(2)}) %collective-permute-start.6) | collective-permute-done | bytes 196640 | tf_op jit(solution)/shard_map/ppermute | solution.py:49
  135.1 8.0 %collective-permute-start.10 = (bf16[64,768]{1,0:T(8,128)(2,1)S(1)}, bf16[64,768]{1,0:T(8,128)(2,1)S(1)}, u32[]{:S(2)}, u32[]{:S(2)}) collective-permute-start(bf16[64,768]{1,0:T(8,128)(2,1)S(1)} %fusion.14), channel_id=1, source_target_pairs={{0,4},{1,5},{2,30},{3,31},{4,8},{5,9},{6,2},{7,3},{8,12},{9,13},{1... | collective-permute-start | bytes 294920 | tf_op jit(solution)/shard_map/ppermute | solution.py:49
  147.1 6.2 %collective-permute-start.12 = (bf16[64,768]{1,0:T(8,128)(2,1)S(1)}, bf16[64,768]{1,0:T(8,128)(2,1)S(1)}, u32[]{:S(2)}, u32[]{:S(2)}) collective-permute-start(bf16[64,768]{1,0:T(8,128)(2,1)S(1)} %collective-permute-done.10), channel_id=1, source_target_pairs={{0,4},{1,5},{2,30},{3,31},{4,8},{5,9},{6,2},{7,3},{8,12},{9,13},{1... | collective-permute-start | bytes 294920 | tf_op jit(solution)/shard_map/ppermute | solution.py:49
  153.7 4.3 %collective-permute-start.13 = (bf16[64,768]{1,0:T(8,128)(2,1)S(1)}, bf16[64,768]{1,0:T(8,128)(2,1)S(1)}, u32[]{:S(2)}, u32[]{:S(2)}) collective-permute-start(bf16[64,768]{1,0:T(8,128)(2,1)S(1)} %collective-permute-done.11), channel_id=1, source_target_pairs={{0,28},{1,29},{2,6},{3,7},{4,0},{5,1},{6,10},{7,11},{8,4},{9,5},{1... | collective-permute-start | bytes 294920 | tf_op jit(solution)/shard_map/ppermute | solution.py:49
  158.1 6.2 %collective-permute-start.14 = (bf16[64,768]{1,0:T(8,128)(2,1)S(1)}, bf16[64,768]{1,0:T(8,128)(2,1)S(1)}, u32[]{:S(2)}, u32[]{:S(2)}) collective-permute-start(bf16[64,768]{1,0:T(8,128)(2,1)S(1)} %collective-permute-done.12), channel_id=1, source_target_pairs={{0,4},{1,5},{2,30},{3,31},{4,8},{5,9},{6,2},{7,3},{8,12},{9,13},{1... | collective-permute-start | bytes 294920 | tf_op jit(solution)/shard_map/ppermute | solution.py:49
  164.3 5.6 %collective-permute-start.15 = (bf16[64,768]{1,0:T(8,128)(2,1)S(1)}, bf16[64,768]{1,0:T(8,128)(2,1)S(1)}, u32[]{:S(2)}, u32[]{:S(2)}) collective-permute-start(bf16[64,768]{1,0:T(8,128)(2,1)S(1)} %collective-permute-done.13), channel_id=1, source_target_pairs={{0,28},{1,29},{2,6},{3,7},{4,0},{5,1},{6,10},{7,11},{8,4},{9,5},{1... | collective-permute-start | bytes 294920 | tf_op jit(solution)/shard_map/ppermute | solution.py:49
  169.9 5.3 %collective-permute-start.16 = (bf16[64,768]{1,0:T(8,128)(2,1)S(1)}, bf16[64,768]{1,0:T(8,128)(2,1)S(1)}, u32[]{:S(2)}, u32[]{:S(2)}) collective-permute-start(bf16[64,768]{1,0:T(8,128)(2,1)S(1)} %collective-permute-done.14), channel_id=1, source_target_pairs={{0,4},{1,5},{2,30},{3,31},{4,8},{5,9},{6,2},{7,3},{8,12},{9,13},{1... | collective-permute-start | bytes 294920 | tf_op jit(solution)/shard_map/ppermute | solution.py:49
  175.3 5.1 %collective-permute-done.16 = bf16[64,768]{1,0:T(8,128)(2,1)S(1)} collective-permute-done((bf16[64,768]{1,0:T(8,128)(2,1)S(1)}, bf16[64,768]{1,0:T(8,128)(2,1)S(1)}, u32[]{:S(2)}, u32[]{:S(2)}) %collective-permute-start.16) | collective-permute-done | bytes 98336 | tf_op jit(solution)/shard_map/ppermute | solution.py:49
  181.7 11.6 %all-to-all-start.2 = ((f32[32,16,256]{2,1,0:T(8,128)}), f32[32,16,256]{2,1,0:T(8,128)S(1)}, u32[]{:S(2)}, u32[]{:S(2)}) async-start(f32[32,16,256]{2,1,0:T(8,128)} %fusion.6), calls=%async_computation.2 | async-start | bytes 1048576 | tf_op jit(solution)/shard_map/all_to_all | solution.py:11
  193.5 11.2 %all-to-all-done.2 = f32[32,16,256]{2,1,0:T(8,128)S(1)} async-done(((f32[32,16,256]{2,1,0:T(8,128)}), f32[32,16,256]{2,1,0:T(8,128)S(1)}, u32[]{:S(2)}, u32[]{:S(2)}) %all-to-all-start.2) | async-done | bytes 524320 | tf_op jit(solution)/shard_map/all_to_all | solution.py:11
  205.6 10.3 %all_to_all.20 = f32[4,64,128]{2,1,0:T(8,128)S(1)} all-to-all(f32[4,64,128]{2,1,0:T(8,128)S(1)} %pad_maximum_fusion.4), channel_id=1, replica_groups={{0,1,2,3},{4,5,6,7},{8,9,10,11},{12,13,14,15},{16,17,18,19},{20,21,22,2..., dimensions={0} | all-to-all | bytes 262144 | tf_op jit(solution)/shard_map/all_to_all | solution.py:11
  (83 shorter events, 23.8 us)
Async XLA Ops:
  1.4 18.7 %all-to-all-start = ((bf16[4,64,128]{2,1,0:T(8,128)(2,1)}), bf16[4,64,128]{2,1,0:T(8,128)(2,1)S(1)}, u32[]{:S(2)}, u32[]{:S(2)}) async-start(bf16[4,64,128]{2,1,0:T(8,128)(2,1)} %broadcast_in_dim.68), calls=%async_computation | async-start | bytes 131072 | tf_op jit(solution)/shard_map/all_to_all | solution.py:11
  9.1 27.7 %collective-permute-start = (bf16[64,2304]{1,0:T(8,128)(2,1)S(1)}, bf16[64,2304]{1,0:T(8,128)(2,1)S(1)}, u32[]{:S(2)}, u32[]{:S(2)}) collective-permute-start(bf16[64,2304]{1,0:T(8,128)(2,1)S(1)} %pad_maximum_fusion.1), channel_id=1, source_target_pairs={{0,1},{1,2},{2,3},{3,0},{4,5},{5,6},{6,7},{7,4},{8,9},{9,10},{10,1... | collective-permute-start | bytes 884744 | tf_op jit(solution)/shard_map/ppermute | solution.py:52
  12.5 24.3 %collective-permute-start.1 = (bf16[64,2304]{1,0:T(8,128)(2,1)S(1)}, bf16[64,2304]{1,0:T(8,128)(2,1)S(1)}, u32[]{:S(2)}, u32[]{:S(2)}) collective-permute-start(bf16[64,2304]{1,0:T(8,128)(2,1)S(1)} %pad_maximum_fusion.2), channel_id=1, source_target_pairs={{0,2},{1,3},{2,0},{3,1},{4,6},{5,7},{6,4},{7,5},{8,10},{9,11},{10,... | collective-permute-start | bytes 884744 | tf_op jit(solution)/shard_map/ppermute | solution.py:52
  16.5 20.4 %collective-permute-start.2 = (bf16[64,2304]{1,0:T(8,128)(2,1)S(1)}, bf16[64,2304]{1,0:T(8,128)(2,1)S(1)}, u32[]{:S(2)}, u32[]{:S(2)}) collective-permute-start(bf16[64,2304]{1,0:T(8,128)(2,1)S(1)} %pad_maximum_fusion.3), channel_id=1, source_target_pairs={{0,3},{1,0},{2,1},{3,2},{4,7},{5,4},{6,5},{7,6},{8,11},{9,8},{10,9... | collective-permute-start | bytes 884744 | tf_op jit(solution)/shard_map/ppermute | solution.py:52
  21.1 24.6 %all-to-all-start.1 = ((bf16[32,16,256]{2,1,0:T(8,128)(2,1)}), bf16[32,16,256]{2,1,0:T(8,128)(2,1)S(1)}, u32[]{:S(2)}, u32[]{:S(2)}) async-start(bf16[32,16,256]{2,1,0:T(8,128)(2,1)} %bitcast.8), calls=%async_computation.1 | async-start | bytes 524288 | tf_op jit(solution)/shard_map/all_to_all | solution.py:11
  36.8 94.5 %copy-start.2 = (bf16[64,2304]{1,0:T(8,128)(2,1)}, bf16[64,2304]{1,0:T(8,128)(2,1)S(1)}, u32[]{:S(2)}) copy-start(bf16[64,2304]{1,0:T(8,128)(2,1)S(1)} %collective-permute-done) | copy-start | bytes 884740
  36.8 94.5 %copy-start.3 = (bf16[64,2304]{1,0:T(8,128)(2,1)}, bf16[64,2304]{1,0:T(8,128)(2,1)S(1)}, u32[]{:S(2)}) copy-start(bf16[64,2304]{1,0:T(8,128)(2,1)S(1)} %collective-permute-done.1) | copy-start | bytes 884740
  36.9 94.4 %copy-start.4 = (bf16[64,2304]{1,0:T(8,128)(2,1)}, bf16[64,2304]{1,0:T(8,128)(2,1)S(1)}, u32[]{:S(2)}) copy-start(bf16[64,2304]{1,0:T(8,128)(2,1)S(1)} %collective-permute-done.2) | copy-start | bytes 884740
  45.9 15.7 %collective-permute-start.3 = (bf16[64,1536]{1,0:T(8,128)(2,1)S(1)}, bf16[64,1536]{1,0:T(8,128)(2,1)S(1)}, u32[]{:S(2)}, u32[]{:S(2)}) collective-permute-start(bf16[64,1536]{1,0:T(8,128)(2,1)S(1)} %convolution_convert_fusion.1), channel_id=1, source_target_pairs={{0,4},{1,5},{2,30},{3,31},{4,8},{5,9},{6,2},{7,3},{8,12},{9,13},{1... | collective-permute-start | bytes 589832 | tf_op jit(solution)/shard_map/ppermute | solution.py:49
  48.5 22.4 %collective-permute-start.7 = (bf16[64,1536]{1,0:T(8,128)(2,1)S(1)}, bf16[64,1536]{1,0:T(8,128)(2,1)S(1)}, u32[]{:S(2)}, u32[]{:S(2)}) collective-permute-start(bf16[64,1536]{1,0:T(8,128)(2,1)S(1)} %convolution_convert_fusion), channel_id=1, source_target_pairs={{0,28},{1,29},{2,6},{3,7},{4,0},{5,1},{6,10},{7,11},{8,4},{9,5},{1... | collective-permute-start | bytes 589832 | tf_op jit(solution)/shard_map/ppermute | solution.py:49
  61.9 22.0 %collective-permute-start.4 = (bf16[64,1536]{1,0:T(8,128)(2,1)S(1)}, bf16[64,1536]{1,0:T(8,128)(2,1)S(1)}, u32[]{:S(2)}, u32[]{:S(2)}) collective-permute-start(bf16[64,1536]{1,0:T(8,128)(2,1)S(1)} %fusion.3), channel_id=1, source_target_pairs={{0,4},{1,5},{2,30},{3,31},{4,8},{5,9},{6,2},{7,3},{8,12},{9,13},{1... | collective-permute-start | bytes 589832 | tf_op jit(solution)/shard_map/ppermute | solution.py:49
  71.2 30.9 %collective-permute-start.8 = (bf16[64,1536]{1,0:T(8,128)(2,1)S(1)}, bf16[64,1536]{1,0:T(8,128)(2,1)S(1)}, u32[]{:S(2)}, u32[]{:S(2)}) collective-permute-start(bf16[64,1536]{1,0:T(8,128)(2,1)S(1)} %fusion.5), channel_id=1, source_target_pairs={{0,28},{1,29},{2,6},{3,7},{4,0},{5,1},{6,10},{7,11},{8,4},{9,5},{1... | collective-permute-start | bytes 589832 | tf_op jit(solution)/shard_map/ppermute | solution.py:49
  84.2 34.5 %collective-permute-start.5 = (bf16[64,1536]{1,0:T(8,128)(2,1)S(1)}, bf16[64,1536]{1,0:T(8,128)(2,1)S(1)}, u32[]{:S(2)}, u32[]{:S(2)}) collective-permute-start(bf16[64,1536]{1,0:T(8,128)(2,1)S(1)} %fusion.2), channel_id=1, source_target_pairs={{0,4},{1,5},{2,30},{3,31},{4,8},{5,9},{6,2},{7,3},{8,12},{9,13},{1... | collective-permute-start | bytes 589832 | tf_op jit(solution)/shard_map/ppermute | solution.py:49
  102.3 29.0 %collective-permute-start.9 = (bf16[64,1536]{1,0:T(8,128)(2,1)S(1)}, bf16[64,1536]{1,0:T(8,128)(2,1)S(1)}, u32[]{:S(2)}, u32[]{:S(2)}) collective-permute-start(bf16[64,1536]{1,0:T(8,128)(2,1)S(1)} %fusion.4), channel_id=1, source_target_pairs={{0,28},{1,29},{2,6},{3,7},{4,0},{5,1},{6,10},{7,11},{8,4},{9,5},{1... | collective-permute-start | bytes 589832 | tf_op jit(solution)/shard_map/ppermute | solution.py:49
  119.0 15.8 %collective-permute-start.6 = (bf16[64,1536]{1,0:T(8,128)(2,1)S(1)}, bf16[64,1536]{1,0:T(8,128)(2,1)S(1)}, u32[]{:S(2)}, u32[]{:S(2)}) collective-permute-start(bf16[64,1536]{1,0:T(8,128)(2,1)S(1)} %fusion.1), channel_id=1, source_target_pairs={{0,4},{1,5},{2,30},{3,31},{4,8},{5,9},{6,2},{7,3},{8,12},{9,13},{1... | collective-permute-start | bytes 589832 | tf_op jit(solution)/shard_map/ppermute | solution.py:49
  135.1 12.0 %collective-permute-start.10 = (bf16[64,768]{1,0:T(8,128)(2,1)S(1)}, bf16[64,768]{1,0:T(8,128)(2,1)S(1)}, u32[]{:S(2)}, u32[]{:S(2)}) collective-permute-start(bf16[64,768]{1,0:T(8,128)(2,1)S(1)} %fusion.14), channel_id=1, source_target_pairs={{0,4},{1,5},{2,30},{3,31},{4,8},{5,9},{6,2},{7,3},{8,12},{9,13},{1... | collective-permute-start | bytes 294920 | tf_op jit(solution)/shard_map/ppermute | solution.py:49
  143.1 10.6 %collective-permute-start.11 = (bf16[64,768]{1,0:T(8,128)(2,1)S(1)}, bf16[64,768]{1,0:T(8,128)(2,1)S(1)}, u32[]{:S(2)}, u32[]{:S(2)}) collective-permute-start(bf16[64,768]{1,0:T(8,128)(2,1)S(1)} %fusion.14), channel_id=1, source_target_pairs={{0,28},{1,29},{2,6},{3,7},{4,0},{5,1},{6,10},{7,11},{8,4},{9,5},{1... | collective-permute-start | bytes 294920 | tf_op jit(solution)/shard_map/ppermute | solution.py:49
  145.1 35.4 %slice-start = ((bf16[64,2304]{1,0:T(8,128)(2,1)}), bf16[64,768]{1,0:T(8,128)(2,1)S(1)}, s32[]{:S(2)}) async-start(bf16[64,2304]{1,0:T(8,128)(2,1)} %copy-done.2), calls=%async_computation.4 | async-start | bytes 196608 | tf_op jit(solution)/shard_map/slice | solution.py:71
  147.1 11.0 %collective-permute-start.12 = (bf16[64,768]{1,0:T(8,128)(2,1)S(1)}, bf16[64,768]{1,0:T(8,128)(2,1)S(1)}, u32[]{:S(2)}, u32[]{:S(2)}) collective-permute-start(bf16[64,768]{1,0:T(8,128)(2,1)S(1)} %collective-permute-done.10), channel_id=1, source_target_pairs={{0,4},{1,5},{2,30},{3,31},{4,8},{5,9},{6,2},{7,3},{8,12},{9,13},{1... | collective-permute-start | bytes 294920 | tf_op jit(solution)/shard_map/ppermute | solution.py:49
  153.7 10.6 %collective-permute-start.13 = (bf16[64,768]{1,0:T(8,128)(2,1)S(1)}, bf16[64,768]{1,0:T(8,128)(2,1)S(1)}, u32[]{:S(2)}, u32[]{:S(2)}) collective-permute-start(bf16[64,768]{1,0:T(8,128)(2,1)S(1)} %collective-permute-done.11), channel_id=1, source_target_pairs={{0,28},{1,29},{2,6},{3,7},{4,0},{5,1},{6,10},{7,11},{8,4},{9,5},{1... | collective-permute-start | bytes 294920 | tf_op jit(solution)/shard_map/ppermute | solution.py:49
  158.1 11.8 %collective-permute-start.14 = (bf16[64,768]{1,0:T(8,128)(2,1)S(1)}, bf16[64,768]{1,0:T(8,128)(2,1)S(1)}, u32[]{:S(2)}, u32[]{:S(2)}) collective-permute-start(bf16[64,768]{1,0:T(8,128)(2,1)S(1)} %collective-permute-done.12), channel_id=1, source_target_pairs={{0,4},{1,5},{2,30},{3,31},{4,8},{5,9},{6,2},{7,3},{8,12},{9,13},{1... | collective-permute-start | bytes 294920 | tf_op jit(solution)/shard_map/ppermute | solution.py:49
  164.3 11.0 %collective-permute-start.15 = (bf16[64,768]{1,0:T(8,128)(2,1)S(1)}, bf16[64,768]{1,0:T(8,128)(2,1)S(1)}, u32[]{:S(2)}, u32[]{:S(2)}) collective-permute-start(bf16[64,768]{1,0:T(8,128)(2,1)S(1)} %collective-permute-done.13), channel_id=1, source_target_pairs={{0,28},{1,29},{2,6},{3,7},{4,0},{5,1},{6,10},{7,11},{8,4},{9,5},{1... | collective-permute-start | bytes 294920 | tf_op jit(solution)/shard_map/ppermute | solution.py:49
  169.9 10.5 %collective-permute-start.16 = (bf16[64,768]{1,0:T(8,128)(2,1)S(1)}, bf16[64,768]{1,0:T(8,128)(2,1)S(1)}, u32[]{:S(2)}, u32[]{:S(2)}) collective-permute-start(bf16[64,768]{1,0:T(8,128)(2,1)S(1)} %collective-permute-done.14), channel_id=1, source_target_pairs={{0,4},{1,5},{2,30},{3,31},{4,8},{5,9},{6,2},{7,3},{8,12},{9,13},{1... | collective-permute-start | bytes 294920 | tf_op jit(solution)/shard_map/ppermute | solution.py:49
  181.7 23.0 %all-to-all-start.2 = ((f32[32,16,256]{2,1,0:T(8,128)}), f32[32,16,256]{2,1,0:T(8,128)S(1)}, u32[]{:S(2)}, u32[]{:S(2)}) async-start(f32[32,16,256]{2,1,0:T(8,128)} %fusion.6), calls=%async_computation.2 | async-start | bytes 1048576 | tf_op jit(solution)/shard_map/all_to_all | solution.py:11
  (6 other events, 110.8 us)

commit v8 on v7

--- a/solution.py
+++ b/solution.py
@@ -94,12 +94,18 @@
 
     steps = ring // 2
     ahead = ship(term(steps).astype(BF16), 1)
-    behind = ship(term(1 - steps).astype(BF16), -1)
+    early = [3, -2, 2, -1, 1]
+    made = [term(k) for k in early]
+    first = term(1 - steps).astype(BF16)
+    first, made = lax.optimization_barrier((first, made))
+    made = dict(zip(early, made))
+    made[0] = term(0)
+    behind = ship(first, -1)
     for k in range(steps - 1, 0, -1):
-        ahead = ship((term(k) + ahead.astype(F32)).astype(BF16), 1)
+        ahead = ship((made[k] + ahead.astype(F32)).astype(BF16), 1)
         if k > 1:
-            behind = ship((term(1 - k) + behind.astype(F32)).astype(BF16), -1)
-    acts = term(0) + ahead.astype(F32) + behind.astype(F32)
+            behind = ship((made[1 - k] + behind.astype(F32)).astype(BF16), -1)
+    acts = made[0] + ahead.astype(F32) + behind.astype(F32)
     own = (jax.nn.silu(acts[:, :units]) * acts[:, units:]).astype(BF16)
 
     hidden = jnp.zeros((ring, chunk, units), BF16)

time: 218 us -> 216 us (level)
  waiting for transfers between devices: 59.2 us -> 72.8 us
  starting transfers between devices: 137 us -> 125 us
  blocking collectives: 10.3 us -> 7.46 us
    ppermute x14, waiting for transfers between devices: 39.3 us -> 52.9 us  [ship(): return lax.ppermute(x, 'tp', pairs)]
    ppermute x14, starting transfers between devices: 92.9 us -> 81.1 us  [ship(): return lax.ppermute(x, 'tp', pairs)]
    ppermute x3, waiting for transfers between devices: 0.01 us -> 3.95 us  [beside(): lax.ppermute(x, 'tp', [(g[i], g[(i + k) % local]) for g in near for i in...]
    all_to_all x3, waiting for transfers between devices: 19.9 us -> 16 us  [exchange(): lax.all_to_all(x, axis, split_axis=0, concat_axis=0, tiled=True, axis_ind...]
    all_to_all x1, blocking collectives: 10.3 us -> 7.46 us  [exchange(): lax.all_to_all(x, axis, split_axis=0, concat_axis=0, tiled=True, axis_ind...]
  transfers between devices with their start and end apart: 20 -> 20, of which waited for: 10 -> 12; matrix products, arithmetic and copies ran while one was open for 2% -> 2% of each run, Pallas kernels for 0% -> 0%
where the time goes in v8:
time: 216 us; the launch traced here: 215 us
  starting transfers between devices  125 us (58%)
  waiting for transfers between devices  72.8 us (34%)
  blocking collectives  7.46 us (3%)
  matrix products  4.92 us (2%)
  local copies, waits for them, and re-layouts  3.12 us (1%)
    ppermute x14, starting transfers between devices, ship(): return lax.ppermute(x, 'tp', pairs)  81.1 us
    ppermute x14, waiting for transfers between devices, ship(): return lax.ppermute(x, 'tp', pairs)  52.9 us
    all_to_all x3, starting transfers between devices, exchange(): lax.all_to_all(x, axis, split_axis=0, concat_axis=0, tiled=True, axis_ind...  34.3 us
    all_to_all x3, waiting for transfers between devices, exchange(): lax.all_to_all(x, axis, split_axis=0, concat_axis=0, tiled=True, axis_ind...  16 us
    ppermute x3, starting transfers between devices, beside(): lax.ppermute(x, 'tp', [(g[i], g[(i + k) % local]) for g in near for i in...  9.55 us
    all_to_all x1, blocking collectives, exchange(): lax.all_to_all(x, axis, split_axis=0, concat_axis=0, tiled=True, axis_ind...  7.46 us
  transfers between devices with their start and end apart: 20, of which 12 were waited for; matrix products, arithmetic and copies ran while one was open for 2% of the time, Pallas kernels for 0%

profile of v8, /device:TPU:1, one launch (start us, length us, event | category | flops | bytes accessed | tf_op | source)
XLA Modules:
  0.0 215.5 jit_solution(10302435988813486903)
XLA Ops:
  1.4 6.4 %all-to-all-start = ((bf16[4,64,128]{2,1,0:T(8,128)(2,1)}), bf16[4,64,128]{2,1,0:T(8,128)(2,1)S(1)}, u32[]{:S(2)}, u32[]{:S(2)}) async-start(bf16[4,64,128]{2,1,0:T(8,128)(2,1)} %broadcast_in_dim.68), calls=%async_computation | async-start | bytes 131072 | tf_op jit(solution)/shard_map/all_to_all | solution.py:11
  9.1 5.2 %collective-permute-start.2 = (bf16[64,2304]{1,0:T(8,128)(2,1)S(1)}, bf16[64,2304]{1,0:T(8,128)(2,1)S(1)}, u32[]{:S(2)}, u32[]{:S(2)}) collective-permute-start(bf16[64,2304]{1,0:T(8,128)(2,1)S(1)} %pad_maximum_fusion.3), channel_id=1, source_target_pairs={{0,3},{1,0},{2,1},{3,2},{4,7},{5,4},{6,5},{7,6},{8,11},{9,8},{10,9... | collective-permute-start | bytes 884744 | tf_op jit(solution)/shard_map/ppermute | solution.py:52
  20.2 15.6 %all-to-all-start.1 = ((bf16[32,16,256]{2,1,0:T(8,128)(2,1)}), bf16[32,16,256]{2,1,0:T(8,128)(2,1)S(1)}, u32[]{:S(2)}, u32[]{:S(2)}) async-start(bf16[32,16,256]{2,1,0:T(8,128)(2,1)} %bitcast.8), calls=%async_computation.1 | async-start | bytes 524288 | tf_op jit(solution)/shard_map/all_to_all | solution.py:11
  36.0 3.9 %collective-permute-done.1 = bf16[64,2304]{1,0:T(8,128)(2,1)S(1)} collective-permute-done((bf16[64,2304]{1,0:T(8,128)(2,1)S(1)}, bf16[64,2304]{1,0:T(8,128)(2,1)S(1)}, u32[]{:S(2)}, u32[]{:S(2)}) %collective-permute-start.1) | collective-permute-done | bytes 294944 | tf_op jit(solution)/shard_map/ppermute | solution.py:52
  40.0 4.8 %all-to-all-done.1 = bf16[32,16,256]{2,1,0:T(8,128)(2,1)S(1)} async-done(((bf16[32,16,256]{2,1,0:T(8,128)(2,1)}), bf16[32,16,256]{2,1,0:T(8,128)(2,1)S(1)}, u32[]{:S(2)}, u32[]{:S(2)}) %all-to-all-start.1) | async-done | bytes 262176 | tf_op jit(solution)/shard_map/all_to_all | solution.py:11
  45.0 3.3 %collective-permute-start.3 = (bf16[64,1536]{1,0:T(8,128)(2,1)S(1)}, bf16[64,1536]{1,0:T(8,128)(2,1)S(1)}, u32[]{:S(2)}, u32[]{:S(2)}) collective-permute-start(bf16[64,1536]{1,0:T(8,128)(2,1)S(1)} %convolution_convert_fusion), channel_id=1, source_target_pairs={{0,4},{1,5},{2,30},{3,31},{4,8},{5,9},{6,2},{7,3},{8,12},{9,13},{1... | collective-permute-start | bytes 589832 | tf_op jit(solution)/shard_map/ppermute | solution.py:49
  49.9 10.6 %collective-permute-start.7 = (bf16[64,1536]{1,0:T(8,128)(2,1)S(1)}, bf16[64,1536]{1,0:T(8,128)(2,1)S(1)}, u32[]{:S(2)}, u32[]{:S(2)}) collective-permute-start(bf16[64,1536]{1,0:T(8,128)(2,1)S(1)} %convolution_convert_fusion.1), channel_id=1, source_target_pairs={{0,28},{1,29},{2,6},{3,7},{4,0},{5,1},{6,10},{7,11},{8,4},{9,5},{1... | collective-permute-start | bytes 589832 | tf_op jit(solution)/shard_map/ppermute | solution.py:49
  63.1 13.9 %collective-permute-done.7 = bf16[64,1536]{1,0:T(8,128)(2,1)S(1)} collective-permute-done((bf16[64,1536]{1,0:T(8,128)(2,1)S(1)}, bf16[64,1536]{1,0:T(8,128)(2,1)S(1)}, u32[]{:S(2)}, u32[]{:S(2)}) %collective-permute-start.7) | collective-permute-done | bytes 196640 | tf_op jit(solution)/shard_map/ppermute | solution.py:49
  77.1 8.2 %collective-permute-start.8 = (bf16[64,1536]{1,0:T(8,128)(2,1)S(1)}, bf16[64,1536]{1,0:T(8,128)(2,1)S(1)}, u32[]{:S(2)}, u32[]{:S(2)}) collective-permute-start(bf16[64,1536]{1,0:T(8,128)(2,1)S(1)} %add_convert_fusion.1), channel_id=1, source_target_pairs={{0,28},{1,29},{2,6},{3,7},{4,0},{5,1},{6,10},{7,11},{8,4},{9,5},{1... | collective-permute-start | bytes 589832 | tf_op jit(solution)/shard_map/ppermute | solution.py:49
  85.3 15.7 %collective-permute-start.5 = (bf16[64,1536]{1,0:T(8,128)(2,1)S(1)}, bf16[64,1536]{1,0:T(8,128)(2,1)S(1)}, u32[]{:S(2)}, u32[]{:S(2)}) collective-permute-start(bf16[64,1536]{1,0:T(8,128)(2,1)S(1)} %add_convert_fusion.3), channel_id=1, source_target_pairs={{0,4},{1,5},{2,30},{3,31},{4,8},{5,9},{6,2},{7,3},{8,12},{9,13},{1... | collective-permute-start | bytes 589832 | tf_op jit(solution)/shard_map/ppermute | solution.py:49
  103.6 10.7 %collective-permute-done.5 = bf16[64,1536]{1,0:T(8,128)(2,1)S(1)} collective-permute-done((bf16[64,1536]{1,0:T(8,128)(2,1)S(1)}, bf16[64,1536]{1,0:T(8,128)(2,1)S(1)}, u32[]{:S(2)}, u32[]{:S(2)}) %collective-permute-start.5) | collective-permute-done | bytes 196640 | tf_op jit(solution)/shard_map/ppermute | solution.py:49
  114.3 10.3 %collective-permute-start.6 = (bf16[64,1536]{1,0:T(8,128)(2,1)S(1)}, bf16[64,1536]{1,0:T(8,128)(2,1)S(1)}, u32[]{:S(2)}, u32[]{:S(2)}) collective-permute-start(bf16[64,1536]{1,0:T(8,128)(2,1)S(1)} %add_convert_fusion.2), channel_id=1, source_target_pairs={{0,4},{1,5},{2,30},{3,31},{4,8},{5,9},{6,2},{7,3},{8,12},{9,13},{1... | collective-permute-start | bytes 589832 | tf_op jit(solution)/shard_map/ppermute | solution.py:49
  124.7 5.3 %collective-permute-done.6 = bf16[64,1536]{1,0:T(8,128)(2,1)S(1)} collective-permute-done((bf16[64,1536]{1,0:T(8,128)(2,1)S(1)}, bf16[64,1536]{1,0:T(8,128)(2,1)S(1)}, u32[]{:S(2)}, u32[]{:S(2)}) %collective-permute-start.6) | collective-permute-done | bytes 196640 | tf_op jit(solution)/shard_map/ppermute | solution.py:49
  130.3 3.3 %collective-permute-start.11 = (bf16[64,768]{1,0:T(8,128)(2,1)S(1)}, bf16[64,768]{1,0:T(8,128)(2,1)S(1)}, u32[]{:S(2)}, u32[]{:S(2)}) collective-permute-start(bf16[64,768]{1,0:T(8,128)(2,1)S(1)} %fusion.9), channel_id=1, source_target_pairs={{0,28},{1,29},{2,6},{3,7},{4,0},{5,1},{6,10},{7,11},{8,4},{9,5},{1... | collective-permute-start | bytes 294920 | tf_op jit(solution)/shard_map/ppermute | solution.py:49
  133.6 6.7 %collective-permute-start.10 = (bf16[64,768]{1,0:T(8,128)(2,1)S(1)}, bf16[64,768]{1,0:T(8,128)(2,1)S(1)}, u32[]{:S(2)}, u32[]{:S(2)}) collective-permute-start(bf16[64,768]{1,0:T(8,128)(2,1)S(1)} %fusion.9), channel_id=1, source_target_pairs={{0,4},{1,5},{2,30},{3,31},{4,8},{5,9},{6,2},{7,3},{8,12},{9,13},{1... | collective-permute-start | bytes 294920 | tf_op jit(solution)/shard_map/ppermute | solution.py:49
  141.5 4.7 %collective-permute-start.13 = (bf16[64,768]{1,0:T(8,128)(2,1)S(1)}, bf16[64,768]{1,0:T(8,128)(2,1)S(1)}, u32[]{:S(2)}, u32[]{:S(2)}) collective-permute-start(bf16[64,768]{1,0:T(8,128)(2,1)S(1)} %collective-permute-done.11), channel_id=1, source_target_pairs={{0,28},{1,29},{2,6},{3,7},{4,0},{5,1},{6,10},{7,11},{8,4},{9,5},{1... | collective-permute-start | bytes 294920 | tf_op jit(solution)/shard_map/ppermute | solution.py:49
  148.7 3.5 %collective-permute-start.12 = (bf16[64,768]{1,0:T(8,128)(2,1)S(1)}, bf16[64,768]{1,0:T(8,128)(2,1)S(1)}, u32[]{:S(2)}, u32[]{:S(2)}) collective-permute-start(bf16[64,768]{1,0:T(8,128)(2,1)S(1)} %collective-permute-done.10), channel_id=1, source_target_pairs={{0,4},{1,5},{2,30},{3,31},{4,8},{5,9},{6,2},{7,3},{8,12},{9,13},{1... | collective-permute-start | bytes 294920 | tf_op jit(solution)/shard_map/ppermute | solution.py:49
  152.3 6.6 %collective-permute-start.15 = (bf16[64,768]{1,0:T(8,128)(2,1)S(1)}, bf16[64,768]{1,0:T(8,128)(2,1)S(1)}, u32[]{:S(2)}, u32[]{:S(2)}) collective-permute-start(bf16[64,768]{1,0:T(8,128)(2,1)S(1)} %collective-permute-done.13), channel_id=1, source_target_pairs={{0,28},{1,29},{2,6},{3,7},{4,0},{5,1},{6,10},{7,11},{8,4},{9,5},{1... | collective-permute-start | bytes 294920 | tf_op jit(solution)/shard_map/ppermute | solution.py:49
  158.9 3.2 %collective-permute-done.12 = bf16[64,768]{1,0:T(8,128)(2,1)S(1)} collective-permute-done((bf16[64,768]{1,0:T(8,128)(2,1)S(1)}, bf16[64,768]{1,0:T(8,128)(2,1)S(1)}, u32[]{:S(2)}, u32[]{:S(2)}) %collective-permute-start.12) | collective-permute-done | bytes 98336 | tf_op jit(solution)/shard_map/ppermute | solution.py:49
  164.0 8.3 %collective-permute-done.14 = bf16[64,768]{1,0:T(8,128)(2,1)S(1)} collective-permute-done((bf16[64,768]{1,0:T(8,128)(2,1)S(1)}, bf16[64,768]{1,0:T(8,128)(2,1)S(1)}, u32[]{:S(2)}, u32[]{:S(2)}) %collective-permute-start.14) | collective-permute-done | bytes 98336 | tf_op jit(solution)/shard_map/ppermute | solution.py:49
  174.3 7.3 %collective-permute-done.16 = bf16[64,768]{1,0:T(8,128)(2,1)S(1)} collective-permute-done((bf16[64,768]{1,0:T(8,128)(2,1)S(1)}, bf16[64,768]{1,0:T(8,128)(2,1)S(1)}, u32[]{:S(2)}, u32[]{:S(2)}) %collective-permute-start.16) | collective-permute-done | bytes 98336 | tf_op jit(solution)/shard_map/ppermute | solution.py:49
  182.8 12.3 %all-to-all-start.2 = ((f32[32,16,256]{2,1,0:T(8,128)}), f32[32,16,256]{2,1,0:T(8,128)S(1)}, u32[]{:S(2)}, u32[]{:S(2)}) async-start(f32[32,16,256]{2,1,0:T(8,128)} %fusion.1), calls=%async_computation.2 | async-start | bytes 1048576 | tf_op jit(solution)/shard_map/all_to_all | solution.py:11
  195.3 11.2 %all-to-all-done.2 = f32[32,16,256]{2,1,0:T(8,128)S(1)} async-done(((f32[32,16,256]{2,1,0:T(8,128)}), f32[32,16,256]{2,1,0:T(8,128)S(1)}, u32[]{:S(2)}, u32[]{:S(2)}) %all-to-all-start.2) | async-done | bytes 524320 | tf_op jit(solution)/shard_map/all_to_all | solution.py:11
  207.4 7.5 %all_to_all.20 = f32[4,64,128]{2,1,0:T(8,128)S(1)} all-to-all(f32[4,64,128]{2,1,0:T(8,128)S(1)} %pad_maximum_fusion.4), channel_id=1, replica_groups={{0,1,2,3},{4,5,6,7},{8,9,10,11},{12,13,14,15},{16,17,18,19},{20,21,22,2..., dimensions={0} | all-to-all | bytes 262144 | tf_op jit(solution)/shard_map/all_to_all | solution.py:11
  (88 shorter events, 26.4 us)
Async XLA Ops:
  1.4 17.8 %all-to-all-start = ((bf16[4,64,128]{2,1,0:T(8,128)(2,1)}), bf16[4,64,128]{2,1,0:T(8,128)(2,1)S(1)}, u32[]{:S(2)}, u32[]{:S(2)}) async-start(bf16[4,64,128]{2,1,0:T(8,128)(2,1)} %broadcast_in_dim.68), calls=%async_computation | async-start | bytes 131072 | tf_op jit(solution)/shard_map/all_to_all | solution.py:11
  9.1 26.8 %collective-permute-start.2 = (bf16[64,2304]{1,0:T(8,128)(2,1)S(1)}, bf16[64,2304]{1,0:T(8,128)(2,1)S(1)}, u32[]{:S(2)}, u32[]{:S(2)}) collective-permute-start(bf16[64,2304]{1,0:T(8,128)(2,1)S(1)} %pad_maximum_fusion.3), channel_id=1, source_target_pairs={{0,3},{1,0},{2,1},{3,2},{4,7},{5,4},{6,5},{7,6},{8,11},{9,8},{10,9... | collective-permute-start | bytes 884744 | tf_op jit(solution)/shard_map/ppermute | solution.py:52
  14.3 21.6 %collective-permute-start = (bf16[64,2304]{1,0:T(8,128)(2,1)S(1)}, bf16[64,2304]{1,0:T(8,128)(2,1)S(1)}, u32[]{:S(2)}, u32[]{:S(2)}) collective-permute-start(bf16[64,2304]{1,0:T(8,128)(2,1)S(1)} %pad_maximum_fusion.1), channel_id=1, source_target_pairs={{0,1},{1,2},{2,3},{3,0},{4,5},{5,6},{6,7},{7,4},{8,9},{9,10},{10,1... | collective-permute-start | bytes 884744 | tf_op jit(solution)/shard_map/ppermute | solution.py:52
  16.2 23.7 %collective-permute-start.1 = (bf16[64,2304]{1,0:T(8,128)(2,1)S(1)}, bf16[64,2304]{1,0:T(8,128)(2,1)S(1)}, u32[]{:S(2)}, u32[]{:S(2)}) collective-permute-start(bf16[64,2304]{1,0:T(8,128)(2,1)S(1)} %pad_maximum_fusion.2), channel_id=1, source_target_pairs={{0,2},{1,3},{2,0},{3,1},{4,6},{5,7},{6,4},{7,5},{8,10},{9,11},{10,... | collective-permute-start | bytes 884744 | tf_op jit(solution)/shard_map/ppermute | solution.py:52
  20.2 24.6 %all-to-all-start.1 = ((bf16[32,16,256]{2,1,0:T(8,128)(2,1)}), bf16[32,16,256]{2,1,0:T(8,128)(2,1)S(1)}, u32[]{:S(2)}, u32[]{:S(2)}) async-start(bf16[32,16,256]{2,1,0:T(8,128)(2,1)} %bitcast.8), calls=%async_computation.1 | async-start | bytes 524288 | tf_op jit(solution)/shard_map/all_to_all | solution.py:11
  35.9 88.8 %copy-start.2 = (bf16[64,2304]{1,0:T(8,128)(2,1)}, bf16[64,2304]{1,0:T(8,128)(2,1)S(1)}, u32[]{:S(2)}) copy-start(bf16[64,2304]{1,0:T(8,128)(2,1)S(1)} %collective-permute-done.2) | copy-start | bytes 884740
  35.9 88.8 %copy-start.3 = (bf16[64,2304]{1,0:T(8,128)(2,1)}, bf16[64,2304]{1,0:T(8,128)(2,1)S(1)}, u32[]{:S(2)}) copy-start(bf16[64,2304]{1,0:T(8,128)(2,1)S(1)} %collective-permute-done) | copy-start | bytes 884740
  39.9 84.8 %copy-start.4 = (bf16[64,2304]{1,0:T(8,128)(2,1)}, bf16[64,2304]{1,0:T(8,128)(2,1)S(1)}, u32[]{:S(2)}) copy-start(bf16[64,2304]{1,0:T(8,128)(2,1)S(1)} %collective-permute-done.1) | copy-start | bytes 884740
  45.0 16.1 %collective-permute-start.3 = (bf16[64,1536]{1,0:T(8,128)(2,1)S(1)}, bf16[64,1536]{1,0:T(8,128)(2,1)S(1)}, u32[]{:S(2)}, u32[]{:S(2)}) collective-permute-start(bf16[64,1536]{1,0:T(8,128)(2,1)S(1)} %convolution_convert_fusion), channel_id=1, source_target_pairs={{0,4},{1,5},{2,30},{3,31},{4,8},{5,9},{6,2},{7,3},{8,12},{9,13},{1... | collective-permute-start | bytes 589832 | tf_op jit(solution)/shard_map/ppermute | solution.py:49
  49.9 27.1 %collective-permute-start.7 = (bf16[64,1536]{1,0:T(8,128)(2,1)S(1)}, bf16[64,1536]{1,0:T(8,128)(2,1)S(1)}, u32[]{:S(2)}, u32[]{:S(2)}) collective-permute-start(bf16[64,1536]{1,0:T(8,128)(2,1)S(1)} %convolution_convert_fusion.1), channel_id=1, source_target_pairs={{0,28},{1,29},{2,6},{3,7},{4,0},{5,1},{6,10},{7,11},{8,4},{9,5},{1... | collective-permute-start | bytes 589832 | tf_op jit(solution)/shard_map/ppermute | solution.py:49
  61.1 24.1 %collective-permute-start.4 = (bf16[64,1536]{1,0:T(8,128)(2,1)S(1)}, bf16[64,1536]{1,0:T(8,128)(2,1)S(1)}, u32[]{:S(2)}, u32[]{:S(2)}) collective-permute-start(bf16[64,1536]{1,0:T(8,128)(2,1)S(1)} %add_convert_fusion.4), channel_id=1, source_target_pairs={{0,4},{1,5},{2,30},{3,31},{4,8},{5,9},{6,2},{7,3},{8,12},{9,13},{1... | collective-permute-start | bytes 589832 | tf_op jit(solution)/shard_map/ppermute | solution.py:49
  77.1 23.9 %collective-permute-start.8 = (bf16[64,1536]{1,0:T(8,128)(2,1)S(1)}, bf16[64,1536]{1,0:T(8,128)(2,1)S(1)}, u32[]{:S(2)}, u32[]{:S(2)}) collective-permute-start(bf16[64,1536]{1,0:T(8,128)(2,1)S(1)} %add_convert_fusion.1), channel_id=1, source_target_pairs={{0,28},{1,29},{2,6},{3,7},{4,0},{5,1},{6,10},{7,11},{8,4},{9,5},{1... | collective-permute-start | bytes 589832 | tf_op jit(solution)/shard_map/ppermute | solution.py:49
  85.3 29.0 %collective-permute-start.5 = (bf16[64,1536]{1,0:T(8,128)(2,1)S(1)}, bf16[64,1536]{1,0:T(8,128)(2,1)S(1)}, u32[]{:S(2)}, u32[]{:S(2)}) collective-permute-start(bf16[64,1536]{1,0:T(8,128)(2,1)S(1)} %add_convert_fusion.3), channel_id=1, source_target_pairs={{0,4},{1,5},{2,30},{3,31},{4,8},{5,9},{6,2},{7,3},{8,12},{9,13},{1... | collective-permute-start | bytes 589832 | tf_op jit(solution)/shard_map/ppermute | solution.py:49
  101.0 23.7 %collective-permute-start.9 = (bf16[64,1536]{1,0:T(8,128)(2,1)S(1)}, bf16[64,1536]{1,0:T(8,128)(2,1)S(1)}, u32[]{:S(2)}, u32[]{:S(2)}) collective-permute-start(bf16[64,1536]{1,0:T(8,128)(2,1)S(1)} %add_convert_fusion), channel_id=1, source_target_pairs={{0,28},{1,29},{2,6},{3,7},{4,0},{5,1},{6,10},{7,11},{8,4},{9,5},{1... | collective-permute-start | bytes 589832 | tf_op jit(solution)/shard_map/ppermute | solution.py:49
  114.3 15.7 %collective-permute-start.6 = (bf16[64,1536]{1,0:T(8,128)(2,1)S(1)}, bf16[64,1536]{1,0:T(8,128)(2,1)S(1)}, u32[]{:S(2)}, u32[]{:S(2)}) collective-permute-start(bf16[64,1536]{1,0:T(8,128)(2,1)S(1)} %add_convert_fusion.2), channel_id=1, source_target_pairs={{0,4},{1,5},{2,30},{3,31},{4,8},{5,9},{6,2},{7,3},{8,12},{9,13},{1... | collective-permute-start | bytes 589832 | tf_op jit(solution)/shard_map/ppermute | solution.py:49
  130.3 11.2 %collective-permute-start.11 = (bf16[64,768]{1,0:T(8,128)(2,1)S(1)}, bf16[64,768]{1,0:T(8,128)(2,1)S(1)}, u32[]{:S(2)}, u32[]{:S(2)}) collective-permute-start(bf16[64,768]{1,0:T(8,128)(2,1)S(1)} %fusion.9), channel_id=1, source_target_pairs={{0,28},{1,29},{2,6},{3,7},{4,0},{5,1},{6,10},{7,11},{8,4},{9,5},{1... | collective-permute-start | bytes 294920 | tf_op jit(solution)/shard_map/ppermute | solution.py:49
  133.6 15.1 %collective-permute-start.10 = (bf16[64,768]{1,0:T(8,128)(2,1)S(1)}, bf16[64,768]{1,0:T(8,128)(2,1)S(1)}, u32[]{:S(2)}, u32[]{:S(2)}) collective-permute-start(bf16[64,768]{1,0:T(8,128)(2,1)S(1)} %fusion.9), channel_id=1, source_target_pairs={{0,4},{1,5},{2,30},{3,31},{4,8},{5,9},{6,2},{7,3},{8,12},{9,13},{1... | collective-permute-start | bytes 294920 | tf_op jit(solution)/shard_map/ppermute | solution.py:49
  140.4 41.2 %slice-start = ((bf16[64,2304]{1,0:T(8,128)(2,1)}), bf16[64,768]{1,0:T(8,128)(2,1)S(1)}, s32[]{:S(2)}) async-start(bf16[64,2304]{1,0:T(8,128)(2,1)} %copy-done.2), calls=%async_computation.4 | async-start | bytes 196608 | tf_op jit(solution)/shard_map/slice | solution.py:71
  141.5 10.7 %collective-permute-start.13 = (bf16[64,768]{1,0:T(8,128)(2,1)S(1)}, bf16[64,768]{1,0:T(8,128)(2,1)S(1)}, u32[]{:S(2)}, u32[]{:S(2)}) collective-permute-start(bf16[64,768]{1,0:T(8,128)(2,1)S(1)} %collective-permute-done.11), channel_id=1, source_target_pairs={{0,28},{1,29},{2,6},{3,7},{4,0},{5,1},{6,10},{7,11},{8,4},{9,5},{1... | collective-permute-start | bytes 294920 | tf_op jit(solution)/shard_map/ppermute | solution.py:49
  148.7 13.3 %collective-permute-start.12 = (bf16[64,768]{1,0:T(8,128)(2,1)S(1)}, bf16[64,768]{1,0:T(8,128)(2,1)S(1)}, u32[]{:S(2)}, u32[]{:S(2)}) collective-permute-start(bf16[64,768]{1,0:T(8,128)(2,1)S(1)} %collective-permute-done.10), channel_id=1, source_target_pairs={{0,4},{1,5},{2,30},{3,31},{4,8},{5,9},{6,2},{7,3},{8,12},{9,13},{1... | collective-permute-start | bytes 294920 | tf_op jit(solution)/shard_map/ppermute | solution.py:49
  152.3 22.0 %collective-permute-start.15 = (bf16[64,768]{1,0:T(8,128)(2,1)S(1)}, bf16[64,768]{1,0:T(8,128)(2,1)S(1)}, u32[]{:S(2)}, u32[]{:S(2)}) collective-permute-start(bf16[64,768]{1,0:T(8,128)(2,1)S(1)} %collective-permute-done.13), channel_id=1, source_target_pairs={{0,28},{1,29},{2,6},{3,7},{4,0},{5,1},{6,10},{7,11},{8,4},{9,5},{1... | collective-permute-start | bytes 294920 | tf_op jit(solution)/shard_map/ppermute | solution.py:49
  162.1 10.3 %collective-permute-start.14 = (bf16[64,768]{1,0:T(8,128)(2,1)S(1)}, bf16[64,768]{1,0:T(8,128)(2,1)S(1)}, u32[]{:S(2)}, u32[]{:S(2)}) collective-permute-start(bf16[64,768]{1,0:T(8,128)(2,1)S(1)} %collective-permute-done.12), channel_id=1, source_target_pairs={{0,4},{1,5},{2,30},{3,31},{4,8},{5,9},{6,2},{7,3},{8,12},{9,13},{1... | collective-permute-start | bytes 294920 | tf_op jit(solution)/shard_map/ppermute | solution.py:49
  172.3 9.3 %collective-permute-start.16 = (bf16[64,768]{1,0:T(8,128)(2,1)S(1)}, bf16[64,768]{1,0:T(8,128)(2,1)S(1)}, u32[]{:S(2)}, u32[]{:S(2)}) collective-permute-start(bf16[64,768]{1,0:T(8,128)(2,1)S(1)} %collective-permute-done.14), channel_id=1, source_target_pairs={{0,4},{1,5},{2,30},{3,31},{4,8},{5,9},{6,2},{7,3},{8,12},{9,13},{1... | collective-permute-start | bytes 294920 | tf_op jit(solution)/shard_map/ppermute | solution.py:49
  182.8 23.7 %all-to-all-start.2 = ((f32[32,16,256]{2,1,0:T(8,128)}), f32[32,16,256]{2,1,0:T(8,128)S(1)}, u32[]{:S(2)}, u32[]{:S(2)}) async-start(f32[32,16,256]{2,1,0:T(8,128)} %fusion.1), calls=%async_computation.2 | async-start | bytes 1048576 | tf_op jit(solution)/shard_map/all_to_all | solution.py:11
  (6 other events, 122.3 us)

commit v9 on v8

--- a/solution.py
+++ b/solution.py
@@ -63,12 +63,15 @@
         e = lax.rem(me + k, local)
         g = lax.dynamic_index_in_dim(gate_weight, e, 0, keepdims=False)
         u = lax.dynamic_index_in_dim(up_weight, e, 0, keepdims=False)
-        d = lax.dynamic_index_in_dim(down_weight, e, 0, keepdims=False)
-        return jnp.concatenate([g, u, d], axis=1)
+        return jnp.concatenate([g, u], axis=1)
 
-    blocks = [in_block(0)] + [beside(in_block(k), k) for k in range(1, local)]
-    w_in = jnp.concatenate([b[:, : 2 * units] for b in blocks], axis=0)
-    w_down = jnp.concatenate([b[:, 2 * units :] for b in blocks], axis=0)
+    def down_block(k):
+        return lax.dynamic_index_in_dim(
+            down_weight, lax.rem(me + k, local), 0, keepdims=False
+        )
+
+    w_in = [in_block(0)] + [beside(in_block(k), k) for k in range(1, local)]
+    w_in = jnp.concatenate(w_in, axis=0)
 
     rt = routing.T
     expert = jnp.arange(ep, dtype=jnp.int32) * local + me
@@ -85,7 +88,12 @@
     mix = jnp.where(pick, factor[:, None, :], 0.0).reshape(slots, rows)
 
     outgoing = rows_dot(place, xt).astype(BF16)
+    sent = [down_block(k) for k in range(1, local)]
+    outgoing, sent = lax.optimization_barrier((outgoing, sent))
     x = exchange(outgoing.reshape(ep, capacity, -1), "ep")
+    w_down = [down_block(0)] + [beside(b, k + 1) for k, b in enumerate(sent)]
+    w_down = jnp.concatenate(w_down, axis=0)
+
     x = x.reshape(ring, chunk, -1)
 
     def term(k):

time: 216 us -> 217 us (level)
  starting transfers between devices: 125 us -> 147 us
  waiting for transfers between devices: 72.8 us -> 51.7 us
    ppermute x14, waiting for transfers between devices: 52.9 us -> 31.7 us  [ship(): return lax.ppermute(x, 'tp', pairs)]
    ppermute x3 -> x6, starting transfers between devices: 9.55 us -> 19.6 us  [beside(): lax.ppermute(x, 'tp', [(g[i], g[(i + k) % local]) for g in near for i in...]
    ppermute x14, starting transfers between devices: 81.1 us -> 87.3 us  [ship(): return lax.ppermute(x, 'tp', pairs)]
    all_to_all x3, starting transfers between devices: 34.3 us -> 39.7 us  [exchange(): lax.all_to_all(x, axis, split_axis=0, concat_axis=0, tiled=True, axis_ind...]
    all_to_all x3, waiting for transfers between devices: 16 us -> 20 us  [exchange(): lax.all_to_all(x, axis, split_axis=0, concat_axis=0, tiled=True, axis_ind...]
    ppermute x3 -> x6, waiting for transfers between devices: 3.95 us -> 0.02 us  [beside(): lax.ppermute(x, 'tp', [(g[i], g[(i + k) % local]) for g in near for i in...]
  transfers between devices with their start and end apart: 20 -> 23, of which waited for: 12 -> 11; matrix products, arithmetic and copies ran while one was open for 2% -> 2% of each run, Pallas kernels for 0% -> 0%
where the time goes in v9:
time: 217 us; the launch traced here: 216 us
  starting transfers between devices  147 us (68%)
  waiting for transfers between devices  51.7 us (24%)
  blocking collectives  7.54 us (3%)
  matrix products  4.94 us (2%)
  local copies, waits for them, and re-layouts  3.15 us (1%)
    ppermute x14, starting transfers between devices, ship(): return lax.ppermute(x, 'tp', pairs)  87.3 us
    all_to_all x3, starting transfers between devices, exchange(): lax.all_to_all(x, axis, split_axis=0, concat_axis=0, tiled=True, axis_ind...  39.7 us
    ppermute x14, waiting for transfers between devices, ship(): return lax.ppermute(x, 'tp', pairs)  31.7 us
    all_to_all x3, waiting for transfers between devices, exchange(): lax.all_to_all(x, axis, split_axis=0, concat_axis=0, tiled=True, axis_ind...  20 us
    ppermute x6, starting transfers between devices, beside(): lax.ppermute(x, 'tp', [(g[i], g[(i + k) % local]) for g in near for i in...  19.6 us
    all_to_all x1, blocking collectives, exchange(): lax.all_to_all(x, axis, split_axis=0, concat_axis=0, tiled=True, axis_ind...  7.54 us
  transfers between devices with their start and end apart: 23, of which 11 were waited for; matrix products, arithmetic and copies ran while one was open for 2% of the time, Pallas kernels for 0%

profile of v9, /device:TPU:1, one launch (start us, length us, event | category | flops | bytes accessed | tf_op | source)
XLA Modules:
  0.0 216.0 jit_solution(18277695895273063184)
XLA Ops:
  1.3 6.4 %all-to-all-start = ((bf16[4,64,128]{2,1,0:T(8,128)(2,1)}), bf16[4,64,128]{2,1,0:T(8,128)(2,1)S(1)}, u32[]{:S(2)}, u32[]{:S(2)}) async-start(bf16[4,64,128]{2,1,0:T(8,128)(2,1)} %broadcast_in_dim.68), calls=%async_computation | async-start | bytes 131072 | tf_op jit(solution)/shard_map/all_to_all | solution.py:11
  9.1 3.5 %collective-permute-start = (bf16[64,1536]{1,0:T(8,128)(2,1)S(1)}, bf16[64,1536]{1,0:T(8,128)(2,1)S(1)}, u32[]{:S(2)}, u32[]{:S(2)}) collective-permute-start(bf16[64,1536]{1,0:T(8,128)(2,1)S(1)} %pad_maximum_fusion.1), channel_id=1, source_target_pairs={{0,1},{1,2},{2,3},{3,0},{4,5},{5,6},{6,7},{7,4},{8,9},{9,10},{10,1... | collective-permute-start | bytes 589832 | tf_op jit(solution)/shard_map/ppermute | solution.py:52
  12.6 4.0 %collective-permute-start.1 = (bf16[64,1536]{1,0:T(8,128)(2,1)S(1)}, bf16[64,1536]{1,0:T(8,128)(2,1)S(1)}, u32[]{:S(2)}, u32[]{:S(2)}) collective-permute-start(bf16[64,1536]{1,0:T(8,128)(2,1)S(1)} %pad_maximum_fusion.2), channel_id=1, source_target_pairs={{0,2},{1,3},{2,0},{3,1},{4,6},{5,7},{6,4},{7,5},{8,10},{9,11},{10,... | collective-permute-start | bytes 589832 | tf_op jit(solution)/shard_map/ppermute | solution.py:52
  16.7 3.1 %collective-permute-start.2 = (bf16[64,1536]{1,0:T(8,128)(2,1)S(1)}, bf16[64,1536]{1,0:T(8,128)(2,1)S(1)}, u32[]{:S(2)}, u32[]{:S(2)}) collective-permute-start(bf16[64,1536]{1,0:T(8,128)(2,1)S(1)} %pad_maximum_fusion.3), channel_id=1, source_target_pairs={{0,3},{1,0},{2,1},{3,2},{4,7},{5,4},{6,5},{7,6},{8,11},{9,8},{10,9... | collective-permute-start | bytes 589832 | tf_op jit(solution)/shard_map/ppermute | solution.py:52
  21.3 15.6 %all-to-all-start.1 = ((bf16[32,16,256]{2,1,0:T(8,128)(2,1)}), bf16[32,16,256]{2,1,0:T(8,128)(2,1)S(1)}, u32[]{:S(2)}, u32[]{:S(2)}) async-start(bf16[32,16,256]{2,1,0:T(8,128)(2,1)} %bitcast.11), calls=%async_computation.1 | async-start | bytes 524288 | tf_op jit(solution)/shard_map/all_to_all | solution.py:11
  37.1 8.8 %all-to-all-done.1 = bf16[32,16,256]{2,1,0:T(8,128)(2,1)S(1)} async-done(((bf16[32,16,256]{2,1,0:T(8,128)(2,1)}), bf16[32,16,256]{2,1,0:T(8,128)(2,1)S(1)}, u32[]{:S(2)}, u32[]{:S(2)}) %all-to-all-start.1) | async-done | bytes 262176 | tf_op jit(solution)/shard_map/all_to_all | solution.py:11
  50.0 10.2 %collective-permute-start.7 = (bf16[64,1536]{1,0:T(8,128)(2,1)S(1)}, bf16[64,1536]{1,0:T(8,128)(2,1)S(1)}, u32[]{:S(2)}, u32[]{:S(2)}) collective-permute-start(bf16[64,1536]{1,0:T(8,128)(2,1)S(1)} %convolution_convert_fusion.1), channel_id=1, source_target_pairs={{0,28},{1,29},{2,6},{3,7},{4,0},{5,1},{6,10},{7,11},{8,4},{9,5},{1... | collective-permute-start | bytes 589832 | tf_op jit(solution)/shard_map/ppermute | solution.py:49
  61.9 2.7 %collective-permute-start.4 = (bf16[64,1536]{1,0:T(8,128)(2,1)S(1)}, bf16[64,1536]{1,0:T(8,128)(2,1)S(1)}, u32[]{:S(2)}, u32[]{:S(2)}) collective-permute-start(bf16[64,1536]{1,0:T(8,128)(2,1)S(1)} %add_convert_fusion.4), channel_id=1, source_target_pairs={{0,4},{1,5},{2,30},{3,31},{4,8},{5,9},{6,2},{7,3},{8,12},{9,13},{1... | collective-permute-start | bytes 589832 | tf_op jit(solution)/shard_map/ppermute | solution.py:49
  64.7 7.6 %collective-permute-done.7 = bf16[64,1536]{1,0:T(8,128)(2,1)S(1)} collective-permute-done((bf16[64,1536]{1,0:T(8,128)(2,1)S(1)}, bf16[64,1536]{1,0:T(8,128)(2,1)S(1)}, u32[]{:S(2)}, u32[]{:S(2)}) %collective-permute-start.7) | collective-permute-done | bytes 196640 | tf_op jit(solution)/shard_map/ppermute | solution.py:49
  72.3 6.8 %collective-permute-start.8 = (bf16[64,1536]{1,0:T(8,128)(2,1)S(1)}, bf16[64,1536]{1,0:T(8,128)(2,1)S(1)}, u32[]{:S(2)}, u32[]{:S(2)}) collective-permute-start(bf16[64,1536]{1,0:T(8,128)(2,1)S(1)} %add_convert_fusion.1), channel_id=1, source_target_pairs={{0,28},{1,29},{2,6},{3,7},{4,0},{5,1},{6,10},{7,11},{8,4},{9,5},{1... | collective-permute-start | bytes 589832 | tf_op jit(solution)/shard_map/ppermute | solution.py:49
  79.1 4.2 %collective-permute-done.4 = bf16[64,1536]{1,0:T(8,128)(2,1)S(1)} collective-permute-done((bf16[64,1536]{1,0:T(8,128)(2,1)S(1)}, bf16[64,1536]{1,0:T(8,128)(2,1)S(1)}, u32[]{:S(2)}, u32[]{:S(2)}) %collective-permute-start.4) | collective-permute-done | bytes 196640 | tf_op jit(solution)/shard_map/ppermute | solution.py:49
  83.3 17.7 %collective-permute-start.5 = (bf16[64,1536]{1,0:T(8,128)(2,1)S(1)}, bf16[64,1536]{1,0:T(8,128)(2,1)S(1)}, u32[]{:S(2)}, u32[]{:S(2)}) collective-permute-start(bf16[64,1536]{1,0:T(8,128)(2,1)S(1)} %add_convert_fusion.3), channel_id=1, source_target_pairs={{0,4},{1,5},{2,30},{3,31},{4,8},{5,9},{6,2},{7,3},{8,12},{9,13},{1... | collective-permute-start | bytes 589832 | tf_op jit(solution)/shard_map/ppermute | solution.py:49
  103.0 6.3 %collective-permute-done.5 = bf16[64,1536]{1,0:T(8,128)(2,1)S(1)} collective-permute-done((bf16[64,1536]{1,0:T(8,128)(2,1)S(1)}, bf16[64,1536]{1,0:T(8,128)(2,1)S(1)}, u32[]{:S(2)}, u32[]{:S(2)}) %collective-permute-start.5) | collective-permute-done | bytes 196640 | tf_op jit(solution)/shard_map/ppermute | solution.py:49
  109.4 15.8 %collective-permute-start.6 = (bf16[64,1536]{1,0:T(8,128)(2,1)S(1)}, bf16[64,1536]{1,0:T(8,128)(2,1)S(1)}, u32[]{:S(2)}, u32[]{:S(2)}) collective-permute-start(bf16[64,1536]{1,0:T(8,128)(2,1)S(1)} %add_convert_fusion.2), channel_id=1, source_target_pairs={{0,4},{1,5},{2,30},{3,31},{4,8},{5,9},{6,2},{7,3},{8,12},{9,13},{1... | collective-permute-start | bytes 589832 | tf_op jit(solution)/shard_map/ppermute | solution.py:49
  129.1 5.2 %collective-permute-start.19 = (bf16[64,768]{1,0:T(8,128)(2,1)S(1)}, bf16[64,768]{1,0:T(8,128)(2,1)S(1)}, u32[]{:S(2)}, u32[]{:S(2)}) collective-permute-start(bf16[64,768]{1,0:T(8,128)(2,1)S(1)} %get-tuple-element.24), channel_id=1, source_target_pairs={{0,3},{1,0},{2,1},{3,2},{4,7},{5,4},{6,5},{7,6},{8,11},{9,8},{10,9... | collective-permute-start | bytes 294920 | tf_op jit(solution)/shard_map/ppermute | solution.py:52
  137.2 6.5 %collective-permute-start.11 = (bf16[64,768]{1,0:T(8,128)(2,1)S(1)}, bf16[64,768]{1,0:T(8,128)(2,1)S(1)}, u32[]{:S(2)}, u32[]{:S(2)}) collective-permute-start(bf16[64,768]{1,0:T(8,128)(2,1)S(1)} %fusion.9), channel_id=1, source_target_pairs={{0,28},{1,29},{2,6},{3,7},{4,0},{5,1},{6,10},{7,11},{8,4},{9,5},{1... | collective-permute-start | bytes 294920 | tf_op jit(solution)/shard_map/ppermute | solution.py:49
  146.6 5.0 %collective-permute-done.11 = bf16[64,768]{1,0:T(8,128)(2,1)S(1)} collective-permute-done((bf16[64,768]{1,0:T(8,128)(2,1)S(1)}, bf16[64,768]{1,0:T(8,128)(2,1)S(1)}, u32[]{:S(2)}, u32[]{:S(2)}) %collective-permute-start.11) | collective-permute-done | bytes 98336 | tf_op jit(solution)/shard_map/ppermute | solution.py:49
  151.6 2.7 %collective-permute-start.13 = (bf16[64,768]{1,0:T(8,128)(2,1)S(1)}, bf16[64,768]{1,0:T(8,128)(2,1)S(1)}, u32[]{:S(2)}, u32[]{:S(2)}) collective-permute-start(bf16[64,768]{1,0:T(8,128)(2,1)S(1)} %collective-permute-done.11), channel_id=1, source_target_pairs={{0,28},{1,29},{2,6},{3,7},{4,0},{5,1},{6,10},{7,11},{8,4},{9,5},{1... | collective-permute-start | bytes 294920 | tf_op jit(solution)/shard_map/ppermute | solution.py:49
  154.4 6.4 %collective-permute-start.14 = (bf16[64,768]{1,0:T(8,128)(2,1)S(1)}, bf16[64,768]{1,0:T(8,128)(2,1)S(1)}, u32[]{:S(2)}, u32[]{:S(2)}) collective-permute-start(bf16[64,768]{1,0:T(8,128)(2,1)S(1)} %collective-permute-done.12), channel_id=1, source_target_pairs={{0,4},{1,5},{2,30},{3,31},{4,8},{5,9},{6,2},{7,3},{8,12},{9,13},{1... | collective-permute-start | bytes 294920 | tf_op jit(solution)/shard_map/ppermute | solution.py:49
  164.4 7.3 %collective-permute-start.16 = (bf16[64,768]{1,0:T(8,128)(2,1)S(1)}, bf16[64,768]{1,0:T(8,128)(2,1)S(1)}, u32[]{:S(2)}, u32[]{:S(2)}) collective-permute-start(bf16[64,768]{1,0:T(8,128)(2,1)S(1)} %collective-permute-done.14), channel_id=1, source_target_pairs={{0,4},{1,5},{2,30},{3,31},{4,8},{5,9},{6,2},{7,3},{8,12},{9,13},{1... | collective-permute-start | bytes 294920 | tf_op jit(solution)/shard_map/ppermute | solution.py:49
  172.2 4.4 %collective-permute-done.16 = bf16[64,768]{1,0:T(8,128)(2,1)S(1)} collective-permute-done((bf16[64,768]{1,0:T(8,128)(2,1)S(1)}, bf16[64,768]{1,0:T(8,128)(2,1)S(1)}, u32[]{:S(2)}, u32[]{:S(2)}) %collective-permute-start.16) | collective-permute-done | bytes 98336 | tf_op jit(solution)/shard_map/ppermute | solution.py:49
  177.9 17.7 %all-to-all-start.2 = ((f32[32,16,256]{2,1,0:T(8,128)}), f32[32,16,256]{2,1,0:T(8,128)S(1)}, u32[]{:S(2)}, u32[]{:S(2)}) async-start(f32[32,16,256]{2,1,0:T(8,128)} %fusion.1), calls=%async_computation.2 | async-start | bytes 1048576 | tf_op jit(solution)/shard_map/all_to_all | solution.py:11
  195.8 11.2 %all-to-all-done.2 = f32[32,16,256]{2,1,0:T(8,128)S(1)} async-done(((f32[32,16,256]{2,1,0:T(8,128)}), f32[32,16,256]{2,1,0:T(8,128)S(1)}, u32[]{:S(2)}, u32[]{:S(2)}) %all-to-all-start.2) | async-done | bytes 524320 | tf_op jit(solution)/shard_map/all_to_all | solution.py:11
  207.9 7.5 %all_to_all.20 = f32[4,64,128]{2,1,0:T(8,128)S(1)} all-to-all(f32[4,64,128]{2,1,0:T(8,128)S(1)} %pad_maximum_fusion.4), channel_id=1, replica_groups={{0,1,2,3},{4,5,6,7},{8,9,10,11},{12,13,14,15},{16,17,18,19},{20,21,22,2..., dimensions={0} | all-to-all | bytes 262144 | tf_op jit(solution)/shard_map/all_to_all | solution.py:11
  (77 shorter events, 28.6 us)
Async XLA Ops:
  1.3 19.0 %all-to-all-start = ((bf16[4,64,128]{2,1,0:T(8,128)(2,1)}), bf16[4,64,128]{2,1,0:T(8,128)(2,1)S(1)}, u32[]{:S(2)}, u32[]{:S(2)}) async-start(bf16[4,64,128]{2,1,0:T(8,128)(2,1)} %broadcast_in_dim.68), calls=%async_computation | async-start | bytes 131072 | tf_op jit(solution)/shard_map/all_to_all | solution.py:11
  9.1 27.9 %collective-permute-start = (bf16[64,1536]{1,0:T(8,128)(2,1)S(1)}, bf16[64,1536]{1,0:T(8,128)(2,1)S(1)}, u32[]{:S(2)}, u32[]{:S(2)}) collective-permute-start(bf16[64,1536]{1,0:T(8,128)(2,1)S(1)} %pad_maximum_fusion.1), channel_id=1, source_target_pairs={{0,1},{1,2},{2,3},{3,0},{4,5},{5,6},{6,7},{7,4},{8,9},{9,10},{10,1... | collective-permute-start | bytes 589832 | tf_op jit(solution)/shard_map/ppermute | solution.py:52
  12.6 24.4 %collective-permute-start.1 = (bf16[64,1536]{1,0:T(8,128)(2,1)S(1)}, bf16[64,1536]{1,0:T(8,128)(2,1)S(1)}, u32[]{:S(2)}, u32[]{:S(2)}) collective-permute-start(bf16[64,1536]{1,0:T(8,128)(2,1)S(1)} %pad_maximum_fusion.2), channel_id=1, source_target_pairs={{0,2},{1,3},{2,0},{3,1},{4,6},{5,7},{6,4},{7,5},{8,10},{9,11},{10,... | collective-permute-start | bytes 589832 | tf_op jit(solution)/shard_map/ppermute | solution.py:52
  16.7 20.4 %collective-permute-start.2 = (bf16[64,1536]{1,0:T(8,128)(2,1)S(1)}, bf16[64,1536]{1,0:T(8,128)(2,1)S(1)}, u32[]{:S(2)}, u32[]{:S(2)}) collective-permute-start(bf16[64,1536]{1,0:T(8,128)(2,1)S(1)} %pad_maximum_fusion.3), channel_id=1, source_target_pairs={{0,3},{1,0},{2,1},{3,2},{4,7},{5,4},{6,5},{7,6},{8,11},{9,8},{10,9... | collective-permute-start | bytes 589832 | tf_op jit(solution)/shard_map/ppermute | solution.py:52
  21.3 24.6 %all-to-all-start.1 = ((bf16[32,16,256]{2,1,0:T(8,128)(2,1)}), bf16[32,16,256]{2,1,0:T(8,128)(2,1)S(1)}, u32[]{:S(2)}, u32[]{:S(2)}) async-start(bf16[32,16,256]{2,1,0:T(8,128)(2,1)} %bitcast.11), calls=%async_computation.1 | async-start | bytes 524288 | tf_op jit(solution)/shard_map/all_to_all | solution.py:11
  46.2 15.7 %collective-permute-start.3 = (bf16[64,1536]{1,0:T(8,128)(2,1)S(1)}, bf16[64,1536]{1,0:T(8,128)(2,1)S(1)}, u32[]{:S(2)}, u32[]{:S(2)}) collective-permute-start(bf16[64,1536]{1,0:T(8,128)(2,1)S(1)} %convolution_convert_fusion), channel_id=1, source_target_pairs={{0,4},{1,5},{2,30},{3,31},{4,8},{5,9},{6,2},{7,3},{8,12},{9,13},{1... | collective-permute-start | bytes 589832 | tf_op jit(solution)/shard_map/ppermute | solution.py:49
  50.0 22.3 %collective-permute-start.7 = (bf16[64,1536]{1,0:T(8,128)(2,1)S(1)}, bf16[64,1536]{1,0:T(8,128)(2,1)S(1)}, u32[]{:S(2)}, u32[]{:S(2)}) collective-permute-start(bf16[64,1536]{1,0:T(8,128)(2,1)S(1)} %convolution_convert_fusion.1), channel_id=1, source_target_pairs={{0,28},{1,29},{2,6},{3,7},{4,0},{5,1},{6,10},{7,11},{8,4},{9,5},{1... | collective-permute-start | bytes 589832 | tf_op jit(solution)/shard_map/ppermute | solution.py:49
  61.9 21.4 %collective-permute-start.4 = (bf16[64,1536]{1,0:T(8,128)(2,1)S(1)}, bf16[64,1536]{1,0:T(8,128)(2,1)S(1)}, u32[]{:S(2)}, u32[]{:S(2)}) collective-permute-start(bf16[64,1536]{1,0:T(8,128)(2,1)S(1)} %add_convert_fusion.4), channel_id=1, source_target_pairs={{0,4},{1,5},{2,30},{3,31},{4,8},{5,9},{6,2},{7,3},{8,12},{9,13},{1... | collective-permute-start | bytes 589832 | tf_op jit(solution)/shard_map/ppermute | solution.py:49
  72.3 28.7 %collective-permute-start.8 = (bf16[64,1536]{1,0:T(8,128)(2,1)S(1)}, bf16[64,1536]{1,0:T(8,128)(2,1)S(1)}, u32[]{:S(2)}, u32[]{:S(2)}) collective-permute-start(bf16[64,1536]{1,0:T(8,128)(2,1)S(1)} %add_convert_fusion.1), channel_id=1, source_target_pairs={{0,28},{1,29},{2,6},{3,7},{4,0},{5,1},{6,10},{7,11},{8,4},{9,5},{1... | collective-permute-start | bytes 589832 | tf_op jit(solution)/shard_map/ppermute | solution.py:49
  83.3 26.0 %collective-permute-start.5 = (bf16[64,1536]{1,0:T(8,128)(2,1)S(1)}, bf16[64,1536]{1,0:T(8,128)(2,1)S(1)}, u32[]{:S(2)}, u32[]{:S(2)}) collective-permute-start(bf16[64,1536]{1,0:T(8,128)(2,1)S(1)} %add_convert_fusion.3), channel_id=1, source_target_pairs={{0,4},{1,5},{2,30},{3,31},{4,8},{5,9},{6,2},{7,3},{8,12},{9,13},{1... | collective-permute-start | bytes 589832 | tf_op jit(solution)/shard_map/ppermute | solution.py:49
  101.1 33.1 %collective-permute-start.9 = (bf16[64,1536]{1,0:T(8,128)(2,1)S(1)}, bf16[64,1536]{1,0:T(8,128)(2,1)S(1)}, u32[]{:S(2)}, u32[]{:S(2)}) collective-permute-start(bf16[64,1536]{1,0:T(8,128)(2,1)S(1)} %add_convert_fusion), channel_id=1, source_target_pairs={{0,28},{1,29},{2,6},{3,7},{4,0},{5,1},{6,10},{7,11},{8,4},{9,5},{1... | collective-permute-start | bytes 589832 | tf_op jit(solution)/shard_map/ppermute | solution.py:49
  109.4 24.9 %collective-permute-start.6 = (bf16[64,1536]{1,0:T(8,128)(2,1)S(1)}, bf16[64,1536]{1,0:T(8,128)(2,1)S(1)}, u32[]{:S(2)}, u32[]{:S(2)}) collective-permute-start(bf16[64,1536]{1,0:T(8,128)(2,1)S(1)} %add_convert_fusion.2), channel_id=1, source_target_pairs={{0,4},{1,5},{2,30},{3,31},{4,8},{5,9},{6,2},{7,3},{8,12},{9,13},{1... | collective-permute-start | bytes 589832 | tf_op jit(solution)/shard_map/ppermute | solution.py:49
  125.2 51.4 %collective-permute-start.17 = (bf16[64,768]{1,0:T(8,128)(2,1)S(1)}, bf16[64,768]{1,0:T(8,128)(2,1)S(1)}, u32[]{:S(2)}, u32[]{:S(2)}) collective-permute-start(bf16[64,768]{1,0:T(8,128)(2,1)S(1)} %get-tuple-element.22), channel_id=1, source_target_pairs={{0,1},{1,2},{2,3},{3,0},{4,5},{5,6},{6,7},{7,4},{8,9},{9,10},{10,1... | collective-permute-start | bytes 294920 | tf_op jit(solution)/shard_map/ppermute | solution.py:52
  127.1 49.5 %collective-permute-start.18 = (bf16[64,768]{1,0:T(8,128)(2,1)S(1)}, bf16[64,768]{1,0:T(8,128)(2,1)S(1)}, u32[]{:S(2)}, u32[]{:S(2)}) collective-permute-start(bf16[64,768]{1,0:T(8,128)(2,1)S(1)} %get-tuple-element.23), channel_id=1, source_target_pairs={{0,2},{1,3},{2,0},{3,1},{4,6},{5,7},{6,4},{7,5},{8,10},{9,11},{10,... | collective-permute-start | bytes 294920 | tf_op jit(solution)/shard_map/ppermute | solution.py:52
  129.1 47.6 %collective-permute-start.19 = (bf16[64,768]{1,0:T(8,128)(2,1)S(1)}, bf16[64,768]{1,0:T(8,128)(2,1)S(1)}, u32[]{:S(2)}, u32[]{:S(2)}) collective-permute-start(bf16[64,768]{1,0:T(8,128)(2,1)S(1)} %get-tuple-element.24), channel_id=1, source_target_pairs={{0,3},{1,0},{2,1},{3,2},{4,7},{5,4},{6,5},{7,6},{8,11},{9,8},{10,9... | collective-permute-start | bytes 294920 | tf_op jit(solution)/shard_map/ppermute | solution.py:52
  134.6 9.6 %collective-permute-start.10 = (bf16[64,768]{1,0:T(8,128)(2,1)S(1)}, bf16[64,768]{1,0:T(8,128)(2,1)S(1)}, u32[]{:S(2)}, u32[]{:S(2)}) collective-permute-start(bf16[64,768]{1,0:T(8,128)(2,1)S(1)} %fusion.9), channel_id=1, source_target_pairs={{0,4},{1,5},{2,30},{3,31},{4,8},{5,9},{6,2},{7,3},{8,12},{9,13},{1... | collective-permute-start | bytes 294920 | tf_op jit(solution)/shard_map/ppermute | solution.py:49
  137.2 14.4 %collective-permute-start.11 = (bf16[64,768]{1,0:T(8,128)(2,1)S(1)}, bf16[64,768]{1,0:T(8,128)(2,1)S(1)}, u32[]{:S(2)}, u32[]{:S(2)}) collective-permute-start(bf16[64,768]{1,0:T(8,128)(2,1)S(1)} %fusion.9), channel_id=1, source_target_pairs={{0,28},{1,29},{2,6},{3,7},{4,0},{5,1},{6,10},{7,11},{8,4},{9,5},{1... | collective-permute-start | bytes 294920 | tf_op jit(solution)/shard_map/ppermute | solution.py:49
  144.2 10.1 %collective-permute-start.12 = (bf16[64,768]{1,0:T(8,128)(2,1)S(1)}, bf16[64,768]{1,0:T(8,128)(2,1)S(1)}, u32[]{:S(2)}, u32[]{:S(2)}) collective-permute-start(bf16[64,768]{1,0:T(8,128)(2,1)S(1)} %collective-permute-done.10), channel_id=1, source_target_pairs={{0,4},{1,5},{2,30},{3,31},{4,8},{5,9},{6,2},{7,3},{8,12},{9,13},{1... | collective-permute-start | bytes 294920 | tf_op jit(solution)/shard_map/ppermute | solution.py:49
  151.6 10.9 %collective-permute-start.13 = (bf16[64,768]{1,0:T(8,128)(2,1)S(1)}, bf16[64,768]{1,0:T(8,128)(2,1)S(1)}, u32[]{:S(2)}, u32[]{:S(2)}) collective-permute-start(bf16[64,768]{1,0:T(8,128)(2,1)S(1)} %collective-permute-done.11), channel_id=1, source_target_pairs={{0,28},{1,29},{2,6},{3,7},{4,0},{5,1},{6,10},{7,11},{8,4},{9,5},{1... | collective-permute-start | bytes 294920 | tf_op jit(solution)/shard_map/ppermute | solution.py:49
  154.4 10.0 %collective-permute-start.14 = (bf16[64,768]{1,0:T(8,128)(2,1)S(1)}, bf16[64,768]{1,0:T(8,128)(2,1)S(1)}, u32[]{:S(2)}, u32[]{:S(2)}) collective-permute-start(bf16[64,768]{1,0:T(8,128)(2,1)S(1)} %collective-permute-done.12), channel_id=1, source_target_pairs={{0,4},{1,5},{2,30},{3,31},{4,8},{5,9},{6,2},{7,3},{8,12},{9,13},{1... | collective-permute-start | bytes 294920 | tf_op jit(solution)/shard_map/ppermute | solution.py:49
  162.5 9.7 %collective-permute-start.15 = (bf16[64,768]{1,0:T(8,128)(2,1)S(1)}, bf16[64,768]{1,0:T(8,128)(2,1)S(1)}, u32[]{:S(2)}, u32[]{:S(2)}) collective-permute-start(bf16[64,768]{1,0:T(8,128)(2,1)S(1)} %collective-permute-done.13), channel_id=1, source_target_pairs={{0,28},{1,29},{2,6},{3,7},{4,0},{5,1},{6,10},{7,11},{8,4},{9,5},{1... | collective-permute-start | bytes 294920 | tf_op jit(solution)/shard_map/ppermute | solution.py:49
  164.4 12.2 %collective-permute-start.16 = (bf16[64,768]{1,0:T(8,128)(2,1)S(1)}, bf16[64,768]{1,0:T(8,128)(2,1)S(1)}, u32[]{:S(2)}, u32[]{:S(2)}) collective-permute-start(bf16[64,768]{1,0:T(8,128)(2,1)S(1)} %collective-permute-done.14), channel_id=1, source_target_pairs={{0,4},{1,5},{2,30},{3,31},{4,8},{5,9},{6,2},{7,3},{8,12},{9,13},{1... | collective-permute-start | bytes 294920 | tf_op jit(solution)/shard_map/ppermute | solution.py:49
  177.9 17.7 %copy-start.2 = (s32[128,8]{0,1:T(8,128)S(1)}, s32[128,8]{0,1:T(8,128)}, u32[]{:S(2)}) copy-start(s32[128,8]{0,1:T(8,128)} %param.8) | copy-start | bytes 12292
  177.9 29.2 %all-to-all-start.2 = ((f32[32,16,256]{2,1,0:T(8,128)}), f32[32,16,256]{2,1,0:T(8,128)S(1)}, u32[]{:S(2)}, u32[]{:S(2)}) async-start(f32[32,16,256]{2,1,0:T(8,128)} %fusion.1), calls=%async_computation.2 | async-start | bytes 1048576 | tf_op jit(solution)/shard_map/all_to_all | solution.py:11
  (2 other events, 21.9 us)

commit v10 on v9

--- a/solution.py
+++ b/solution.py
@@ -36,9 +36,9 @@
     here = lax.div(z, local)
 
     def sign_of(r):
-        return 1 if r < local // 2 else -1
+        return 1 if r % 2 == 0 else -1
 
-    sign = jnp.where(me < local // 2, 1, -1)
+    sign = 1 - 2 * lax.rem(me, 2)
 
     def ship(x, side):
         pairs = [
@@ -102,12 +102,11 @@
 
     steps = ring // 2
     ahead = ship(term(steps).astype(BF16), 1)
-    early = [3, -2, 2, -1, 1]
+    early = [3, -2, 2, -1, 1, 0]
     made = [term(k) for k in early]
     first = term(1 - steps).astype(BF16)
     first, made = lax.optimization_barrier((first, made))
     made = dict(zip(early, made))
-    made[0] = term(0)
     behind = ship(first, -1)
     for k in range(steps - 1, 0, -1):
         ahead = ship((made[k] + ahead.astype(F32)).astype(BF16), 1)

time: 217 us -> 221 us (1.018)
  starting transfers between devices: 147 us -> 127 us
  waiting for transfers between devices: 51.7 us -> 67.6 us
  blocking collectives: 7.54 us -> 14.6 us
    ppermute x14, starting transfers between devices: 87.3 us -> 67.2 us  [ship(): return lax.ppermute(x, 'tp', pairs)]
    ppermute x14, waiting for transfers between devices: 31.7 us -> 47.6 us  [ship(): return lax.ppermute(x, 'tp', pairs)]
    all_to_all x1, blocking collectives: 7.54 us -> 14.6 us  [exchange(): lax.all_to_all(x, axis, split_axis=0, concat_axis=0, tiled=True, axis_ind...]
  transfers between devices with their start and end apart: 23 -> 23, of which waited for: 11 -> 13; matrix products, arithmetic and copies ran while one was open for 2% -> 2% of each run, Pallas kernels for 0% -> 0%
where the time goes in v10:
time: 221 us; the launch traced here: 220 us
  starting transfers between devices  127 us (57%)
  waiting for transfers between devices  67.6 us (31%)
  blocking collectives  14.6 us (7%)
  matrix products  4.94 us (2%)
  local copies, waits for them, and re-layouts  3.15 us (1%)
    ppermute x14, starting transfers between devices, ship(): return lax.ppermute(x, 'tp', pairs)  67.2 us
    ppermute x14, waiting for transfers between devices, ship(): return lax.ppermute(x, 'tp', pairs)  47.6 us
    all_to_all x3, starting transfers between devices, exchange(): lax.all_to_all(x, axis, split_axis=0, concat_axis=0, tiled=True, axis_ind...  40.4 us
    all_to_all x3, waiting for transfers between devices, exchange(): lax.all_to_all(x, axis, split_axis=0, concat_axis=0, tiled=True, axis_ind...  20 us
    ppermute x6, starting transfers between devices, beside(): lax.ppermute(x, 'tp', [(g[i], g[(i + k) % local]) for g in near for i in...  19.6 us
    all_to_all x1, blocking collectives, exchange(): lax.all_to_all(x, axis, split_axis=0, concat_axis=0, tiled=True, axis_ind...  14.6 us
  transfers between devices with their start and end apart: 23, of which 13 were waited for; matrix products, arithmetic and copies ran while one was open for 2% of the time, Pallas kernels for 0%

profile of v10, /device:TPU:1, one launch (start us, length us, event | category | flops | bytes accessed | tf_op | source)
XLA Modules:
  0.0 219.7 jit_solution(10824782910972423295)
XLA Ops:
  1.3 6.4 %all-to-all-start = ((bf16[4,64,128]{2,1,0:T(8,128)(2,1)}), bf16[4,64,128]{2,1,0:T(8,128)(2,1)S(1)}, u32[]{:S(2)}, u32[]{:S(2)}) async-start(bf16[4,64,128]{2,1,0:T(8,128)(2,1)} %broadcast_in_dim.68), calls=%async_computation | async-start | bytes 131072 | tf_op jit(solution)/shard_map/all_to_all | solution.py:11
  9.1 3.5 %collective-permute-start = (bf16[64,1536]{1,0:T(8,128)(2,1)S(1)}, bf16[64,1536]{1,0:T(8,128)(2,1)S(1)}, u32[]{:S(2)}, u32[]{:S(2)}) collective-permute-start(bf16[64,1536]{1,0:T(8,128)(2,1)S(1)} %pad_maximum_fusion.1), channel_id=1, source_target_pairs={{0,1},{1,2},{2,3},{3,0},{4,5},{5,6},{6,7},{7,4},{8,9},{9,10},{10,1... | collective-permute-start | bytes 589832 | tf_op jit(solution)/shard_map/ppermute | solution.py:52
  12.6 4.0 %collective-permute-start.1 = (bf16[64,1536]{1,0:T(8,128)(2,1)S(1)}, bf16[64,1536]{1,0:T(8,128)(2,1)S(1)}, u32[]{:S(2)}, u32[]{:S(2)}) collective-permute-start(bf16[64,1536]{1,0:T(8,128)(2,1)S(1)} %pad_maximum_fusion.2), channel_id=1, source_target_pairs={{0,2},{1,3},{2,0},{3,1},{4,6},{5,7},{6,4},{7,5},{8,10},{9,11},{10,... | collective-permute-start | bytes 589832 | tf_op jit(solution)/shard_map/ppermute | solution.py:52
  16.7 3.1 %collective-permute-start.2 = (bf16[64,1536]{1,0:T(8,128)(2,1)S(1)}, bf16[64,1536]{1,0:T(8,128)(2,1)S(1)}, u32[]{:S(2)}, u32[]{:S(2)}) collective-permute-start(bf16[64,1536]{1,0:T(8,128)(2,1)S(1)} %pad_maximum_fusion.3), channel_id=1, source_target_pairs={{0,3},{1,0},{2,1},{3,2},{4,7},{5,4},{6,5},{7,6},{8,11},{9,8},{10,9... | collective-permute-start | bytes 589832 | tf_op jit(solution)/shard_map/ppermute | solution.py:52
  21.4 15.6 %all-to-all-start.1 = ((bf16[32,16,256]{2,1,0:T(8,128)(2,1)}), bf16[32,16,256]{2,1,0:T(8,128)(2,1)S(1)}, u32[]{:S(2)}, u32[]{:S(2)}) async-start(bf16[32,16,256]{2,1,0:T(8,128)(2,1)} %bitcast.11), calls=%async_computation.1 | async-start | bytes 524288 | tf_op jit(solution)/shard_map/all_to_all | solution.py:11
  37.1 8.8 %all-to-all-done.1 = bf16[32,16,256]{2,1,0:T(8,128)(2,1)S(1)} async-done(((bf16[32,16,256]{2,1,0:T(8,128)(2,1)}), bf16[32,16,256]{2,1,0:T(8,128)(2,1)S(1)}, u32[]{:S(2)}, u32[]{:S(2)}) %all-to-all-start.1) | async-done | bytes 262176 | tf_op jit(solution)/shard_map/all_to_all | solution.py:11
  46.2 2.3 %collective-permute-start.3 = (bf16[64,1536]{1,0:T(8,128)(2,1)S(1)}, bf16[64,1536]{1,0:T(8,128)(2,1)S(1)}, u32[]{:S(2)}, u32[]{:S(2)}) collective-permute-start(bf16[64,1536]{1,0:T(8,128)(2,1)S(1)} %convolution_convert_fusion), channel_id=1, source_target_pairs={{0,4},{1,29},{2,6},{3,31},{4,8},{5,1},{6,10},{7,3},{8,12},{9,5},{1... | collective-permute-start | bytes 589832 | tf_op jit(solution)/shard_map/ppermute | solution.py:49
  50.3 10.2 %collective-permute-start.7 = (bf16[64,1536]{1,0:T(8,128)(2,1)S(1)}, bf16[64,1536]{1,0:T(8,128)(2,1)S(1)}, u32[]{:S(2)}, u32[]{:S(2)}) collective-permute-start(bf16[64,1536]{1,0:T(8,128)(2,1)S(1)} %convolution_convert_fusion.1), channel_id=1, source_target_pairs={{0,28},{1,5},{2,30},{3,7},{4,0},{5,9},{6,2},{7,11},{8,4},{9,13},{1... | collective-permute-start | bytes 589832 | tf_op jit(solution)/shard_map/ppermute | solution.py:49
  60.5 5.6 %collective-permute-done.3 = bf16[64,1536]{1,0:T(8,128)(2,1)S(1)} collective-permute-done((bf16[64,1536]{1,0:T(8,128)(2,1)S(1)}, bf16[64,1536]{1,0:T(8,128)(2,1)S(1)}, u32[]{:S(2)}, u32[]{:S(2)}) %collective-permute-start.3) | collective-permute-done | bytes 196640 | tf_op jit(solution)/shard_map/ppermute | solution.py:49
  68.0 2.9 %collective-permute-done.7 = bf16[64,1536]{1,0:T(8,128)(2,1)S(1)} collective-permute-done((bf16[64,1536]{1,0:T(8,128)(2,1)S(1)}, bf16[64,1536]{1,0:T(8,128)(2,1)S(1)}, u32[]{:S(2)}, u32[]{:S(2)}) %collective-permute-start.7) | collective-permute-done | bytes 196640 | tf_op jit(solution)/shard_map/ppermute | solution.py:49
  71.0 6.4 %collective-permute-start.8 = (bf16[64,1536]{1,0:T(8,128)(2,1)S(1)}, bf16[64,1536]{1,0:T(8,128)(2,1)S(1)}, u32[]{:S(2)}, u32[]{:S(2)}) collective-permute-start(bf16[64,1536]{1,0:T(8,128)(2,1)S(1)} %add_convert_fusion.1), channel_id=1, source_target_pairs={{0,28},{1,5},{2,30},{3,7},{4,0},{5,9},{6,2},{7,11},{8,4},{9,13},{1... | collective-permute-start | bytes 589832 | tf_op jit(solution)/shard_map/ppermute | solution.py:49
  77.4 9.3 %collective-permute-done.4 = bf16[64,1536]{1,0:T(8,128)(2,1)S(1)} collective-permute-done((bf16[64,1536]{1,0:T(8,128)(2,1)S(1)}, bf16[64,1536]{1,0:T(8,128)(2,1)S(1)}, u32[]{:S(2)}, u32[]{:S(2)}) %collective-permute-start.4) | collective-permute-done | bytes 196640 | tf_op jit(solution)/shard_map/ppermute | solution.py:49
  88.7 10.2 %collective-permute-done.8 = bf16[64,1536]{1,0:T(8,128)(2,1)S(1)} collective-permute-done((bf16[64,1536]{1,0:T(8,128)(2,1)S(1)}, bf16[64,1536]{1,0:T(8,128)(2,1)S(1)}, u32[]{:S(2)}, u32[]{:S(2)}) %collective-permute-start.8) | collective-permute-done | bytes 196640 | tf_op jit(solution)/shard_map/ppermute | solution.py:49
  100.9 9.1 %collective-permute-done.5 = bf16[64,1536]{1,0:T(8,128)(2,1)S(1)} collective-permute-done((bf16[64,1536]{1,0:T(8,128)(2,1)S(1)}, bf16[64,1536]{1,0:T(8,128)(2,1)S(1)}, u32[]{:S(2)}, u32[]{:S(2)}) %collective-permute-start.5) | collective-permute-done | bytes 196640 | tf_op jit(solution)/shard_map/ppermute | solution.py:49
  114.1 2.2 collective-permute-start.18
  116.3 4.7 %collective-permute-start.19 = (bf16[64,768]{1,0:T(8,128)(2,1)S(1)}, bf16[64,768]{1,0:T(8,128)(2,1)S(1)}, u32[]{:S(2)}, u32[]{:S(2)}) collective-permute-start(bf16[64,768]{1,0:T(8,128)(2,1)S(1)} %get-tuple-element.26), channel_id=1, source_target_pairs={{0,3},{1,0},{2,1},{3,2},{4,7},{5,4},{6,5},{7,6},{8,11},{9,8},{10,9... | collective-permute-start | bytes 294920 | tf_op jit(solution)/shard_map/ppermute | solution.py:52
  121.4 5.9 %collective-permute-done.6 = bf16[64,1536]{1,0:T(8,128)(2,1)S(1)} collective-permute-done((bf16[64,1536]{1,0:T(8,128)(2,1)S(1)}, bf16[64,1536]{1,0:T(8,128)(2,1)S(1)}, u32[]{:S(2)}, u32[]{:S(2)}) %collective-permute-start.6) | collective-permute-done | bytes 196640 | tf_op jit(solution)/shard_map/ppermute | solution.py:49
  127.4 7.8 %collective-permute-start.10 = (bf16[64,768]{1,0:T(8,128)(2,1)S(1)}, bf16[64,768]{1,0:T(8,128)(2,1)S(1)}, u32[]{:S(2)}, u32[]{:S(2)}) collective-permute-start(bf16[64,768]{1,0:T(8,128)(2,1)S(1)} %fusion.8), channel_id=1, source_target_pairs={{0,4},{1,29},{2,6},{3,31},{4,8},{5,1},{6,10},{7,3},{8,12},{9,5},{1... | collective-permute-start | bytes 294920 | tf_op jit(solution)/shard_map/ppermute | solution.py:49
  137.7 8.9 %collective-permute-start.12 = (bf16[64,768]{1,0:T(8,128)(2,1)S(1)}, bf16[64,768]{1,0:T(8,128)(2,1)S(1)}, u32[]{:S(2)}, u32[]{:S(2)}) collective-permute-start(bf16[64,768]{1,0:T(8,128)(2,1)S(1)} %collective-permute-done.10), channel_id=1, source_target_pairs={{0,4},{1,29},{2,6},{3,31},{4,8},{5,1},{6,10},{7,3},{8,12},{9,5},{1... | collective-permute-start | bytes 294920 | tf_op jit(solution)/shard_map/ppermute | solution.py:49
  150.1 9.4 %collective-permute-start.14 = (bf16[64,768]{1,0:T(8,128)(2,1)S(1)}, bf16[64,768]{1,0:T(8,128)(2,1)S(1)}, u32[]{:S(2)}, u32[]{:S(2)}) collective-permute-start(bf16[64,768]{1,0:T(8,128)(2,1)S(1)} %collective-permute-done.12), channel_id=1, source_target_pairs={{0,4},{1,29},{2,6},{3,31},{4,8},{5,1},{6,10},{7,3},{8,12},{9,5},{1... | collective-permute-start | bytes 294920 | tf_op jit(solution)/shard_map/ppermute | solution.py:49
  161.7 8.8 %collective-permute-start.16 = (bf16[64,768]{1,0:T(8,128)(2,1)S(1)}, bf16[64,768]{1,0:T(8,128)(2,1)S(1)}, u32[]{:S(2)}, u32[]{:S(2)}) collective-permute-start(bf16[64,768]{1,0:T(8,128)(2,1)S(1)} %collective-permute-done.14), channel_id=1, source_target_pairs={{0,4},{1,29},{2,6},{3,31},{4,8},{5,1},{6,10},{7,3},{8,12},{9,5},{1... | collective-permute-start | bytes 294920 | tf_op jit(solution)/shard_map/ppermute | solution.py:49
  173.7 18.4 %all-to-all-start.2 = ((f32[32,16,256]{2,1,0:T(8,128)}), f32[32,16,256]{2,1,0:T(8,128)S(1)}, u32[]{:S(2)}, u32[]{:S(2)}) async-start(f32[32,16,256]{2,1,0:T(8,128)} %fusion), calls=%async_computation.2 | async-start | bytes 1048576 | tf_op jit(solution)/shard_map/all_to_all | solution.py:11
  192.4 11.2 %all-to-all-done.2 = f32[32,16,256]{2,1,0:T(8,128)S(1)} async-done(((f32[32,16,256]{2,1,0:T(8,128)}), f32[32,16,256]{2,1,0:T(8,128)S(1)}, u32[]{:S(2)}, u32[]{:S(2)}) %all-to-all-start.2) | async-done | bytes 524320 | tf_op jit(solution)/shard_map/all_to_all | solution.py:11
  204.4 14.6 %all_to_all.20 = f32[4,64,128]{2,1,0:T(8,128)S(1)} all-to-all(f32[4,64,128]{2,1,0:T(8,128)S(1)} %pad_maximum_fusion.4), channel_id=1, replica_groups={{0,1,2,3},{4,5,6,7},{8,9,10,11},{12,13,14,15},{16,17,18,19},{20,21,22,2..., dimensions={0} | all-to-all | bytes 262144 | tf_op jit(solution)/shard_map/all_to_all | solution.py:11
  (78 shorter events, 29.7 us)
Async XLA Ops:
  1.3 19.0 %all-to-all-start = ((bf16[4,64,128]{2,1,0:T(8,128)(2,1)}), bf16[4,64,128]{2,1,0:T(8,128)(2,1)S(1)}, u32[]{:S(2)}, u32[]{:S(2)}) async-start(bf16[4,64,128]{2,1,0:T(8,128)(2,1)} %broadcast_in_dim.68), calls=%async_computation | async-start | bytes 131072 | tf_op jit(solution)/shard_map/all_to_all | solution.py:11
  9.1 27.9 %collective-permute-start = (bf16[64,1536]{1,0:T(8,128)(2,1)S(1)}, bf16[64,1536]{1,0:T(8,128)(2,1)S(1)}, u32[]{:S(2)}, u32[]{:S(2)}) collective-permute-start(bf16[64,1536]{1,0:T(8,128)(2,1)S(1)} %pad_maximum_fusion.1), channel_id=1, source_target_pairs={{0,1},{1,2},{2,3},{3,0},{4,5},{5,6},{6,7},{7,4},{8,9},{9,10},{10,1... | collective-permute-start | bytes 589832 | tf_op jit(solution)/shard_map/ppermute | solution.py:52
  12.6 24.4 %collective-permute-start.1 = (bf16[64,1536]{1,0:T(8,128)(2,1)S(1)}, bf16[64,1536]{1,0:T(8,128)(2,1)S(1)}, u32[]{:S(2)}, u32[]{:S(2)}) collective-permute-start(bf16[64,1536]{1,0:T(8,128)(2,1)S(1)} %pad_maximum_fusion.2), channel_id=1, source_target_pairs={{0,2},{1,3},{2,0},{3,1},{4,6},{5,7},{6,4},{7,5},{8,10},{9,11},{10,... | collective-permute-start | bytes 589832 | tf_op jit(solution)/shard_map/ppermute | solution.py:52
  16.7 20.4 %collective-permute-start.2 = (bf16[64,1536]{1,0:T(8,128)(2,1)S(1)}, bf16[64,1536]{1,0:T(8,128)(2,1)S(1)}, u32[]{:S(2)}, u32[]{:S(2)}) collective-permute-start(bf16[64,1536]{1,0:T(8,128)(2,1)S(1)} %pad_maximum_fusion.3), channel_id=1, source_target_pairs={{0,3},{1,0},{2,1},{3,2},{4,7},{5,4},{6,5},{7,6},{8,11},{9,8},{10,9... | collective-permute-start | bytes 589832 | tf_op jit(solution)/shard_map/ppermute | solution.py:52
  21.4 24.6 %all-to-all-start.1 = ((bf16[32,16,256]{2,1,0:T(8,128)(2,1)}), bf16[32,16,256]{2,1,0:T(8,128)(2,1)S(1)}, u32[]{:S(2)}, u32[]{:S(2)}) async-start(bf16[32,16,256]{2,1,0:T(8,128)(2,1)} %bitcast.11), calls=%async_computation.1 | async-start | bytes 524288 | tf_op jit(solution)/shard_map/all_to_all | solution.py:11
  46.2 19.9 %collective-permute-start.3 = (bf16[64,1536]{1,0:T(8,128)(2,1)S(1)}, bf16[64,1536]{1,0:T(8,128)(2,1)S(1)}, u32[]{:S(2)}, u32[]{:S(2)}) collective-permute-start(bf16[64,1536]{1,0:T(8,128)(2,1)S(1)} %convolution_convert_fusion), channel_id=1, source_target_pairs={{0,4},{1,29},{2,6},{3,31},{4,8},{5,1},{6,10},{7,3},{8,12},{9,5},{1... | collective-permute-start | bytes 589832 | tf_op jit(solution)/shard_map/ppermute | solution.py:49
  50.3 20.7 %collective-permute-start.7 = (bf16[64,1536]{1,0:T(8,128)(2,1)S(1)}, bf16[64,1536]{1,0:T(8,128)(2,1)S(1)}, u32[]{:S(2)}, u32[]{:S(2)}) collective-permute-start(bf16[64,1536]{1,0:T(8,128)(2,1)S(1)} %convolution_convert_fusion.1), channel_id=1, source_target_pairs={{0,28},{1,5},{2,30},{3,7},{4,0},{5,9},{6,2},{7,11},{8,4},{9,13},{1... | collective-permute-start | bytes 589832 | tf_op jit(solution)/shard_map/ppermute | solution.py:49
  66.1 20.6 %collective-permute-start.4 = (bf16[64,1536]{1,0:T(8,128)(2,1)S(1)}, bf16[64,1536]{1,0:T(8,128)(2,1)S(1)}, u32[]{:S(2)}, u32[]{:S(2)}) collective-permute-start(bf16[64,1536]{1,0:T(8,128)(2,1)S(1)} %add_convert_fusion.4), channel_id=1, source_target_pairs={{0,4},{1,29},{2,6},{3,31},{4,8},{5,1},{6,10},{7,3},{8,12},{9,5},{1... | collective-permute-start | bytes 589832 | tf_op jit(solution)/shard_map/ppermute | solution.py:49
  71.0 27.9 %collective-permute-start.8 = (bf16[64,1536]{1,0:T(8,128)(2,1)S(1)}, bf16[64,1536]{1,0:T(8,128)(2,1)S(1)}, u32[]{:S(2)}, u32[]{:S(2)}) collective-permute-start(bf16[64,1536]{1,0:T(8,128)(2,1)S(1)} %add_convert_fusion.1), channel_id=1, source_target_pairs={{0,28},{1,5},{2,30},{3,7},{4,0},{5,9},{6,2},{7,11},{8,4},{9,13},{1... | collective-permute-start | bytes 589832 | tf_op jit(solution)/shard_map/ppermute | solution.py:49
  86.8 23.2 %collective-permute-start.5 = (bf16[64,1536]{1,0:T(8,128)(2,1)S(1)}, bf16[64,1536]{1,0:T(8,128)(2,1)S(1)}, u32[]{:S(2)}, u32[]{:S(2)}) collective-permute-start(bf16[64,1536]{1,0:T(8,128)(2,1)S(1)} %add_convert_fusion.3), channel_id=1, source_target_pairs={{0,4},{1,29},{2,6},{3,31},{4,8},{5,1},{6,10},{7,3},{8,12},{9,5},{1... | collective-permute-start | bytes 589832 | tf_op jit(solution)/shard_map/ppermute | solution.py:49
  99.0 22.4 %collective-permute-start.9 = (bf16[64,1536]{1,0:T(8,128)(2,1)S(1)}, bf16[64,1536]{1,0:T(8,128)(2,1)S(1)}, u32[]{:S(2)}, u32[]{:S(2)}) collective-permute-start(bf16[64,1536]{1,0:T(8,128)(2,1)S(1)} %add_convert_fusion), channel_id=1, source_target_pairs={{0,28},{1,5},{2,30},{3,7},{4,0},{5,9},{6,2},{7,11},{8,4},{9,13},{1... | collective-permute-start | bytes 589832 | tf_op jit(solution)/shard_map/ppermute | solution.py:49
  110.0 17.2 %collective-permute-start.6 = (bf16[64,1536]{1,0:T(8,128)(2,1)S(1)}, bf16[64,1536]{1,0:T(8,128)(2,1)S(1)}, u32[]{:S(2)}, u32[]{:S(2)}) collective-permute-start(bf16[64,1536]{1,0:T(8,128)(2,1)S(1)} %add_convert_fusion.2), channel_id=1, source_target_pairs={{0,4},{1,29},{2,6},{3,31},{4,8},{5,1},{6,10},{7,3},{8,12},{9,5},{1... | collective-permute-start | bytes 589832 | tf_op jit(solution)/shard_map/ppermute | solution.py:49
  112.0 60.5 %collective-permute-start.17 = (bf16[64,768]{1,0:T(8,128)(2,1)S(1)}, bf16[64,768]{1,0:T(8,128)(2,1)S(1)}, u32[]{:S(2)}, u32[]{:S(2)}) collective-permute-start(bf16[64,768]{1,0:T(8,128)(2,1)S(1)} %get-tuple-element.24), channel_id=1, source_target_pairs={{0,1},{1,2},{2,3},{3,0},{4,5},{5,6},{6,7},{7,4},{8,9},{9,10},{10,1... | collective-permute-start | bytes 294920 | tf_op jit(solution)/shard_map/ppermute | solution.py:52
  114.1 58.4 %collective-permute-start.18 = (bf16[64,768]{1,0:T(8,128)(2,1)S(1)}, bf16[64,768]{1,0:T(8,128)(2,1)S(1)}, u32[]{:S(2)}, u32[]{:S(2)}) collective-permute-start(bf16[64,768]{1,0:T(8,128)(2,1)S(1)} %get-tuple-element.25), channel_id=1, source_target_pairs={{0,2},{1,3},{2,0},{3,1},{4,6},{5,7},{6,4},{7,5},{8,10},{9,11},{10,... | collective-permute-start | bytes 294920 | tf_op jit(solution)/shard_map/ppermute | solution.py:52
  116.3 56.2 %collective-permute-start.19 = (bf16[64,768]{1,0:T(8,128)(2,1)S(1)}, bf16[64,768]{1,0:T(8,128)(2,1)S(1)}, u32[]{:S(2)}, u32[]{:S(2)}) collective-permute-start(bf16[64,768]{1,0:T(8,128)(2,1)S(1)} %get-tuple-element.26), channel_id=1, source_target_pairs={{0,3},{1,0},{2,1},{3,2},{4,7},{5,4},{6,5},{7,6},{8,11},{9,8},{10,9... | collective-permute-start | bytes 294920 | tf_op jit(solution)/shard_map/ppermute | solution.py:52
  127.4 10.3 %collective-permute-start.10 = (bf16[64,768]{1,0:T(8,128)(2,1)S(1)}, bf16[64,768]{1,0:T(8,128)(2,1)S(1)}, u32[]{:S(2)}, u32[]{:S(2)}) collective-permute-start(bf16[64,768]{1,0:T(8,128)(2,1)S(1)} %fusion.8), channel_id=1, source_target_pairs={{0,4},{1,29},{2,6},{3,31},{4,8},{5,1},{6,10},{7,3},{8,12},{9,5},{1... | collective-permute-start | bytes 294920 | tf_op jit(solution)/shard_map/ppermute | solution.py:49
  135.1 11.4 %collective-permute-start.11 = (bf16[64,768]{1,0:T(8,128)(2,1)S(1)}, bf16[64,768]{1,0:T(8,128)(2,1)S(1)}, u32[]{:S(2)}, u32[]{:S(2)}) collective-permute-start(bf16[64,768]{1,0:T(8,128)(2,1)S(1)} %fusion.8), channel_id=1, source_target_pairs={{0,28},{1,5},{2,30},{3,7},{4,0},{5,9},{6,2},{7,11},{8,4},{9,13},{1... | collective-permute-start | bytes 294920 | tf_op jit(solution)/shard_map/ppermute | solution.py:49
  137.7 12.4 %collective-permute-start.12 = (bf16[64,768]{1,0:T(8,128)(2,1)S(1)}, bf16[64,768]{1,0:T(8,128)(2,1)S(1)}, u32[]{:S(2)}, u32[]{:S(2)}) collective-permute-start(bf16[64,768]{1,0:T(8,128)(2,1)S(1)} %collective-permute-done.10), channel_id=1, source_target_pairs={{0,4},{1,29},{2,6},{3,31},{4,8},{5,1},{6,10},{7,3},{8,12},{9,5},{1... | collective-permute-start | bytes 294920 | tf_op jit(solution)/shard_map/ppermute | solution.py:49
  146.6 13.1 %collective-permute-start.13 = (bf16[64,768]{1,0:T(8,128)(2,1)S(1)}, bf16[64,768]{1,0:T(8,128)(2,1)S(1)}, u32[]{:S(2)}, u32[]{:S(2)}) collective-permute-start(bf16[64,768]{1,0:T(8,128)(2,1)S(1)} %collective-permute-done.11), channel_id=1, source_target_pairs={{0,28},{1,5},{2,30},{3,7},{4,0},{5,9},{6,2},{7,11},{8,4},{9,13},{1... | collective-permute-start | bytes 294920 | tf_op jit(solution)/shard_map/ppermute | solution.py:49
  150.1 11.6 %collective-permute-start.14 = (bf16[64,768]{1,0:T(8,128)(2,1)S(1)}, bf16[64,768]{1,0:T(8,128)(2,1)S(1)}, u32[]{:S(2)}, u32[]{:S(2)}) collective-permute-start(bf16[64,768]{1,0:T(8,128)(2,1)S(1)} %collective-permute-done.12), channel_id=1, source_target_pairs={{0,4},{1,29},{2,6},{3,31},{4,8},{5,1},{6,10},{7,3},{8,12},{9,5},{1... | collective-permute-start | bytes 294920 | tf_op jit(solution)/shard_map/ppermute | solution.py:49
  159.7 10.8 %collective-permute-start.15 = (bf16[64,768]{1,0:T(8,128)(2,1)S(1)}, bf16[64,768]{1,0:T(8,128)(2,1)S(1)}, u32[]{:S(2)}, u32[]{:S(2)}) collective-permute-start(bf16[64,768]{1,0:T(8,128)(2,1)S(1)} %collective-permute-done.13), channel_id=1, source_target_pairs={{0,28},{1,5},{2,30},{3,7},{4,0},{5,9},{6,2},{7,11},{8,4},{9,13},{1... | collective-permute-start | bytes 294920 | tf_op jit(solution)/shard_map/ppermute | solution.py:49
  161.7 10.8 %collective-permute-start.16 = (bf16[64,768]{1,0:T(8,128)(2,1)S(1)}, bf16[64,768]{1,0:T(8,128)(2,1)S(1)}, u32[]{:S(2)}, u32[]{:S(2)}) collective-permute-start(bf16[64,768]{1,0:T(8,128)(2,1)S(1)} %collective-permute-done.14), channel_id=1, source_target_pairs={{0,4},{1,29},{2,6},{3,31},{4,8},{5,1},{6,10},{7,3},{8,12},{9,5},{1... | collective-permute-start | bytes 294920 | tf_op jit(solution)/shard_map/ppermute | solution.py:49
  173.7 18.4 %copy-start.2 = (s32[128,8]{0,1:T(8,128)S(1)}, s32[128,8]{0,1:T(8,128)}, u32[]{:S(2)}) copy-start(s32[128,8]{0,1:T(8,128)} %param.8) | copy-start | bytes 12292
  173.7 29.8 %all-to-all-start.2 = ((f32[32,16,256]{2,1,0:T(8,128)}), f32[32,16,256]{2,1,0:T(8,128)S(1)}, u32[]{:S(2)}, u32[]{:S(2)}) async-start(f32[32,16,256]{2,1,0:T(8,128)} %fusion), calls=%async_computation.2 | async-start | bytes 1048576 | tf_op jit(solution)/shard_map/all_to_all | solution.py:11
  (2 other events, 22.0 us)
